TPU v7x, 32 devices: a whole 2x2x4 slice. The times are simulated.
32 devices in a mesh: dp: 8 (over y, x, core), mp: 4 (over z).
Axes of the slice: x: 2, y: 2, z: 4, core: 2. Of those that a mesh axis runs over, the one named last changes fastest.
Arguments:
- frames: bfloat16 [24576, 768], P(('dp', 'mp')), may hold values from -6 to 6
- w_qkv: bfloat16 [3, 768, 768], P(None, 'dp', 'mp'), may hold values from -0.21875 to 0.21875
- b_qv: bfloat16 [2, 768], P(None, ('mp', 'dp')), may hold values from -1.5 to 1.5
- w_out: bfloat16 [768, 768], P('mp', 'dp'), may hold values from -4 to 4
- b_out: float32 [768], P(('dp', 'mp')), may hold values from -1.5 to 1.5
- ln1_gain: float32 [768], P(('dp', 'mp')), may hold values from 0.5 to 1.5
- ln1_bias: float32 [768], P(('dp', 'mp')), may hold values from -1.5 to 1.5
- w_ff1: bfloat16 [768, 3072], P('dp', 'mp'), may hold values from -0.21875 to 0.21875
- b_ff1: bfloat16 [3072], P(('mp', 'dp')), may hold values from -1.5 to 1.5
- w_ff2: bfloat16 [3072, 768], P('mp', 'dp'), may hold values from -0.109375 to 0.109375
- b_ff2: float32 [768], P(('dp', 'mp')), may hold values from -1.5 to 1.5
- ln2_gain: float32 [768], P(('dp', 'mp')), may hold values from 0.5 to 1.5
- ln2_bias: float32 [768], P(('dp', 'mp')), may hold values from -1.5 to 1.5
- cotangent: bfloat16 [24576, 768], P(('dp', 'mp')), may hold values from -6 to 6
- clip_lengths: int32 [16], replicated, may hold values from 384 to 1536, as said below
- clip_slot: int32 [16], replicated, may hold values from 0 to 15, each once
Outputs:
- layer_out: bfloat16 [24576, 768], P(('dp', 'mp'))
- grad_frames: float32 [24576, 768], P(('dp', 'mp'))
- grad_w_qkv: float32 [3, 768, 768], P(None, 'dp', 'mp')
- grad_b_qv: float32 [2, 768], P(None, ('mp', 'dp'))
- grad_w_out: float32 [768, 768], P('mp', 'dp')
- grad_b_out: float32 [768], P(('dp', 'mp'))
- grad_ln1_gain: float32 [768], P(('dp', 'mp'))
- grad_ln1_bias: float32 [768], P(('dp', 'mp'))
- grad_w_ff1: float32 [768, 3072], P('dp', 'mp')
- grad_b_ff1: float32 [3072], P(('mp', 'dp'))
- grad_w_ff2: float32 [3072, 768], P('mp', 'dp')
- grad_b_ff2: float32 [768], P(('dp', 'mp'))
- grad_ln2_gain: float32 [768], P(('dp', 'mp'))
- grad_ln2_bias: float32 [768], P(('dp', 'mp'))
Inputs may be any that keep to these rules, and one draw needn't show every extreme that they name: `clip_lengths`: frames of each clip; the longest clips fill a whole slot of 1536. A permutation: clip c fills slot clip_slot[c].
All inputs are finite; a program needn't handle non-finite values.
Results may differ from a plain program's by a relative error of at most 0.02.
Values may be sent and summed in bfloat16 or wider, within the bound.
A program may use at most 192 MiB of HBM per device.

v0:
```python
import jax
import jax.numpy as jnp
from jax import lax
from jax.sharding import PartitionSpec as P

HEAD = 64
SLOT = 1536
SLOTS_DEV = 2


EPS = 1e-05
SCALE = 0.125


def normalize(field, gain, shift):
    mean = jnp.mean(field, axis=-1, keepdims=True)
    centred = field - mean
    spread = jnp.mean(centred * centred, axis=-1, keepdims=True)
    inverse = lax.rsqrt(spread + EPS)
    scaled = centred * inverse
    return (scaled * gain + shift, scaled, inverse)


def normalize_back(grad, scaled, inverse, gain):
    grad_gain = jnp.sum(grad * scaled, axis=0)
    grad_shift = jnp.sum(grad, axis=0)
    inner = grad * gain
    grad_input = inverse * (
        inner
        - jnp.mean(inner, axis=-1, keepdims=True)
        - scaled * jnp.mean(inner * scaled, axis=-1, keepdims=True)
    )
    return (grad_input, grad_gain, grad_shift)


def gelu_slope(hidden):
    normal_cdf = 0.5 * (1.0 + lax.erf(hidden * 0.7071067811865476))
    return normal_cdf + hidden * jnp.exp(-0.5 * hidden * hidden) * 0.3989422804014327


def attend_slot(query, keys, values, length):
    block = min(512, SLOT)
    count = SLOT // block
    heads = query.shape[1]
    valid = jnp.arange(SLOT) < length

    def one_block(query_block):
        scores = (
            jnp.einsum("qhd,khd->hqk", query_block, keys, preferred_element_type=jnp.float32)
            * SCALE
        )
        scores = jnp.where(valid[None, None, :], scores, -1e30)
        peak = jnp.max(scores, axis=-1, keepdims=True)
        exps = jnp.exp(scores - peak)
        total = jnp.sum(exps, axis=-1, keepdims=True)
        weights = (exps / total).astype(jnp.bfloat16)
        context = jnp.einsum("hqk,khd->qhd", weights, values, preferred_element_type=jnp.float32)
        return (context.astype(jnp.bfloat16), (peak + jnp.log(total))[..., 0])

    context, log_total = lax.map(one_block, query.reshape(count, block, heads, HEAD))
    return (context.reshape(SLOT, heads, HEAD), log_total)


def attend_back(query, keys, values, length, log_total, grad_context):
    block = min(512, SLOT)
    count = SLOT // block
    heads = query.shape[1]
    valid = jnp.arange(SLOT) < length

    def one_block(carry, inputs):
        grad_keys, grad_values = carry
        query_block, total_block, grad_block = inputs
        scores = (
            jnp.einsum("qhd,khd->hqk", query_block, keys, preferred_element_type=jnp.float32)
            * SCALE
        )
        scores = jnp.where(valid[None, None, :], scores, -1e30)
        weights = jnp.exp(scores - total_block[..., None])
        grad_weights = jnp.einsum(
            "qhd,khd->hqk", grad_block, values, preferred_element_type=jnp.float32
        )
        inner = jnp.sum(weights * grad_weights, axis=-1, keepdims=True)
        grad_scores = (weights * (grad_weights - inner)).astype(jnp.bfloat16)
        grad_values = grad_values + jnp.einsum(
            "hqk,qhd->khd",
            weights.astype(jnp.bfloat16),
            grad_block,
            preferred_element_type=jnp.float32,
        )
        grad_keys = grad_keys + SCALE * jnp.einsum(
            "hqk,qhd->khd", grad_scores, query_block, preferred_element_type=jnp.float32
        )
        grad_query = SCALE * jnp.einsum(
            "hqk,khd->qhd", grad_scores, keys, preferred_element_type=jnp.float32
        )
        return ((grad_keys, grad_values), grad_query.astype(jnp.bfloat16))

    empty = jnp.zeros((SLOT, heads, HEAD), jnp.float32)
    blocked = (
        query.reshape(count, block, heads, HEAD),
        log_total,
        grad_context.reshape(count, block, heads, HEAD),
    )
    (grad_keys, grad_values), grad_query = lax.scan(one_block, (empty, empty), blocked)
    return (
        grad_query.reshape(SLOT, heads, HEAD),
        grad_keys.astype(jnp.bfloat16),
        grad_values.astype(jnp.bfloat16),
    )


def body(
    frames,
    w_qkv,
    b_qv,
    w_out,
    b_out,
    ln1_gain,
    ln1_bias,
    w_ff1,
    b_ff1,
    w_ff2,
    b_ff2,
    ln2_gain,
    ln2_bias,
    cotangent,
    clip_lengths,
    clip_slot,
):
    qkv_weight, qv_bias, out_weight, up_weight, up_bias, down_weight = (
        lax.all_gather(w_qkv, "dp", axis=1, tiled=True),
        lax.all_gather(b_qv, "dp", axis=1, tiled=True),
        lax.all_gather(w_out, "dp", axis=1, tiled=True),
        lax.all_gather(w_ff1, "dp", axis=0, tiled=True),
        lax.all_gather(b_ff1, "dp", axis=0, tiled=True),
        lax.all_gather(w_ff2, "dp", axis=1, tiled=True),
    )
    out_bias, gain_one, shift_one, down_bias, gain_two, shift_two = (
        lax.all_gather(b_out, ("dp", "mp"), axis=0, tiled=True),
        lax.all_gather(ln1_gain, ("dp", "mp"), axis=0, tiled=True),
        lax.all_gather(ln1_bias, ("dp", "mp"), axis=0, tiled=True),
        lax.all_gather(b_ff2, ("dp", "mp"), axis=0, tiled=True),
        lax.all_gather(ln2_gain, ("dp", "mp"), axis=0, tiled=True),
        lax.all_gather(ln2_bias, ("dp", "mp"), axis=0, tiled=True),
    )
    local_width = out_weight.shape[0]
    heads_here = local_width // HEAD
    own_rows = frames.shape[0]
    all_rows = own_rows * lax.axis_size("mp")
    slot_ids = lax.axis_index("dp") * SLOTS_DEV + jnp.arange(SLOTS_DEV, dtype=jnp.int32)
    slot_length = jnp.sum(
        jnp.where(clip_slot[None, :] == slot_ids[:, None], clip_lengths[None, :], 0), axis=1
    )
    slot_shape = (SLOTS_DEV, SLOT, heads_here, HEAD)
    inputs = lax.all_gather(frames, "mp", axis=0, tiled=True)
    projected = jnp.einsum("rd,cdh->crh", inputs, qkv_weight, preferred_element_type=jnp.float32)
    query = (projected[0] + qv_bias[0].astype(jnp.float32)).astype(jnp.bfloat16).reshape(slot_shape)
    keys = projected[1].astype(jnp.bfloat16).reshape(slot_shape)
    values = (
        (projected[2] + qv_bias[1].astype(jnp.float32)).astype(jnp.bfloat16).reshape(slot_shape)
    )
    context, log_total = lax.map(
        lambda items: attend_slot(*items), (query, keys, values, slot_length)
    )
    context = context.reshape(all_rows, local_width)
    attn_total = lax.psum_scatter(
        jnp.dot(context, out_weight, preferred_element_type=jnp.float32).astype(jnp.bfloat16),
        "mp",
        scatter_dimension=0,
        tiled=True,
    ).astype(jnp.float32)
    pre_one = attn_total + out_bias + frames.astype(jnp.float32)
    middle, scaled_one, inverse_one = normalize(pre_one, gain_one, shift_one)
    middle_rows = lax.all_gather(middle.astype(jnp.bfloat16), "mp", axis=0, tiled=True)
    hidden = jnp.dot(middle_rows, up_weight, preferred_element_type=jnp.float32) + up_bias.astype(
        jnp.float32
    )
    active = jax.nn.gelu(hidden, approximate=False).astype(jnp.bfloat16)
    ffn_total = lax.psum_scatter(
        jnp.dot(active, down_weight, preferred_element_type=jnp.float32).astype(jnp.bfloat16),
        "mp",
        scatter_dimension=0,
        tiled=True,
    ).astype(jnp.float32)
    pre_two = ffn_total + down_bias + middle
    output, scaled_two, inverse_two = normalize(pre_two, gain_two, shift_two)
    grad_pre_two, grad_gain_two, grad_shift_two = normalize_back(
        cotangent.astype(jnp.float32), scaled_two, inverse_two, gain_two
    )
    grad_down_bias = jnp.sum(grad_pre_two, axis=0)
    grad_rows_two = lax.all_gather(grad_pre_two.astype(jnp.bfloat16), "mp", axis=0, tiled=True)
    grad_down = jnp.einsum("rf,rd->fd", active, grad_rows_two, preferred_element_type=jnp.float32)
    grad_active = jnp.einsum(
        "rd,fd->rf", grad_rows_two, down_weight, preferred_element_type=jnp.float32
    )
    grad_hidden = (grad_active * gelu_slope(hidden)).astype(jnp.bfloat16)
    grad_up = jnp.einsum("rd,rf->df", middle_rows, grad_hidden, preferred_element_type=jnp.float32)
    grad_up_bias = jnp.sum(grad_hidden, axis=0, dtype=jnp.float32)
    grad_middle = grad_pre_two + lax.psum_scatter(
        jnp.einsum("rf,df->rd", grad_hidden, up_weight, preferred_element_type=jnp.float32).astype(
            jnp.bfloat16
        ),
        "mp",
        scatter_dimension=0,
        tiled=True,
    ).astype(jnp.float32)
    grad_pre_one, grad_gain_one, grad_shift_one = normalize_back(
        grad_middle, scaled_one, inverse_one, gain_one
    )
    grad_out_bias = jnp.sum(grad_pre_one, axis=0)
    grad_rows_one = lax.all_gather(grad_pre_one.astype(jnp.bfloat16), "mp", axis=0, tiled=True)
    grad_out = jnp.einsum("rh,rd->hd", context, grad_rows_one, preferred_element_type=jnp.float32)
    grad_context = jnp.einsum(
        "rd,hd->rh", grad_rows_one, out_weight, preferred_element_type=jnp.float32
    ).astype(jnp.bfloat16)
    grad_query, grad_keys, grad_values = lax.map(
        lambda items: attend_back(*items),
        (query, keys, values, slot_length, log_total, grad_context.reshape(slot_shape)),
    )
    stacked = jnp.stack(
        [
            grad_query.reshape(all_rows, local_width),
            grad_keys.reshape(all_rows, local_width),
            grad_values.reshape(all_rows, local_width),
        ]
    )
    grad_qkv = jnp.einsum("rd,crh->cdh", inputs, stacked, preferred_element_type=jnp.float32)
    grad_qv_bias = jnp.stack(
        [
            jnp.sum(stacked[0], axis=0, dtype=jnp.float32),
            jnp.sum(stacked[2], axis=0, dtype=jnp.float32),
        ]
    )
    grad_input = grad_pre_one + lax.psum_scatter(
        jnp.einsum("crh,cdh->rd", stacked, qkv_weight, preferred_element_type=jnp.float32).astype(
            jnp.bfloat16
        ),
        "mp",
        scatter_dimension=0,
        tiled=True,
    ).astype(jnp.float32)
    summed = (
        lax.psum_scatter(grad_qkv, "dp", scatter_dimension=1, tiled=True),
        lax.psum_scatter(grad_qv_bias, "dp", scatter_dimension=1, tiled=True),
        lax.psum_scatter(grad_out, "dp", scatter_dimension=1, tiled=True),
        lax.psum_scatter(grad_up, "dp", scatter_dimension=0, tiled=True),
        lax.psum_scatter(grad_up_bias, "dp", scatter_dimension=0, tiled=True),
        lax.psum_scatter(grad_down, "dp", scatter_dimension=1, tiled=True),
    )
    vectors = (
        lax.psum_scatter(grad_out_bias, ("dp", "mp"), scatter_dimension=0, tiled=True),
        lax.psum_scatter(grad_gain_one, ("dp", "mp"), scatter_dimension=0, tiled=True),
        lax.psum_scatter(grad_shift_one, ("dp", "mp"), scatter_dimension=0, tiled=True),
        lax.psum_scatter(grad_down_bias, ("dp", "mp"), scatter_dimension=0, tiled=True),
        lax.psum_scatter(grad_gain_two, ("dp", "mp"), scatter_dimension=0, tiled=True),
        lax.psum_scatter(grad_shift_two, ("dp", "mp"), scatter_dimension=0, tiled=True),
    )
    return (
        output.astype(jnp.bfloat16),
        grad_input,
        summed[0],
        summed[1],
        summed[2],
        vectors[0],
        vectors[1],
        vectors[2],
        summed[3],
        summed[4],
        summed[5],
        vectors[3],
        vectors[4],
        vectors[5],
    )


def solution(mesh):
    placed = (
        P(("dp", "mp"), None),
        P(None, "dp", "mp"),
        P(None, ("mp", "dp")),
        P("mp", "dp"),
        P(("dp", "mp")),
        P(("dp", "mp")),
        P(("dp", "mp")),
        P("dp", "mp"),
        P(("mp", "dp")),
        P("mp", "dp"),
        P(("dp", "mp")),
        P(("dp", "mp")),
        P(("dp", "mp")),
        P(("dp", "mp"), None),
        P(),
        P(),
    )
    return jax.shard_map(
        body,
        mesh=mesh,
        in_specs=placed,
        out_specs=(
            P(("dp", "mp"), None),
            P(("dp", "mp"), None),
            P(None, "dp", "mp"),
            P(None, ("mp", "dp")),
            P("mp", "dp"),
            P(("dp", "mp")),
            P(("dp", "mp")),
            P(("dp", "mp")),
            P("dp", "mp"),
            P(("mp", "dp")),
            P("mp", "dp"),
            P(("dp", "mp")),
            P(("dp", "mp")),
            P(("dp", "mp")),
        ),
        check_vma=False,
    )
```

profile of v0, /device:TPU:8, one launch (start us, length us, event | category | flops | bytes accessed | tf_op | source)
XLA Modules:
  0.0 1308.9 jit_solution(13542362670212928923)
XLA Ops:
  31.3 12.5 all_gather.48
  43.8 54.5 %all-gather.8.cloned.1.call-done = bf16[3072,768]{1,0:T(8,128)(2,1)} async-done(((bf16[768,768]{1,0:T(8,128)(2,1)}), bf16[3072,768]{1,0:T(8,128)(2,1)}) %all-gather.8.cloned.1.call-update) | async-done | bytes 4718608 | tf_op jit(solution)/shard_map/all_gather | solution.py:155
  122.6 93.1 %while.55 = (s32[]{:T(128)}, bf16[2,1536,3,64]{1,0,3,2:T(2,128)(2,1)}, f32[2,3,3,512]{3,2,1,0:T(4,128)}, bf16[2,1536,3,64]{1,3,2,0:T(8,128)(2,1)}, bf16[2,1536,3...) while((s32[]{:T(128)}, ...), condition=%wide.region_6.7_spmd, body=%wide.region_1.6_spmd.sunk | while | flops 632389632 | bytes 39431484 | solution.py:162
  126.2 21.3 %while.58 = (s32[]{:T(128)}, bf16[3,512,3,64]{1,3,2,0:T(8,128)(2,1)S(1)}, f32[3,3,512]{2,1,0:T(4,128)S(1)}, bf16[3,512,3,64]{1,3,2,0:T(8,128)(2,1)S(1)}, bf16[15...) while((s32[]{:T(128)}, ...), condition=%wide.region_5.5_spmd.clone, body=%wide.region_2.4_spmd.clone.sunk | while | flops 632389632 | bytes 29951084 | solution.py:60
  150.7 18.2 %dynamic_update_slice.46 = bf16[2,1536,3,64]{1,0,3,2:T(2,128)(2,1)} dynamic-update-slice(bf16[2,1536,3,64]{1,0,3,2:T(2,128)(2,1)} %get-tuple-element.891, bf16[1,1536,3,64]{1,0,3,2:T(2,128)(2,1)S(1)} %copy.137, s32[]{:T(128)S(6)} %copy.178, s32[]{:T(128)} %constant.85.clone.1..sunk, s32[]{:T(128)} %constant.85.clone.1..sunk, s32[]{:T(128)} %constant.85.clone.1..sunk) | dynamic-update-slice | bytes 1179652 | tf_op jit(solution)/shard_map/while/body/jit(dynamic_update_index_in_dim)/dynamic_update_slice | solution.py:162
  172.6 21.3 %while.58 = (s32[]{:T(128)}, bf16[3,512,3,64]{1,3,2,0:T(8,128)(2,1)S(1)}, f32[3,3,512]{2,1,0:T(4,128)S(1)}, bf16[3,512,3,64]{1,3,2,0:T(8,128)(2,1)S(1)}, bf16[15...) while((s32[]{:T(128)}, ...), condition=%wide.region_5.5_spmd.clone, body=%wide.region_2.4_spmd.clone.sunk | while | flops 632389632 | bytes 29951084 | solution.py:60
  197.1 18.2 %dynamic_update_slice.46 = bf16[2,1536,3,64]{1,0,3,2:T(2,128)(2,1)} dynamic-update-slice(bf16[2,1536,3,64]{1,0,3,2:T(2,128)(2,1)} %get-tuple-element.891, bf16[1,1536,3,64]{1,0,3,2:T(2,128)(2,1)S(1)} %copy.137, s32[]{:T(128)S(6)} %copy.178, s32[]{:T(128)} %constant.85.clone.1..sunk, s32[]{:T(128)} %constant.85.clone.1..sunk, s32[]{:T(128)} %constant.85.clone.1..sunk) | dynamic-update-slice | bytes 1179652 | tf_op jit(solution)/shard_map/while/body/jit(dynamic_update_index_in_dim)/dynamic_update_slice | solution.py:162
  223.7 47.6 %all-reduce.16 = (f32[768]{0:T(1024)S(1)}, f32[768]{0:T(1024)S(1)}, f32[768]{0:T(1024)S(1)}, f32[768]{0:T(1024)S(1)}, f32[768]{0:T(1024)S(1)}) all-reduce(f32[768]{0:T(1024)S(1)} %dynamic-update-slice.2, f32[768]{0:T(1024)S(1)} %dynamic-update-slice.1, f32[768]{0:T(1024)S(1)} %dynamic-update-slice, ...), channel_id=1, replica_groups=mesh['dp'=8,'mp'=4] {'dp','mp'}, use_global_device_ids=true, to_apply=%add.2 | all-reduce | flops 3840 | bytes 30720
  271.3 38.3 %reduce-scatter.14.cloned.1.call-done = bf16[768,768]{1,0:T(8,128)(2,1)} async-done(((bf16[3072,768]{1,0:T(8,128)(2,1)}), bf16[768,768]{1,0:T(8,128)(2,1)}) %reduce-scatter.14.cloned.1.call-update) | async-done | bytes 1179664 | tf_op jit(solution)/shard_map/reduce_scatter | solution.py:166
  315.9 13.6 %all-reduce.3 = bf16[768]{0:T(1024)(128)(2,1)S(1)} all-reduce(bf16[768]{0:T(1024)(128)(2,1)S(1)} %dynamic-update-slice.3), channel_id=1, replica_groups=mesh['dp'=8,'mp'=4] {'dp'}, use_global_device_ids=true, to_apply=%add.3 | all-reduce | flops 768 | bytes 3072
  329.5 71.4 %all-gather.10.cloned.1.call-done = bf16[3072,768]{1,0:T(8,128)(2,1)} async-done(((bf16[768,768]{1,0:T(8,128)(2,1)}), bf16[3072,768]{1,0:T(8,128)(2,1)}) %all-gather.10.cloned.1.call-update) | async-done | bytes 4718608 | tf_op jit(solution)/shard_map/all_gather | solution.py:174
  400.9 26.3 %fusion.44 = (bf16[3072,768]{1,0:T(8,128)(2,1)}, f32[3072,768]{1,0:T(8,128)}) fusion(f32[768]{0:T(1024)S(1)} %convert_element_type.116, bf16[3072,768]{1,0:T(8,128)(2,1)} %all-gather.10.cloned.1.call-done, bf16[768,768]{1,0:T(8,128)(2,1)} %all-gather.12.cloned.1.call-done), kind=kOutput, calls=%fused_computation.64 | convolution fusion | flops 3779592192 | bytes 20057088 | tf_op jit(solution)/shard_map/dot_general | solution.py:175
  436.5 86.0 %reduce-scatter.16.cloned.1.call-done = bf16[768,768]{1,0:T(8,128)(2,1)} async-done(((bf16[3072,768]{1,0:T(8,128)(2,1)}), bf16[768,768]{1,0:T(8,128)(2,1)}) %reduce-scatter.16.cloned.1.call-update) | async-done | bytes 1179664 | tf_op jit(solution)/shard_map/reduce_scatter | solution.py:179
  531.0 87.3 %all-gather.16.cloned.1.call-done = bf16[3072,768]{1,0:T(8,128)(2,1)} async-done(((bf16[768,768]{1,0:T(8,128)(2,1)}), bf16[3072,768]{1,0:T(8,128)(2,1)}) %all-gather.16.cloned.1.call-update) | async-done | bytes 4718608 | tf_op jit(solution)/shard_map/all_gather | solution.py:191
  618.2 10.5 convert_reduce_fusion
  636.6 86.4 %reduce-scatter.18.cloned.1.call-done = bf16[768,768]{1,0:T(8,128)(2,1)} async-done(((bf16[3072,768]{1,0:T(8,128)(2,1)}), bf16[768,768]{1,0:T(8,128)(2,1)}) %reduce-scatter.18.cloned.1.call-update) | async-done | bytes 1179664 | tf_op jit(solution)/shard_map/reduce_scatter | solution.py:199
  729.5 87.3 %all-gather.18.cloned.1.call-done = bf16[3072,768]{1,0:T(8,128)(2,1)} async-done(((bf16[768,768]{1,0:T(8,128)(2,1)}), bf16[3072,768]{1,0:T(8,128)(2,1)}) %all-gather.18.cloned.1.call-update) | async-done | bytes 4718608 | tf_op jit(solution)/shard_map/all_gather | solution.py:211
  823.1 208.8 %while.57 = (s32[]{:T(128)}, bf16[2,1536,3,64]{3,2,1,0:T(4,128)(2,1)}, bf16[2,1536,3,64]{1,3,2,0:T(8,128)(2,1)}, bf16[2,1536,3,64]{1,3,2,0:T(8,128)(2,1)}, bf16[...) while((s32[]{:T(128)}, ...), condition=%wide.region_22.23_spmd, body=%wide.region_18.22_spmd.sunk | while | flops 1533444096 | bytes 171120256 | solution.py:216
  832.3 87.5 %while.59 = (s32[]{:T(128)}, f32[1536,3,64]{0,2,1:T(8,128)S(1)}, f32[1536,3,64]{0,2,1:T(8,128)S(1)}, bf16[3,512,3,64]{1,3,2,0:T(8,128)(2,1)}, bf16[3,512,3,64]{1...) while((s32[]{:T(128)}, f32[1536,3,64]{0,2,1:T(8,128)S(1)}, ...), condition=%wide.region_21.21_spmd.clone, body=%wide.region_19.20_spmd.clone.sunk | while | flops 1532854272 | bytes 134907104 | solution.py:104
  936.7 87.5 %while.59 = (s32[]{:T(128)}, f32[1536,3,64]{0,2,1:T(8,128)S(1)}, f32[1536,3,64]{0,2,1:T(8,128)S(1)}, bf16[3,512,3,64]{1,3,2,0:T(8,128)(2,1)}, bf16[3,512,3,64]{1...) while((s32[]{:T(128)}, f32[1536,3,64]{0,2,1:T(8,128)S(1)}, ...), condition=%wide.region_21.21_spmd.clone, body=%wide.region_19.20_spmd.clone.sunk | while | flops 1532854272 | bytes 134907104 | solution.py:104
  1108.0 14.2 %all-reduce.17 = (f32[2,192]{1,0:T(2,128)S(1)}, f32[768]{0:T(1024)S(1)}) all-reduce(f32[2,192]{1,0:T(2,128)S(1)} %pad_maximum_fusion, f32[768]{0:T(1024)S(1)} %copy-done.33), channel_id=7, replica_groups=mesh['dp'=8,'mp'=4] {'dp'}, use_global_device_ids=true, to_apply=%region_27.28.clone | all-reduce | flops 1152 | bytes 9216
  1126.9 81.6 %reduce-scatter.20.cloned.1.call-done = bf16[768,768]{1,0:T(8,128)(2,1)} async-done(((bf16[3072,768]{1,0:T(8,128)(2,1)}), bf16[768,768]{1,0:T(8,128)(2,1)}) %reduce-scatter.20.cloned.1.call-update) | async-done | bytes 1179664 | tf_op jit(solution)/shard_map/reduce_scatter | solution.py:234
  1212.4 40.2 %all-reduce.15 = (f32[768]{0:T(1024)S(1)}, f32[768]{0:T(1024)S(1)}, f32[768]{0:T(1024)S(1)}, f32[768]{0:T(1024)S(1)}, f32[768]{0:T(1024)S(1)}, /*index=5*/f32[768]{0:T(1024)S(1)}, f32[768]{0:T(1024)S(1)}) all-reduce(f32[768]{0:T(1024)S(1)} %dynamic-update-slice.6, ...), channel_id=1, replica_groups=mesh['dp'=8,'mp'=4] {'dp','mp'}, use_global_device_ids=true, to_apply=%add.6 | all-reduce | flops 5376 | bytes 43008
  1257.6 44.0 %reduce-scatter.24.cloned.1.call-done = f32[768,96]{0,1:T(8,128)} async-done(((f32[768,768]{0,1:T(8,128)}), f32[768,96]{0,1:T(8,128)}) %reduce-scatter.24.cloned.1.call-update) | async-done | bytes 294928 | tf_op jit(solution)/shard_map/reduce_scatter | solution.py:248
  (377 shorter events, 451.2 us)
Async XLA Ops:
  8.0 90.2 %all-gather.8.cloned.1.call-start = ((), (), s32[]{:S(2)}) async-start(), calls=%async_computation.8 | async-start | bytes 5898240 | tf_op jit(solution)/shard_map/all_gather | solution.py:155
  8.7 300.8 %reduce-scatter.14.cloned.1.call-start = ((), (), s32[]{:S(2)}) async-start(), calls=%async_computation.9 | async-start | bytes 5898240 | tf_op jit(solution)/shard_map/reduce_scatter | solution.py:166
  43.8 60.4 %copy-start.18 = (bf16[3,768,192]{2,0,1:T(4,128)(2,1)}, bf16[3,768,192]{2,0,1:T(4,128)(2,1)S(1)}, u32[]{:S(2)}) copy-start(bf16[3,768,192]{2,0,1:T(4,128)(2,1)S(1)} %all_gather.48) | copy-start | bytes 2654212
  221.8 87.7 %copy-start.4 = (bf16[768,768]{1,0:T(8,128)(2,1)S(1)}, bf16[768,768]{1,0:T(8,128)(2,1)}, u32[]{:S(2)}) copy-start(bf16[768,768]{1,0:T(8,128)(2,1)} %param.24) | copy-start | bytes 3538948
  221.8 107.7 %all-gather.12.cloned.1.call-start = ((), (), s32[]{:S(2)}) async-start(), calls=%async_computation.11 | async-start | bytes 1327104 | tf_op jit(solution)/shard_map/all_gather | solution.py:134
  222.4 178.5 %all-gather.10.cloned.1.call-start = ((), (), s32[]{:S(2)}) async-start(), calls=%async_computation.10 | async-start | bytes 5898240 | tf_op jit(solution)/shard_map/all_gather | solution.py:174
  271.3 257.3 %copy-start.26 = (f32[768]{0:T(1024)}, f32[768]{0:T(1024)S(1)}, u32[]{:S(2)}) copy-start(f32[768]{0:T(1024)S(1)} %get-tuple-element.521) | copy-start | bytes 9220
  313.8 113.8 %all-gather.14.cloned.1.call-start = ((), (), s32[]{:S(2)}) async-start(), calls=%async_computation.12 | async-start | bytes 1327104 | tf_op jit(solution)/shard_map/all_gather | solution.py:136
  314.4 208.1 %reduce-scatter.16.cloned.1.call-start = ((), (), s32[]{:S(2)}) async-start(), calls=%async_computation.13 | async-start | bytes 5898240 | tf_op jit(solution)/shard_map/reduce_scatter | solution.py:179
  436.5 181.8 %all-gather.16.cloned.1.call-start = ((), (), s32[]{:S(2)}) async-start(), calls=%async_computation.14 | async-start | bytes 5898240 | tf_op jit(solution)/shard_map/all_gather | solution.py:191
  530.9 192.0 %reduce-scatter.18.cloned.1.call-start = ((), (), s32[]{:S(2)}) async-start(), calls=%async_computation.15 | async-start | bytes 5898240 | tf_op jit(solution)/shard_map/reduce_scatter | solution.py:199
  618.2 12.7 copy-start.35
  636.5 180.3 %all-gather.18.cloned.1.call-start = ((), (), s32[]{:S(2)}) async-start(), calls=%async_computation.16 | async-start | bytes 5898240 | tf_op jit(solution)/shard_map/all_gather | solution.py:211
  729.4 394.0 %reduce-scatter.28.cloned.1.call-start = ((), (), s32[]{:S(2)}) async-start(), calls=%async_computation.21 | async-start | bytes 884736
  1041.4 83.7 %reduce-scatter.26.cloned.1.call-start = ((), (), s32[]{:S(2)}) async-start(), calls=%async_computation.20 | async-start | bytes 2211840
  1041.8 7.6 copy-start.7
  1073.5 135.1 %reduce-scatter.20.cloned.1.call-start = ((), (), s32[]{:S(2)}) async-start(), calls=%async_computation.17 | async-start | bytes 5898240 | tf_op jit(solution)/shard_map/reduce_scatter | solution.py:234
  1082.1 175.5 %reduce-scatter.22.cloned.1.call-start = ((), (), s32[]{:S(2)}) async-start(), calls=%async_computation.18 | async-start | bytes 2654208 | tf_op jit(solution)/shard_map/reduce_scatter | solution.py:246
  1091.4 210.2 %reduce-scatter.24.cloned.1.call-start = ((), (), s32[]{:S(2)}) async-start(), calls=%async_computation.19 | async-start | bytes 2654208 | tf_op jit(solution)/shard_map/reduce_scatter | solution.py:248
  1091.5 11.3 copy-start.42
  1208.6 47.5 %copy-start.3 = (f32[768,768]{1,0:T(8,128)S(1)}, f32[768,768]{1,0:T(8,128)}, u32[]{:S(2)}) copy-start(f32[768,768]{1,0:T(8,128)} %copy-done.2) | copy-start | bytes 7077892
  1208.6 47.5 %copy-start.23 = (f32[768]{0:T(1024)S(1)}, f32[768]{0:T(1024)}, u32[]{:S(2)}) copy-start(f32[768]{0:T(1024)} %copy-done.22) | copy-start | bytes 9220
  1208.6 47.5 %copy-start.25 = (f32[768]{0:T(1024)S(1)}, f32[768]{0:T(1024)}, u32[]{:S(2)}) copy-start(f32[768]{0:T(1024)} %copy-done.24) | copy-start | bytes 9220
  1208.6 47.5 %copy-start.27 = (f32[768]{0:T(1024)S(1)}, f32[768]{0:T(1024)}, u32[]{:S(2)}) copy-start(f32[768]{0:T(1024)} %copy-done.26) | copy-start | bytes 9220
  (48 other events, 171.2 us)
Sparse Core Ops, SparseCore 0:
  10.4 87.8 all-gather.7
  222.0 87.5 reduce-scatter.13
  531.0 87.1 all-gather.15
  729.6 87.1 all-gather.17
Sparse Core Ops, SparseCore 1:
  224.2 24.9 all-gather.11
  313.9 87.0 all-gather.9
  402.7 24.9 all-gather.13
  436.5 85.9 reduce-scatter.15
  636.6 86.3 reduce-scatter.17
  1041.5 36.0 reduce-scatter.27
  1080.8 40.1 reduce-scatter.25
  1123.2 85.3 reduce-scatter.19
  1212.4 43.0 reduce-scatter.21
  1259.4 42.2 reduce-scatter.23
where the time goes:
time: 1330 us; the launch traced here: 1310 us
  waiting for transfers between devices  639 us (48%)
  matrix products  239 us (18%)
  local copies, waits for them, and re-layouts  153 us (12%)
  blocking collectives  147 us (11%)
  other arithmetic  109 us (8%)
  between operations  18.7 us (1%)
    unnamed x4, blocking collectives  116 us
    all_gather x1, waiting for transfers between devices, body(): lax.all_gather(grad_pre_two.astype(jnp.bfloat16), 'mp', axis=0, tiled=True)  87.3 us
    all_gather x1, waiting for transfers between devices, body(): lax.all_gather(grad_pre_one.astype(jnp.bfloat16), 'mp', axis=0, tiled=True)  87.3 us
    reduce_scatter x1, waiting for transfers between devices, body(): lax.psum_scatter(jnp.einsum('rf,df->rd', grad_hidden, up_weight, preferre...  86.4 us
    reduce_scatter x1, waiting for transfers between devices, body(): lax.psum_scatter(jnp.dot(active, down_weight, preferred_element_type=jnp....  86 us
    reduce_scatter x1, waiting for transfers between devices, body(): lax.psum_scatter(jnp.einsum('crh,cdh->rd', stacked, qkv_weight, preferred...  81.6 us
    all_gather x1, waiting for transfers between devices, body(): lax.all_gather(middle.astype(jnp.bfloat16), 'mp', axis=0, tiled=True)  71.4 us
    convert_element_type x6, other arithmetic, one_block(): grad_scores = (weights * (grad_weights - inner)).astype(jnp.bfloat16)  56 us
  transfers between devices with their start and end apart: 14, of which 10 were waited for; matrix products, arithmetic and copies ran while one was open for 8% of the time, Pallas kernels for 0%

commit v1 on v0

v1 whole, which is shorter than its diff:
```python
import functools

import jax
import jax.numpy as jnp
from jax import lax
from jax.experimental import pallas as pl
from jax.experimental.pallas import tpu as pltpu
from jax.sharding import PartitionSpec as P

HEAD = 64
SLOT = 1536
EPS = 1e-05
SCALE = 0.125
MASKED = -1e30
BOTH = ("dp", "mp")
F32 = jnp.float32
BF16 = jnp.bfloat16
NN = (((1,), (0,)), ((), ()))
NT = (((1,), (1,)), ((), ()))


def mul(left, right, dims=NN):
    return lax.dot_general(left, right, dims, preferred_element_type=F32)


def lanes(shape):
    return lax.broadcasted_iota(jnp.int32, shape, 1)


def three_parts(value):
    high = value.astype(BF16).astype(F32)
    rest = value - high
    middle = rest.astype(BF16).astype(F32)
    return high, middle, rest - middle


def head_block(value, place):
    block = value[:, 128 * (place // 2) : 128 * (place // 2) + 128]
    return pltpu.roll(block, HEAD, 1) if place % 2 else block


def pair(low, high):
    return jnp.where(lanes(low.shape) < HEAD, low, pltpu.roll(high, HEAD, 1))


def norm_parts(field):
    mean = jnp.mean(field, axis=-1, keepdims=True)
    centred = field - mean
    spread = jnp.mean(centred * centred, axis=-1, keepdims=True)
    inverse = lax.rsqrt(spread + EPS)
    return centred * inverse, inverse


def norm_back(grad, scaled, inverse, gain):
    inner = grad * gain
    return inverse * (
        inner
        - jnp.mean(inner, axis=-1, keepdims=True)
        - scaled * jnp.mean(inner * scaled, axis=-1, keepdims=True)
    )


def weight(ref, first, last):
    return ref[:, 0, :, first:last].reshape(ref.shape[0] * ref.shape[2], last - first)


def attend_kernel(
    valid_ref, own_ref, other_ref, w_ref, qv_bias_ref, out_bias_ref, pre_ref, ctx_ref, q_ref, k_ref, v_ref
):
    group, groups = pl.program_id(0), pl.num_programs(0)
    rows = own_ref.shape[0]
    bias = qv_bias_ref[0]
    projected = mul(own_ref[...], weight(w_ref, 0, 640)) + bias
    projected_other = mul(other_ref[...], weight(w_ref, 128, 640)) + bias[:, 128:]
    lane = lanes((rows, 128))
    row = lax.broadcasted_iota(jnp.int32, (rows, 128), 0)
    contexts = []
    for head in range(3):
        query = jnp.where(
            lane < HEAD, head_block(projected, head).astype(BF16).astype(F32) * SCALE, jnp.where(lane == HEAD, 1.0, 0.0)
        )
        for half, (source, shift) in enumerate(((projected, 0), (projected_other, 2))):
            mask = jnp.where(row < valid_ref[half], 0.0, MASKED)
            tail = jnp.where(lane == HEAD, mask, jnp.where(lane < HEAD + 4, 1.0, 0.0))
            keys = jnp.where(lane < HEAD, head_block(source, 3 + head - shift), tail)
            values = jnp.where(
                lane < HEAD, head_block(source, 6 + head - shift), jnp.where(lane < HEAD + 3, 1.0, 0.0)
            )
            k_ref[head, half * rows : (half + 1) * rows, :] = keys.astype(BF16)
            v_ref[head, half * rows : (half + 1) * rows, :] = values.astype(BF16)
        step = 256
        pieces = []
        for first in range(0, rows, step):
            query_here = query[first : first + step]
            scores = mul(query_here.astype(BF16), k_ref[head], NT)
            peak = jnp.max(scores, axis=1, keepdims=True)
            exps = jnp.exp(scores - peak).astype(BF16)
            mixed = mul(exps, v_ref[head])
            lane_here = lanes((step, 128))
            total = jnp.sum(jnp.where(lane_here == HEAD, mixed, 0.0), axis=1, keepdims=True)
            pieces.append(mixed / total)
            high, middle, low = three_parts(-(peak + jnp.log(total)))
            kept = jnp.where(
                lane_here == HEAD + 1,
                high,
                jnp.where(lane_here == HEAD + 2, middle, jnp.where(lane_here == HEAD + 3, low, query_here)),
            )
            q_ref[head, first : first + step, :] = kept.astype(BF16)
        contexts.append(jnp.concatenate(pieces, axis=0))
    first_half = jnp.where(lane < HEAD, 0.0, pltpu.roll(contexts[0], HEAD, 1)).astype(BF16)
    second_half = pair(contexts[1], contexts[2]).astype(BF16)
    ctx_ref[0, :, 0:128] = first_half
    ctx_ref[0, :, 128:256] = second_half
    part = mul(ctx_ref[0], weight(w_ref, 512, 768), NT)

    @pl.when(group == 0)
    def _():
        pre_ref[...] = part + (out_bias_ref[...] + own_ref[...].astype(F32))

    @pl.when(group > 0)
    def _():
        pre_ref[...] += part


def attend(valid, own, other, weights, qv_bias, out_bias):
    rows, width = own.shape
    groups = weights.shape[1]
    whole = lambda g: (0, 0)
    by_group = lambda g: (g, 0, 0)
    flops = groups * (2 * 2 * rows * width * 640 + 3 * 4 * rows * SLOT * 128)
    return pl.pallas_call(
        attend_kernel,
        name="attend",
        grid=(groups,),
        in_specs=[
            pl.BlockSpec(memory_space=pltpu.SMEM),
            pl.BlockSpec((rows, width), whole),
            pl.BlockSpec((rows, width), whole),
            pl.BlockSpec((weights.shape[0], 1) + weights.shape[2:], lambda g: (0, g, 0, 0)),
            pl.BlockSpec((1, 1, 640), by_group),
            pl.BlockSpec((1, width), whole),
        ],
        out_specs=[
            pl.BlockSpec((rows, width), whole),
            pl.BlockSpec((1, rows, 256), by_group),
            pl.BlockSpec((3, rows, 128), by_group),
            pl.BlockSpec((3, SLOT, 128), by_group),
            pl.BlockSpec((3, SLOT, 128), by_group),
        ],
        out_shape=[
            jax.ShapeDtypeStruct((rows, width), F32),
            jax.ShapeDtypeStruct((groups, rows, 256), BF16),
            jax.ShapeDtypeStruct((3 * groups, rows, 128), BF16),
            jax.ShapeDtypeStruct((3 * groups, SLOT, 128), BF16),
            jax.ShapeDtypeStruct((3 * groups, SLOT, 128), BF16),
        ],
        cost_estimate=pl.CostEstimate(flops=4 * flops, bytes_accessed=24 << 20, transcendentals=12 * rows * SLOT),
        compiler_params=pltpu.CompilerParams(vmem_limit_bytes=60 << 20),
    )(valid, own, other, weights, qv_bias, out_bias)


def up_kernel(pre_ref, gain_ref, shift_ref, w_ref, bias_ref, hidden_ref, active_ref, low_ref, low_t_ref):
    @pl.when(pl.program_id(0) == 0)
    def _():
        scaled, _ = norm_parts(pre_ref[...])
        low = (scaled * gain_ref[...] + shift_ref[...]).astype(BF16)
        low_ref[...] = low
        low_t_ref[...] = low.T

    hidden = mul(low_ref[...], weight(w_ref, 0, w_ref.shape[3])) + bias_ref[0]
    hidden_ref[0] = hidden
    active_ref[0] = (hidden * (0.5 * (1.0 + lax.erf(hidden * 0.7071067811865476)))).astype(BF16)


def up(pre, gain, shift, weights, bias):
    rows, width = pre.shape
    groups, units = weights.shape[1], weights.shape[3]
    whole = lambda g: (0, 0)
    by_group = lambda g: (g, 0, 0)
    return pl.pallas_call(
        up_kernel,
        name="up",
        grid=(groups,),
        in_specs=[
            pl.BlockSpec((rows, width), whole),
            pl.BlockSpec((1, width), whole),
            pl.BlockSpec((1, width), whole),
            pl.BlockSpec((weights.shape[0], 1) + weights.shape[2:], lambda g: (0, g, 0, 0)),
            pl.BlockSpec((1, 1, units), by_group),
        ],
        out_specs=[
            pl.BlockSpec((1, rows, units), by_group),
            pl.BlockSpec((1, rows, units), by_group),
            pl.BlockSpec((rows, width), whole),
            pl.BlockSpec((width, rows), whole),
        ],
        out_shape=[
            jax.ShapeDtypeStruct((groups, rows, units), F32),
            jax.ShapeDtypeStruct((groups, rows, units), BF16),
            jax.ShapeDtypeStruct((rows, width), BF16),
            jax.ShapeDtypeStruct((width, rows), BF16),
        ],
        cost_estimate=pl.CostEstimate(
            flops=2 * groups * rows * width * units, bytes_accessed=24 << 20, transcendentals=groups * rows * units
        ),
        compiler_params=pltpu.CompilerParams(vmem_limit_bytes=60 << 20),
    )(pre, gain, shift, weights, bias)


def down_kernel(
    groups,
    pre_ref,
    cot_ref,
    vec_ref,
    active_ref,
    hidden_ref,
    w2_ref,
    w1_ref,
    low_t_ref,
    out_ref,
    grad_pre_ref,
    grad_low_ref,
    grad_low_t_ref,
    grad_w2_ref,
    grad_w1_ref,
    sums_ref,
    up_bias_ref,
    total_ref,
    upper_ref,
    upper_low_ref,
    upper_low_t_ref,
):
    step = pl.program_id(0)

    @pl.when(step < groups)
    def _():
        part = mul(active_ref[0], weight(w2_ref, 0, w2_ref.shape[3]), NT)

        @pl.when(step == 0)
        def _():
            total_ref[...] = part

        @pl.when(step > 0)
        def _():
            total_ref[...] += part

    @pl.when(step == groups - 1)
    def _():
        gain_one, shift_one = vec_ref[1:2], vec_ref[2:3]
        down_bias, gain_two, shift_two = vec_ref[3:4], vec_ref[4:5], vec_ref[5:6]
        middle = norm_parts(pre_ref[...])[0] * gain_one + shift_one
        scaled, inverse = norm_parts(total_ref[...] + down_bias + middle)
        out_ref[...] = (scaled * gain_two + shift_two).astype(BF16)
        cotangent = cot_ref[...].astype(F32)
        grad = norm_back(cotangent, scaled, inverse, gain_two)
        sums_ref[4:5] = jnp.sum(cotangent * scaled, axis=0, keepdims=True)
        sums_ref[5:6] = jnp.sum(cotangent, axis=0, keepdims=True)
        sums_ref[3:4] = jnp.sum(grad, axis=0, keepdims=True)
        upper_ref[...] = grad
        low = grad.astype(BF16)
        upper_low_ref[...] = low
        upper_low_t_ref[...] = low.T

    @pl.when(step >= groups)
    def _():
        grad_active = mul(upper_low_ref[...], weight(w2_ref, 0, w2_ref.shape[3]))
        hidden = hidden_ref[0]
        cdf = 0.5 * (1.0 + lax.erf(hidden * 0.7071067811865476))
        slope = cdf + hidden * jnp.exp(-0.5 * hidden * hidden) * 0.3989422804014327
        grad_hidden = (grad_active * slope).astype(BF16)
        up_bias_ref[0] = jnp.sum(grad_hidden.astype(F32), axis=0, keepdims=True)
        shape = grad_w2_ref.shape
        grad_w2_ref[...] = mul(upper_low_t_ref[...], active_ref[0]).astype(BF16).reshape(shape)
        grad_w1_ref[...] = mul(low_t_ref[...], grad_hidden).astype(BF16).reshape(shape)
        part = mul(grad_hidden, weight(w1_ref, 0, w1_ref.shape[3]), NT)

        @pl.when(step == groups)
        def _():
            total_ref[...] = part

        @pl.when(step > groups)
        def _():
            total_ref[...] += part

    @pl.when(step == 2 * groups - 1)
    def _():
        scaled, inverse = norm_parts(pre_ref[...])
        grad_middle = upper_ref[...] + total_ref[...]
        grad = norm_back(grad_middle, scaled, inverse, vec_ref[1:2])
        sums_ref[1:2] = jnp.sum(grad_middle * scaled, axis=0, keepdims=True)
        sums_ref[2:3] = jnp.sum(grad_middle, axis=0, keepdims=True)
        sums_ref[0:1] = jnp.sum(grad, axis=0, keepdims=True)
        sums_ref[6:8] = jnp.zeros_like(sums_ref[6:8])
        grad_pre_ref[...] = grad
        low = grad.astype(BF16)
        grad_low_ref[...] = low
        grad_low_t_ref[...] = low.T


def down(pre, cotangent, vectors, active, hidden, w2, w1, low_t):
    rows, width = pre.shape
    groups, units = w2.shape[1], w2.shape[3]
    whole = lambda s: (0, 0)
    both = lambda s: (lax.rem(s, groups), 0, 0)
    late = lambda s: (jnp.maximum(s - groups, 0), 0, 0)
    block = (w2.shape[0], 1) + w2.shape[2:]
    w_both = lambda s: (0, lax.rem(s, groups), 0, 0)
    w_late = lambda s: (0, jnp.maximum(s - groups, 0), 0, 0)
    return pl.pallas_call(
        functools.partial(down_kernel, groups),
        name="down",
        grid=(2 * groups,),
        in_specs=[
            pl.BlockSpec((rows, width), whole),
            pl.BlockSpec((rows, width), whole),
            pl.BlockSpec((8, width), whole),
            pl.BlockSpec((1, rows, units), both),
            pl.BlockSpec((1, rows, units), late),
            pl.BlockSpec(block, w_both),
            pl.BlockSpec(block, w_late),
            pl.BlockSpec((width, rows), whole),
        ],
        out_specs=[
            pl.BlockSpec((rows, width), whole),
            pl.BlockSpec((rows, width), whole),
            pl.BlockSpec((rows, width), whole),
            pl.BlockSpec((width, rows), whole),
            pl.BlockSpec(block, w_late),
            pl.BlockSpec(block, w_late),
            pl.BlockSpec((8, width), whole),
            pl.BlockSpec((1, 1, units), late),
        ],
        out_shape=[
            jax.ShapeDtypeStruct((rows, width), BF16),
            jax.ShapeDtypeStruct((rows, width), F32),
            jax.ShapeDtypeStruct((rows, width), BF16),
            jax.ShapeDtypeStruct((width, rows), BF16),
            jax.ShapeDtypeStruct(w2.shape, BF16),
            jax.ShapeDtypeStruct(w1.shape, BF16),
            jax.ShapeDtypeStruct((8, width), F32),
            jax.ShapeDtypeStruct((groups, 1, units), F32),
        ],
        scratch_shapes=[
            pltpu.VMEM((rows, width), F32),
            pltpu.VMEM((rows, width), F32),
            pltpu.VMEM((rows, width), BF16),
            pltpu.VMEM((width, rows), BF16),
        ],
        cost_estimate=pl.CostEstimate(
            flops=10 * groups * rows * width * units, bytes_accessed=48 << 20, transcendentals=groups * rows * units
        ),
        compiler_params=pltpu.CompilerParams(vmem_limit_bytes=63 << 20),
    )(pre, cotangent, vectors, active, hidden, w2, w1, low_t)


def attend_back_kernel(
    grad_ref,
    grad_t_ref,
    own_t_ref,
    other_t_ref,
    w_ref,
    ctx_ref,
    q_ref,
    k_ref,
    v_ref,
    grad_w_ref,
    grad_own_ref,
    grad_other_ref,
    sums_ref,
    other_total_ref,
):
    group, groups = pl.program_id(0), pl.num_programs(0)
    rows = grad_ref.shape[0]
    step = 256
    grad_context = mul(grad_ref[...], weight(w_ref, 512, 768)).astype(BF16).astype(F32)
    lane = lanes((rows, 128))
    grads = []
    for head in range(3):
        place = 1 + head
        grad_head = head_block(grad_context, place)
        context = head_block(ctx_ref[0].astype(F32), place)
        delta = jnp.sum(jnp.where(lane < HEAD, grad_head * context, 0.0), axis=1, keepdims=True)
        high, middle, low = three_parts(-delta)
        tail = jnp.where(
            lane == HEAD, high, jnp.where(lane == HEAD + 1, middle, jnp.where(lane == HEAD + 2, low, 0.0))
        )
        grad_head = jnp.where(lane < HEAD, grad_head, tail).astype(BF16)
        keys_t = k_ref[head].T
        grad_query = []
        grad_keys = grad_values = None
        for first in range(0, rows, step):
            query_here = q_ref[head, first : first + step, :]
            grad_here = grad_head[first : first + step]
            weights = jnp.exp(mul(k_ref[head], query_here, NT))
            grad_scores = (weights * mul(v_ref[head], grad_here, NT)).astype(BF16)
            values_part = mul(weights.astype(BF16), grad_here)
            keys_part = mul(grad_scores, query_here)
            grad_values = values_part if grad_values is None else grad_values + values_part
            grad_keys = keys_part if grad_keys is None else grad_keys + keys_part
            grad_query.append(mul(keys_t, grad_scores))
        grad_query = jnp.concatenate(grad_query, axis=1).T * SCALE
        grads.append((grad_query, grad_keys, grad_values))
    (q0, k0, v0), (q1, k1, v1), (q2, k2, v2) = grads
    blank = jnp.zeros((rows, 128), F32)
    own = jnp.concatenate(
        [
            pair(q0, q1),
            pair(q2, k0[:rows]),
            pair(k1[:rows], k2[:rows]),
            pair(v0[:rows], v1[:rows]),
            pair(v2[:rows], blank),
        ],
        axis=1,
    )
    other = jnp.concatenate(
        [pair(blank, k0[rows:]), pair(k1[rows:], k2[rows:]), pair(v0[rows:], v1[rows:]), pair(v2[rows:], blank)],
        axis=1,
    )
    own_sum = jnp.sum(own, axis=0, keepdims=True)
    other_sum = jnp.sum(other, axis=0, keepdims=True)
    sums_ref[0, :, 0:128] = own_sum[:, 0:128]
    sums_ref[0, :, 128:640] = own_sum[:, 128:] + other_sum
    own, other = own.astype(BF16), other.astype(BF16)
    grad_w = mul(own_t_ref[...], own)
    grad_w_other = mul(other_t_ref[...], other)
    grad_out = mul(grad_t_ref[...], ctx_ref[0])
    shape = (grad_w_ref.shape[0], 1, grad_w_ref.shape[2])
    grad_w_ref[:, :, :, 0:128] = grad_w[:, 0:128].astype(BF16).reshape(shape + (128,))
    grad_w_ref[:, :, :, 128:512] = (grad_w[:, 128:512] + grad_w_other[:, 0:384]).astype(BF16).reshape(shape + (384,))
    grad_w_ref[:, :, :, 512:640] = (
        (grad_w[:, 512:640] + grad_w_other[:, 384:512] + grad_out[:, 0:128]).astype(BF16).reshape(shape + (128,))
    )
    grad_w_ref[:, :, :, 640:768] = grad_out[:, 128:256].astype(BF16).reshape(shape + (128,))
    own_part = mul(own, weight(w_ref, 0, 640), NT)
    other_part = mul(other, weight(w_ref, 128, 640), NT)

    @pl.when(group == 0)
    def _():
        grad_own_ref[...] = own_part
        other_total_ref[...] = other_part

    @pl.when(group > 0)
    def _():
        grad_own_ref[...] += own_part
        other_total_ref[...] += other_part

    @pl.when(group == groups - 1)
    def _():
        grad_other_ref[...] = other_total_ref[...].astype(BF16)


def attend_back(grad, grad_t, own_t, other_t, weights, ctx, query, keys, values):
    rows, width = grad.shape
    groups = weights.shape[1]
    whole = lambda g: (0, 0)
    by_group = lambda g: (g, 0, 0)
    block = pl.BlockSpec((weights.shape[0], 1) + weights.shape[2:], lambda g: (0, g, 0, 0))
    flops = groups * (3 * 2 * rows * width * 640 + 3 * 10 * rows * SLOT * 128)
    return pl.pallas_call(
        attend_back_kernel,
        name="attend_back",
        grid=(groups,),
        in_specs=[
            pl.BlockSpec((rows, width), whole),
            pl.BlockSpec((width, rows), whole),
            pl.BlockSpec((width, rows), whole),
            pl.BlockSpec((width, rows), whole),
            block,
            pl.BlockSpec((1, rows, 256), by_group),
            pl.BlockSpec((3, rows, 128), by_group),
            pl.BlockSpec((3, SLOT, 128), by_group),
            pl.BlockSpec((3, SLOT, 128), by_group),
        ],
        out_specs=[
            block,
            pl.BlockSpec((rows, width), whole),
            pl.BlockSpec((rows, width), whole),
            pl.BlockSpec((1, 1, 640), by_group),
        ],
        out_shape=[
            jax.ShapeDtypeStruct(weights.shape, BF16),
            jax.ShapeDtypeStruct((rows, width), F32),
            jax.ShapeDtypeStruct((rows, width), BF16),
            jax.ShapeDtypeStruct((groups, 1, 640), F32),
        ],
        scratch_shapes=[pltpu.VMEM((rows, width), F32)],
        cost_estimate=pl.CostEstimate(flops=4 * flops, bytes_accessed=32 << 20, transcendentals=12 * rows * SLOT),
        compiler_params=pltpu.CompilerParams(vmem_limit_bytes=63 << 20),
    )(grad, grad_t, own_t, other_t, weights, ctx, query, keys, values)


def gather(local):
    return lax.all_gather(local, BOTH, axis=0, tiled=True)


def scatter(partial):
    return lax.psum_scatter(partial, BOTH, scatter_dimension=0, tiled=True)


def body(
    frames,
    w_qkv,
    b_qv,
    w_out,
    b_out,
    ln1_gain,
    ln1_bias,
    w_ff1,
    b_ff1,
    w_ff2,
    b_ff2,
    ln2_gain,
    ln2_bias,
    cotangent,
    clip_lengths,
    clip_slot,
):
    n_dp, n_mp = lax.axis_size("dp"), lax.axis_size("mp")
    rows, width = frames.shape
    part = w_ff1.shape[0]
    shape = (n_dp, n_mp, part, w_ff1.shape[1])
    share = b_out.shape[0]

    partner = [(m, m ^ 1) for m in range(n_mp)]
    other = lax.ppermute(frames, "mp", partner)
    packed = jnp.concatenate([w_qkv[0], w_qkv[1], w_qkv[2], w_out.T], axis=1)
    w_attn = gather(packed).reshape(shape)
    w1 = gather(w_ff1).reshape(shape)
    w2 = gather(w_ff2.T).reshape(shape)
    small = jnp.concatenate(
        [b_out, ln1_gain, ln1_bias, b_ff2, ln2_gain, ln2_bias, b_qv.reshape(-1).astype(F32), b_ff1.astype(F32)]
    )[None]
    small = gather(small)
    vectors = small[:, : 6 * share].reshape(n_dp * n_mp, 6, share).transpose(1, 0, 2).reshape(6, width)
    vectors = jnp.concatenate([vectors, jnp.zeros((2, width), F32)])
    ordered = small.reshape(n_dp, n_mp, -1).transpose(1, 0, 2)
    qv = ordered[:, :, 6 * share : 8 * share].reshape(n_mp, n_dp, 2, share).transpose(0, 2, 1, 3)
    qv = qv.reshape(n_mp, 2, 1, n_dp * share)
    heads_width = n_dp * share
    qv_bias = jnp.concatenate(
        [qv[:, 0], jnp.zeros((n_mp, 1, heads_width), F32), qv[:, 1], jnp.zeros((n_mp, 1, HEAD), F32)], axis=2
    )
    up_bias = ordered[:, :, 8 * share :].reshape(n_mp, 1, -1)

    index = lax.axis_index("dp") * n_mp + lax.axis_index("mp")
    slot = index // (SLOT // rows)
    half = index % (SLOT // rows)
    length = jnp.sum(jnp.where(clip_slot == slot, clip_lengths, 0))
    valid = jnp.stack([length - half * rows, length - (1 - half) * rows]).astype(jnp.int32)

    pre_one, ctx, query, keys, values = attend(valid, frames, other, w_attn, qv_bias, vectors[0:1])
    hidden, active, low, low_t = up(pre_one, vectors[1:2], vectors[2:3], w1, up_bias)
    output, grad_pre, grad_low, grad_low_t, grad_w2, grad_w1, sums, grad_up_bias = down(
        pre_one, cotangent, vectors, active, hidden, w2, w1, low_t
    )
    flat = (n_dp * n_mp * part, shape[3])
    done_w2 = scatter(grad_w2.reshape(flat))
    done_w1 = scatter(grad_w1.reshape(flat))
    grad_w, grad_own, grad_other, head_sums = attend_back(
        grad_low, grad_low_t, frames.T, other.T, w_attn, ctx, query, keys, values
    )
    returned = lax.ppermute(grad_other, "mp", partner)
    done_w = scatter(grad_w.reshape(flat)).astype(F32)
    grad_input = grad_pre + grad_own + returned.astype(F32)

    sums = sums[:6].reshape(6, n_dp * n_mp, share).transpose(1, 0, 2).reshape(n_dp * n_mp, 6 * share)
    head_sums = jnp.concatenate(
        [head_sums[:, :, :heads_width], head_sums[:, :, 2 * heads_width : 3 * heads_width]], axis=1
    )
    head_sums = head_sums.reshape(n_mp, 2, n_dp, share).transpose(2, 0, 1, 3).reshape(n_dp * n_mp, 2 * share)
    unit_sums = grad_up_bias.reshape(n_mp, n_dp, -1).transpose(1, 0, 2).reshape(n_dp * n_mp, -1)
    small = scatter(jnp.concatenate([sums, head_sums, unit_sums], axis=1))[0]
    (d_out_bias, d_gain1, d_shift1, d_down_bias, d_gain2, d_shift2) = [
        small[i * share : (i + 1) * share] for i in range(6)
    ]
    d_qv = small[6 * share : 8 * share].reshape(2, share)
    d_up_bias = small[8 * share :]
    d_qkv = jnp.stack([done_w[:, i * heads_width : (i + 1) * heads_width] for i in range(3)])
    return (
        output,
        grad_input,
        d_qkv,
        d_qv,
        done_w[:, 3 * heads_width :].T,
        d_out_bias,
        d_gain1,
        d_shift1,
        done_w1.astype(F32),
        d_up_bias,
        done_w2.astype(F32).T,
        d_down_bias,
        d_gain2,
        d_shift2,
    )


def solution(mesh):
    rows, vector, group_vector = P(BOTH, None), P(BOTH), P(("mp", "dp"))
    qkv, qv, out, up_spec = P(None, "dp", "mp"), P(None, ("mp", "dp")), P("mp", "dp"), P("dp", "mp")
    weights = (qkv, qv, out, vector, vector, vector, up_spec, group_vector, out, vector, vector, vector)
    return jax.shard_map(
        body,
        mesh=mesh,
        in_specs=(rows,) + weights + (rows, P(), P()),
        out_specs=(rows, rows) + weights,
        check_vma=False,
    )
```

time: 1330 us -> 656 us (0.49)
  waiting for transfers between devices: 639 us -> 340 us
  matrix products: 239 us -> 0 us
  Pallas kernels: 0 us -> 147 us
  local copies, waits for them, and re-layouts: 153 us -> 26.7 us
  other arithmetic: 109 us -> 12.4 us
  blocking collectives: 147 us -> 101 us
    dot_general x53 -> x0, matrix products: 234 us -> none  [the longest x12 50.2 us: one_block(): jnp.einsum('qhd,khd->hqk', query_block, keys, preferred_element_type=jnp....]
    all_gather x6 -> x3, waiting for transfers between devices: 301 us -> 76.8 us  [gather(): return lax.all_gather(local, BOTH, axis=0, tiled=True)]
    pallas_call x0 -> x4, Pallas kernels: none -> 147 us  [the longest x1 59.5 us: attend_back(): pl.pallas_call(attend_back_kernel, name='attend_back', grid=(groups,), in...]
    reduce_scatter x6 -> x2, waiting for transfers between devices: 336 us -> 219 us  [scatter(): return lax.psum_scatter(partial, BOTH, scatter_dimension=0, tiled=True)]
    convert_element_type x12 -> x2, other arithmetic: 67.9 us -> 1.67 us  [the longest x1 1.64 us: body(): done_w1.astype(F32)]
    dynamic_update_slice x8 -> x0, local copies, waits for them, and re-layouts: 46.3 us -> none  [body(): lax.map(lambda items: attend_slot(*items), (query, keys, values, slot_len...]
    unnamed x16 -> x7, waiting for transfers between devices: 1.91 us -> 43.4 us
    all_gather x3 -> x0, blocking collectives: 31.8 us -> none  [the longest x1 12.5 us: body(): lax.all_gather(w_qkv, 'dp', axis=1, tiled=True)]
  transfers between devices with their start and end apart: 14 -> 8, of which waited for: 10 -> 5; matrix products, arithmetic and copies ran while one was open for 8% -> 5% of each run, Pallas kernels for 0% -> 8%
where the time goes in v1:
time: 656 us; the launch traced here: 643 us
  waiting for transfers between devices  340 us (52%)
  Pallas kernels  147 us (22%)
  blocking collectives  101 us (15%)
  local copies, waits for them, and re-layouts  26.7 us (4%)
  between operations  16 us (2%)
  other arithmetic  12.4 us (2%)
    reduce_scatter x2, waiting for transfers between devices, scatter(): return lax.psum_scatter(partial, BOTH, scatter_dimension=0, tiled=True)  219 us
    unnamed x2, blocking collectives  101 us
    all_gather x3, waiting for transfers between devices, gather(): return lax.all_gather(local, BOTH, axis=0, tiled=True)  76.8 us
    pallas_call x1, Pallas kernels, attend_back(): pl.pallas_call(attend_back_kernel, name='attend_back', grid=(groups,), in...  59.5 us
    unnamed x7, waiting for transfers between devices  43.4 us
    pallas_call x1, Pallas kernels, attend(): pl.pallas_call(attend_kernel, name='attend', grid=(groups,), in_specs=[pl...  39.3 us
    pallas_call x1, Pallas kernels, down(): pl.pallas_call(functools.partial(down_kernel, groups), name='down', grid=...  36.2 us
  transfers between devices with their start and end apart: 8, of which 5 were waited for; matrix products, arithmetic and copies ran while one was open for 5% of the time, Pallas kernels for 8%

profile of v1, /device:TPU:8, one launch (start us, length us, event | category | flops | bytes accessed | tf_op | source)
XLA Modules:
  0.0 642.9 jit_solution(1656733894305385428)
XLA Ops:
  11.4 1.6 copy.100
  13.6 57.5 %all-reduce.1 = f32[9216]{0:T(1024)S(1)} all-reduce(f32[9216]{0:T(1024)S(1)} %dynamic-update-slice), channel_id=2, replica_groups=mesh['dp'=8,'mp'=4] {'dp','mp'}, use_global_device_ids=true, to_apply=%add.1 | all-reduce | flops 9216 | bytes 73728
  78.9 1.4 copy.105.other_ref
  80.4 39.3 %attend.1 = (f32[768,768]{1,0:T(8,128)}, bf16[4,768,256]{2,1,0:T(8,128)(2,1)}, bf16[12,768,128]{2,1,0:T(8,128)(2,1)}, bf16[12,1536,128]{2,1,0:T(8,128)(2,1)}, bf16[12,1536,128]{2,1,0:T(8,128)(2,1)}) custom-call(s32[2]{0:T(128)} %pad_add_fusion.valid_ref, bf16[768,768]{1,0:T(8,128)(2,1)} %own_ref.1, bf16[768,768]{1,0:T(8,128)(2,1)} %copy.105.other_ref, ...), custom_call_target="tpu_custom_call" | custom-call | flops 53150220288 | bytes 25165824 | tf_op jit(solution)/shard_map/attend/pallas_call | solution.py:131
  119.7 23.6 %all-gather.7.cloned.1.call-done = bf16[3072,768]{1,0:T(8,128)(2,1)} async-done(((bf16[96,768]{1,0:T(8,128)(2,1)}), bf16[3072,768]{1,0:T(8,128)(2,1)}) %all-gather.7.cloned.1.call-update) | async-done | bytes 4718608 | tf_op jit(solution)/shard_map/all_gather | solution.py:493
  143.3 11.5 %up.1 = (f32[4,768,768]{2,1,0:T(8,128)}, bf16[4,768,768]{2,1,0:T(8,128)(2,1)}, bf16[768,768]{1,0:T(8,128)(2,1)}, bf16[768,768]{1,0:T(8,128)(2,1)}) custom-call(f32[768,768]{1,0:T(8,128)} %get-tuple-element.34.pre_ref, f32[1,768]{1,0:T(1,128)} %slice.119.gain_ref, f32[1,768]{1,0:T(1,128)} %slice.121.shift_ref, bf16[8,4,96,768]{3,2,1,0:T(8,128)(2,1)} %bitcast.74, ...), custom_call_target="tpu_custom_call" | custom-call | flops 3623878656 | bytes 25165824 | tf_op jit(solution)/shard_map/up/pallas_call | solution.py:180
  154.8 53.2 %all-gather.9.cloned.1.call-done = bf16[3072,768]{1,0:T(8,128)(2,1)} async-done(((bf16[96,768]{1,0:T(8,128)(2,1)}), bf16[3072,768]{1,0:T(8,128)(2,1)}) %all-gather.9.cloned.1.call-update) | async-done | bytes 4718608 | tf_op jit(solution)/shard_map/all_gather | solution.py:493
  208.0 36.2 %down.1 = (bf16[768,768]{1,0:T(8,128)(2,1)}, f32[768,768]{1,0:T(8,128)}, bf16[768,768]{1,0:T(8,128)(2,1)}, bf16[768,768]{1,0:T(8,128)(2,1)}, bf16[8,4,96,768]{3,...) custom-call(f32[768,768]{1,0:T(8,128)} %get-tuple-element.34.pre_ref, ...), custom_call_target="tpu_custom_call" | custom-call | flops 18119393280 | bytes 50331648 | tf_op jit(solution)/shard_map/down/pallas_call | solution.py:309
  244.2 59.5 %attend_back.1 = (bf16[8,4,96,768]{3,2,1,0:T(8,128)(2,1)}, f32[768,768]{1,0:T(8,128)}, bf16[768,768]{1,0:T(8,128)(2,1)}, f32[4,1,640]{2,1,0:T(1,128)}) custom-call(bf16[768,768]{1,0:T(8,128)(2,1)} %get-tuple-element.40.grad_ref, bf16[768,768]{1,0:T(8,128)(2,1)} %get-tuple-element.41.grad_t_ref, bf16[768,768]{1,0:T(8,128)(2,1)} %bitcast.58, ...), custom_call_target="tpu_custom_call" | custom-call | flops 108716359680 | bytes 33554432 | tf_op jit(solution)/shard_map/attend_back/pallas_call | solution.py:459
  306.4 1.4 copy.124
  309.3 1.5 reshape.110
  310.8 1.6 copy.112
  312.4 1.3 reduce
  315.1 1.4 copy.116
  316.6 1.6 pad_maximum_fusion.2
  318.2 43.2 %all-reduce.2 = f32[32,288]{0,1:T(8,128)} all-reduce(f32[32,288]{0,1:T(8,128)} %pad_maximum_fusion.2), channel_id=4, replica_groups=mesh['dp'=8,'mp'=4] {'dp','mp'}, use_global_device_ids=true, to_apply=%region_2.3.clone | all-reduce | flops 9216 | bytes 73728
  363.0 1.5 dynamic-slice_reduce_fusion
  364.5 1.6 dynamic-slice_reduce_fusion.2
  366.1 3.5 convert_add_fusion
  369.6 41.0 %reduce-scatter.11.cloned.1.call-done = bf16[96,768]{1,0:T(8,128)(2,1)} async-done(((bf16[3072,768]{1,0:T(8,128)(2,1)}), bf16[96,768]{1,0:T(8,128)(2,1)}) %reduce-scatter.11.cloned.1.call-update) | async-done | bytes 147472
  413.3 109.1 %reduce-scatter.9.cloned.1.call-done = bf16[96,768]{1,0:T(8,128)(2,1)} async-done(((bf16[3072,768]{1,0:T(8,128)(2,1)}), bf16[96,768]{1,0:T(8,128)(2,1)}) %reduce-scatter.9.cloned.1.call-update) | async-done | bytes 147472 | tf_op jit(solution)/shard_map/reduce_scatter | solution.py:497
  522.4 1.6 convert_bitcast_fusion
  524.0 110.2 %reduce-scatter.7.cloned.1.call-done = bf16[96,768]{1,0:T(8,128)(2,1)} async-done(((bf16[3072,768]{1,0:T(8,128)(2,1)}), bf16[96,768]{1,0:T(8,128)(2,1)}) %reduce-scatter.7.cloned.1.call-update) | async-done | bytes 147472 | tf_op jit(solution)/shard_map/reduce_scatter | solution.py:497
  634.2 1.6 convert_element_type.24
  (95 shorter events, 20.8 us)
Async XLA Ops:
  7.2 5.9 copy-start.13
  7.2 6.0 copy-start.4
  7.2 6.0 copy-start.5
  7.2 6.0 copy-start.6
  7.2 6.0 copy-start.10
  7.2 6.0 copy-start.7
  7.2 6.0 copy-start.8
  7.3 6.0 copy-start.9
  7.3 64.3 %copy-start.11 = (s32[16]{0:T(128)S(1)}, s32[16]{0:T(128)}, u32[]{:S(2)}) copy-start(s32[16]{0:T(128)} %param.30) | copy-start | bytes 196
  7.3 64.2 %copy-start.12 = (s32[16]{0:T(128)S(1)}, s32[16]{0:T(128)}, u32[]{:S(2)}) copy-start(s32[16]{0:T(128)} %param.31) | copy-start | bytes 196
  7.3 73.1 %all-gather.5.cloned.1.call-start = ((), (), s32[]{:S(2)}) async-start(), calls=%async_computation.3 | async-start | bytes 4866048 | tf_op jit(solution)/shard_map/all_gather | solution.py:493
  9.9 133.4 %all-gather.7.cloned.1.call-start = ((), (), s32[]{:S(2)}) async-start(), calls=%async_computation.4 | async-start | bytes 4866048 | tf_op jit(solution)/shard_map/all_gather | solution.py:493
  10.6 197.4 %all-gather.9.cloned.1.call-start = ((), (), s32[]{:S(2)}) async-start(), calls=%async_computation.5 | async-start | bytes 4866048 | tf_op jit(solution)/shard_map/all_gather | solution.py:493
  11.4 399.2 %reduce-scatter.11.cloned.1.call-start = ((), (), s32[]{:S(2)}) async-start(), calls=%async_computation.8 | async-start | bytes 4866048
  13.0 106.7 %copy-start.1 = (bf16[768,768]{0,1:T(8,128)(2,1)}, bf16[768,768]{0,1:T(8,128)(2,1)S(1)}, u32[]{:S(2)}) copy-start(bf16[768,768]{0,1:T(8,128)(2,1)S(1)} %copy.100) | copy-start | bytes 3538948
  13.0 65.9 %collective-permute-start = (bf16[768,768]{0,1:T(8,128)(2,1)S(1)}, bf16[768,768]{0,1:T(8,128)(2,1)S(1)}, u32[]{:S(2)}, u32[]{:S(2)}) collective-permute-start(bf16[768,768]{0,1:T(8,128)(2,1)S(1)} %copy.100), channel_id=1, source_target_pairs={{0,1},{1,0},{2,3},{3,2},{4,5},{5,4},{6,7},{7,6},{8,9},{9,8},{10,11... | collective-permute-start | bytes 3538952 | tf_op jit(solution)/shard_map/ppermute | solution.py:525
  78.9 40.7 %copy-start.2 = (bf16[768,768]{0,1:T(8,128)(2,1)}, bf16[768,768]{0,1:T(8,128)(2,1)S(1)}, u32[]{:S(2)}) copy-start(bf16[768,768]{0,1:T(8,128)(2,1)S(1)} %collective-permute-done) | copy-start | bytes 3538948
  303.8 218.6 %reduce-scatter.9.cloned.1.call-start = ((), (), s32[]{:S(2)}) async-start(), calls=%async_computation.7 | async-start | bytes 4866048 | tf_op jit(solution)/shard_map/reduce_scatter | solution.py:497
  304.4 329.9 %reduce-scatter.7.cloned.1.call-start = ((), (), s32[]{:S(2)}) async-start(), calls=%async_computation.6 | async-start | bytes 4866048 | tf_op jit(solution)/shard_map/reduce_scatter | solution.py:497
  304.4 1.2 copy-start.3
  304.4 61.7 %copy-start = (f32[768,768]{1,0:T(8,128)S(1)}, f32[768,768]{1,0:T(8,128)}, u32[]{:S(2)}) copy-start(f32[768,768]{1,0:T(8,128)} %get-tuple-element.39) | copy-start | bytes 7077892
  304.9 61.1 %collective-permute-start.1 = (bf16[768,768]{1,0:T(8,128)(2,1)}, bf16[768,768]{1,0:T(8,128)(2,1)S(1)}, u32[]{:S(2)}, u32[]{:S(2)}) collective-permute-start(bf16[768,768]{1,0:T(8,128)(2,1)} %get-tuple-element.47), channel_id=1, source_target_pairs={{0,1},{1,0},{2,3},{3,2},{4,5},{5,4},{6,7},{7,6},{8,9},{9,8},{10,11... | collective-permute-start | bytes 3538952 | tf_op jit(solution)/shard_map/ppermute | solution.py:562
Sparse Core Ops, SparseCore 0:
  11.5 66.8 all-gather.4
  81.1 62.0 all-gather.6
  146.1 61.8 all-gather.8
  303.9 106.6 reduce-scatter.10
  415.9 106.4 reduce-scatter.8
  527.7 106.4 reduce-scatter.6

commit v2 on v1

--- a/solution.py
+++ b/solution.py
@@ -15,6 +15,7 @@
 BOTH = ("dp", "mp")
 F32 = jnp.float32
 BF16 = jnp.bfloat16
+MESH = pl.DeviceIdType.MESH
 NN = (((1,), (0,)), ((), ()))
 NT = (((1,), (1,)), ((), ()))
 
@@ -489,12 +490,408 @@
     )(grad, grad_t, own_t, other_t, weights, ctx, query, keys, values)
 
 
-def gather(local):
-    return lax.all_gather(local, BOTH, axis=0, tiled=True)
-
-
-def scatter(partial):
-    return lax.psum_scatter(partial, BOTH, scatter_dimension=0, tiled=True)
+CORE, ALONG_X, ALONG_Y = 1, 2, 4
+DIAGONAL = ALONG_X | ALONG_Y
+COLUMNS = (0, ALONG_X, ALONG_Y, DIAGONAL)
+
+
+def meet(me, z, depth):
+    barrier = pltpu.get_barrier_semaphore()
+    for bit in (CORE, ALONG_X, ALONG_Y):
+        pl.semaphore_signal(barrier, inc=1, device_id=(me ^ bit, z), device_id_type=MESH)
+
+    @pl.when(z > 0)
+    def _():
+        pl.semaphore_signal(barrier, inc=1, device_id=(me, z - 1), device_id_type=MESH)
+
+    @pl.when(z < depth - 1)
+    def _():
+        pl.semaphore_signal(barrier, inc=1, device_id=(me, z + 1), device_id_type=MESH)
+
+    pl.semaphore_wait(barrier, 3 + (z > 0).astype(jnp.int32) + (z < depth - 1).astype(jnp.int32))
+
+
+def near_first(z, depth):
+    yield z, None
+    for distance in range(1, depth):
+        for place in (z - distance, z + distance):
+            yield place, (place >= 0) & (place < depth)
+
+
+def given(condition, action):
+    if condition is None:
+        action()
+    else:
+        pl.when(condition)(action)
+
+
+def halves(rows):
+    return (rows // 2, rows) if rows % 32 == 0 else (rows, rows)
+
+
+UP, DOWN, X, Y, VIA_Y, VIA_X, C0 = range(7)
+GATHER_KINDS = C0 + 4
+
+
+def gather_kernel(count, depth, *refs):
+    locals_, wholes = refs[:count], refs[count : 2 * count]
+    send_sem, recv_sem = refs[2 * count :]
+    me, z = lax.axis_index("dp"), lax.axis_index("mp")
+
+    def copy(which, kind, place, source, target, to):
+        return pltpu.make_async_remote_copy(
+            src_ref=source,
+            dst_ref=target,
+            send_sem=send_sem.at[which, kind, place],
+            recv_sem=recv_sem.at[which, kind, place],
+            device_id=to,
+            device_id_type=MESH,
+        )
+
+    meet(me, z, depth)
+
+    def column(which, place, source, owner, kinds):
+        whole = wholes[which]
+        for kind, to, first, last in kinds:
+            view = source if first == 0 and last == source.shape[0] else source.at[first:last]
+            copy(which, kind, place, view, whole.at[owner, place, first:last], to).start()
+
+    def arrived(which, kind, place, owner, first, last):
+        view = wholes[which].at[owner, place, first:last]
+        copy(which, kind, place, view, view, (me, z)).wait_recv()
+
+    def first_stage(which, place, condition):
+        rows = locals_[which].shape[0]
+
+        def act():
+            own = condition is None
+            source = locals_[which] if own else wholes[which].at[me, place]
+            if not own:
+                pl.when(place < z)(lambda: arrived(which, UP, place, me, 0, rows))
+                pl.when(place > z)(lambda: arrived(which, DOWN, place, me, 0, rows))
+            up_from = (z < depth - 1) if own else (place < z) & (z < depth - 1)
+            down_from = (z > 0) if own else (place > z) & (z > 0)
+            pl.when(up_from)(lambda: column(which, place, source, me, [(UP, (me, z + 1), 0, rows)]))
+            pl.when(down_from)(lambda: column(which, place, source, me, [(DOWN, (me, z - 1), 0, rows)]))
+            column(
+                which,
+                place,
+                source,
+                me,
+                [
+                    (X, (me ^ ALONG_X, z), 0, rows),
+                    (Y, (me ^ ALONG_Y, z), 0, rows),
+                    (C0, (me ^ CORE, z), 0, rows),
+                ],
+            )
+
+        given(condition, act)
+
+    def second_stage(which, place, condition):
+        rows = locals_[which].shape[0]
+        half, _ = halves(rows)
+
+        def act():
+            arrived(which, X, place, me ^ ALONG_X, 0, rows)
+            source = wholes[which].at[me ^ ALONG_X, place]
+            column(
+                which,
+                place,
+                source,
+                me ^ ALONG_X,
+                [(VIA_Y, (me ^ ALONG_Y, z), 0, half), (C0 + 1, (me ^ CORE, z), 0, rows)],
+            )
+            arrived(which, Y, place, me ^ ALONG_Y, 0, rows)
+            source = wholes[which].at[me ^ ALONG_Y, place]
+            kinds = [(C0 + 2, (me ^ CORE, z), 0, rows)]
+            if half < rows:
+                kinds = [(VIA_X, (me ^ ALONG_X, z), half, rows)] + kinds
+            column(which, place, source, me ^ ALONG_Y, kinds)
+
+        given(condition, act)
+
+    def third_stage(which, place, condition):
+        rows = locals_[which].shape[0]
+        half, _ = halves(rows)
+
+        def act():
+            arrived(which, VIA_Y, place, me ^ DIAGONAL, 0, half)
+            if half < rows:
+                arrived(which, VIA_X, place, me ^ DIAGONAL, half, rows)
+            source = wholes[which].at[me ^ DIAGONAL, place]
+            column(which, place, source, me ^ DIAGONAL, [(C0 + 3, (me ^ CORE, z), 0, rows)])
+
+        given(condition, act)
+
+    def last_stage(which, place):
+        rows = locals_[which].shape[0]
+        for number, bit in enumerate(COLUMNS):
+            arrived(which, C0 + number, place, me ^ CORE ^ bit, 0, rows)
+
+    order = []
+    for which in range(count):
+        pltpu.make_async_copy(
+            locals_[which], wholes[which].at[me, z], send_sem.at[which, GATHER_KINDS, 0]
+        ).start()
+        order += [(which,) + item for item in near_first(z, depth)]
+    lag = len(order) // count
+    for step in range(len(order) + 2 * lag):
+        if step < len(order):
+            first_stage(*order[step])
+        if 0 <= step - lag < len(order):
+            second_stage(*order[step - lag])
+        if 0 <= step - 2 * lag:
+            third_stage(*order[step - 2 * lag])
+    for which in range(count):
+        rows = locals_[which].shape[0]
+        half, _ = halves(rows)
+        for place in range(depth):
+            last_stage(which, place)
+        for place, condition in near_first(z, depth):
+
+            def sent(which=which, place=place, own=condition is None):
+                whole = wholes[which].at[me, place]
+                pieces = [(X, 0, rows), (Y, 0, rows), (VIA_Y, 0, half)] + [(C0 + n, 0, rows) for n in range(4)]
+                if half < rows:
+                    pieces.append((VIA_X, half, rows))
+                for kind, first, last in pieces:
+                    view = whole.at[first:last]
+                    copy(which, kind, place, view, view, (me, z)).wait_send()
+                up_from = (z < depth - 1) if own else (place < z) & (z < depth - 1)
+                down_from = (z > 0) if own else (place > z) & (z > 0)
+                pl.when(up_from)(lambda: copy(which, UP, place, whole, whole, (me, z)).wait_send())
+                pl.when(down_from)(lambda: copy(which, DOWN, place, whole, whole, (me, z)).wait_send())
+
+            given(condition, sent)
+        pltpu.make_async_copy(
+            locals_[which], wholes[which].at[me, z], send_sem.at[which, GATHER_KINDS, 0]
+        ).wait()
+
+
+def gather_all(locals_, n_dp, n_mp, number):
+    count = len(locals_)
+    sems = pltpu.SemaphoreType.DMA((count, GATHER_KINDS + 1, n_mp))
+    return pl.pallas_call(
+        functools.partial(gather_kernel, count, n_mp),
+        name="gather",
+        in_specs=[pl.BlockSpec(memory_space=pltpu.VMEM)] * count,
+        out_specs=[pl.BlockSpec(memory_space=pl.ANY)] * count,
+        out_shape=[jax.ShapeDtypeStruct((n_dp, n_mp) + a.shape, a.dtype) for a in locals_],
+        scratch_shapes=[sems, sems],
+        compiler_params=pltpu.CompilerParams(collective_id=number, has_side_effects=True),
+    )(*locals_)
+
+
+TO_X, TO_Y, X_LOW, X_HIGH, Y_LOW, Y_HIGH, Z_UP, Z_DOWN, S0 = range(9)
+SCATTER_KINDS = S0 + 4
+
+
+def scatter_kernel(count, depth, *refs):
+    partials, outs = refs[:count], refs[count : 2 * count]
+    scratch = refs[2 * count : -2]
+    send_sem, recv_sem = refs[-2:]
+    me, z = lax.axis_index("dp"), lax.axis_index("mp")
+
+    def copy(which, kind, place, source, target, to):
+        return pltpu.make_async_remote_copy(
+            src_ref=source,
+            dst_ref=target,
+            send_sem=send_sem.at[which, kind, place],
+            recv_sem=recv_sem.at[which, kind, place],
+            device_id=to,
+            device_id_type=MESH,
+        )
+
+    def bufs(which):
+        return scratch[4 * which : 4 * which + 4]
+
+    def add(target, *others):
+        total = target[...].astype(F32)
+        for other in others:
+            total = total + other[...].astype(F32)
+        target[...] = total.astype(target.dtype)
+
+    meet(me, z, depth)
+    started = []
+
+    def start(which, kind, place, source, target, to):
+        copy(which, kind, place, source, target, to).start()
+        started.append((which, kind, place, source, target))
+
+    def wait(which, kind, place, view):
+        copy(which, kind, place, view, view, (me, z)).wait_recv()
+
+    places = [depth - 1, 0] + list(range(1, depth - 1))[::-1]
+    order = [(which, place) for which in range(count) for place in places]
+    for which, place in order:
+        core = bufs(which)[0]
+        for number in (3, 1, 2, 0):
+            start(
+                which,
+                S0 + number,
+                place,
+                partials[which].at[me ^ CORE ^ COLUMNS[number], place],
+                core.at[number, place],
+                (me ^ CORE, z),
+            )
+
+    def first_stage(which, place):
+        core, diagonal, sides, _ = bufs(which)
+        rows = core.shape[2]
+        half, _ = halves(rows)
+        to_x, to_y = (me ^ ALONG_X, z), (me ^ ALONG_Y, z)
+        for number in (3, 1, 2, 0):
+            view = core.at[number, place]
+            wait(which, S0 + number, place, view)
+            add(view, partials[which].at[me ^ COLUMNS[number], place])
+            if number == 3:
+                start(which, TO_X, place, view.at[0:half], diagonal.at[place, 0:half], to_x)
+                if half < rows:
+                    start(which, TO_Y, place, view.at[half:rows], diagonal.at[place, half:rows], to_y)
+            if number == 1:
+                if half < rows:
+                    start(which, X_LOW, place, view.at[0:half], sides.at[0, place, 0:half], to_x)
+                else:
+                    start(which, X_LOW, place, view, sides.at[0, place], to_x)
+            if number == 2 and half < rows:
+                start(which, Y_HIGH, place, view.at[half:rows], sides.at[1, place, half:rows], to_y)
+
+    def second_stage(which, place):
+        core, diagonal, sides, _ = bufs(which)
+        rows = core.shape[2]
+        half, _ = halves(rows)
+        view = diagonal.at[place, 0:half]
+        wait(which, TO_X, place, view)
+        mine = core.at[2, place, 0:half]
+        add(mine, view)
+        start(which, Y_LOW, place, mine, sides.at[1, place, 0:half], (me ^ ALONG_Y, z))
+        if half < rows:
+            view = diagonal.at[place, half:rows]
+            wait(which, TO_Y, place, view)
+            mine = core.at[1, place, half:rows]
+            add(mine, view)
+            start(which, X_HIGH, place, mine, sides.at[0, place, half:rows], (me ^ ALONG_X, z))
+
+    def third_stage(which, place):
+        core, _, sides, _ = bufs(which)
+        rows = core.shape[2]
+        half, _ = halves(rows)
+        wait(which, X_LOW, place, sides.at[0, place, 0:half])
+        wait(which, Y_LOW, place, sides.at[1, place, 0:half])
+        if half < rows:
+            wait(which, Y_HIGH, place, sides.at[1, place, half:rows])
+            wait(which, X_HIGH, place, sides.at[0, place, half:rows])
+        add(core.at[0, place], sides.at[0, place], sides.at[1, place])
+
+    for step in range(len(order) + 4):
+        if step < len(order):
+            first_stage(*order[step])
+        if 0 <= step - 2 < len(order):
+            second_stage(*order[step - 2])
+        if 0 <= step - 4:
+            third_stage(*order[step - 4])
+
+    for which in range(count):
+        core, _, _, line = bufs(which)
+
+        def send(kind, place, to, which=which, core=core, line=line):
+            way = 0 if kind == Z_UP else 1
+            copy(which, kind, place, core.at[0, place], line.at[way, place], (me, to)).start()
+
+        for distance in range(depth - 1, 0, -1):
+            above, below = z + distance, z - distance
+
+            @pl.when(above < depth)
+            def _(above=above):
+                @pl.when(z > 0)
+                def _():
+                    wait(which, Z_UP, above, line.at[0, above])
+                    add(core.at[0, above], line.at[0, above])
+
+                send(Z_UP, above, z + 1)
+
+            @pl.when(below >= 0)
+            def _(below=below):
+                @pl.when(z < depth - 1)
+                def _():
+                    wait(which, Z_DOWN, below, line.at[1, below])
+                    add(core.at[0, below], line.at[1, below])
+
+                send(Z_DOWN, below, z - 1)
+
+    for which in range(count):
+        core, _, _, line = bufs(which)
+        outs[which][...] = core[0, z].astype(F32)
+
+        @pl.when(z > 0)
+        def _():
+            wait(which, Z_UP, z, line.at[0, z])
+            outs[which][...] += line[0, z].astype(F32)
+
+        @pl.when(z < depth - 1)
+        def _():
+            wait(which, Z_DOWN, z, line.at[1, z])
+            outs[which][...] += line[1, z].astype(F32)
+
+        for distance in range(depth - 1, 0, -1):
+            above, below = z + distance, z - distance
+
+            @pl.when(above < depth)
+            def _(above=above):
+                copy(which, Z_UP, above, core.at[0, above], line.at[0, above], (me, z)).wait_send()
+
+            @pl.when(below >= 0)
+            def _(below=below):
+                copy(which, Z_DOWN, below, core.at[0, below], line.at[1, below], (me, z)).wait_send()
+
+    for which, kind, place, source, target in started:
+        copy(which, kind, place, source, target, (me, z)).wait_send()
+
+
+def scatter_all(partials, number):
+    count = len(partials)
+    n_mp = partials[0].shape[1]
+    sems = pltpu.SemaphoreType.DMA((count, SCATTER_KINDS, n_mp))
+    scratch = []
+    for a in partials:
+        block = a.shape[2:]
+        scratch += [
+            pltpu.VMEM((4, n_mp) + block, a.dtype),
+            pltpu.VMEM((n_mp,) + block, a.dtype),
+            pltpu.VMEM((2, n_mp) + block, a.dtype),
+            pltpu.VMEM((2, n_mp) + block, a.dtype),
+        ]
+    return pl.pallas_call(
+        functools.partial(scatter_kernel, count, n_mp),
+        name="scatter",
+        in_specs=[pl.BlockSpec(memory_space=pltpu.VMEM)] * count,
+        out_specs=[pl.BlockSpec(memory_space=pltpu.VMEM)] * count,
+        out_shape=[jax.ShapeDtypeStruct(a.shape[2:], F32) for a in partials],
+        scratch_shapes=scratch + [sems, sems],
+        compiler_params=pltpu.CompilerParams(
+            collective_id=number, has_side_effects=True, vmem_limit_bytes=60 << 20
+        ),
+    )(*partials)
+
+
+def blocks(local, mesh_shape):
+    return lax.all_gather(local, BOTH, axis=0, tiled=False).reshape(mesh_shape + local.shape)
+
+
+def gather_first(locals_, mesh_shape):
+    if mesh_shape[0] == 8:
+        return gather_all(locals_, *mesh_shape, number=1)
+    return [blocks(local, mesh_shape) for local in locals_]
+
+
+def scatter_sums(partials, number):
+    if partials[0].shape[0] == 8:
+        return scatter_all(partials, number)
+    done = []
+    for partial in partials:
+        flat = partial.reshape((-1,) + partial.shape[3:])
+        done.append(lax.psum_scatter(flat, BOTH, scatter_dimension=0, tiled=True).astype(F32))
+    return done
 
 
 def body(
@@ -517,20 +914,20 @@
 ):
     n_dp, n_mp = lax.axis_size("dp"), lax.axis_size("mp")
     rows, width = frames.shape
-    part = w_ff1.shape[0]
-    shape = (n_dp, n_mp, part, w_ff1.shape[1])
     share = b_out.shape[0]
 
     partner = [(m, m ^ 1) for m in range(n_mp)]
     other = lax.ppermute(frames, "mp", partner)
     packed = jnp.concatenate([w_qkv[0], w_qkv[1], w_qkv[2], w_out.T], axis=1)
-    w_attn = gather(packed).reshape(shape)
-    w1 = gather(w_ff1).reshape(shape)
-    w2 = gather(w_ff2.T).reshape(shape)
     small = jnp.concatenate(
         [b_out, ln1_gain, ln1_bias, b_ff2, ln2_gain, ln2_bias, b_qv.reshape(-1).astype(F32), b_ff1.astype(F32)]
-    )[None]
-    small = gather(small)
+    )
+    entries = small.shape[0]
+    small = jnp.pad(small, (0, -entries % 1024)).reshape(-1, 128)
+    mesh_shape = (n_dp, n_mp)
+    w_attn, small = gather_first([packed, small], mesh_shape)
+    w1, w2 = blocks(w_ff1, mesh_shape), blocks(w_ff2.T, mesh_shape)
+    small = small.reshape(n_dp * n_mp, -1)[:, :entries]
     vectors = small[:, : 6 * share].reshape(n_dp * n_mp, 6, share).transpose(1, 0, 2).reshape(6, width)
     vectors = jnp.concatenate([vectors, jnp.zeros((2, width), F32)])
     ordered = small.reshape(n_dp, n_mp, -1).transpose(1, 0, 2)
@@ -553,14 +950,11 @@
     output, grad_pre, grad_low, grad_low_t, grad_w2, grad_w1, sums, grad_up_bias = down(
         pre_one, cotangent, vectors, active, hidden, w2, w1, low_t
     )
-    flat = (n_dp * n_mp * part, shape[3])
-    done_w2 = scatter(grad_w2.reshape(flat))
-    done_w1 = scatter(grad_w1.reshape(flat))
+    done_w2, done_w1 = scatter_sums([grad_w2, grad_w1], 2)
     grad_w, grad_own, grad_other, head_sums = attend_back(
         grad_low, grad_low_t, frames.T, other.T, w_attn, ctx, query, keys, values
     )
     returned = lax.ppermute(grad_other, "mp", partner)
-    done_w = scatter(grad_w.reshape(flat)).astype(F32)
     grad_input = grad_pre + grad_own + returned.astype(F32)
 
     sums = sums[:6].reshape(6, n_dp * n_mp, share).transpose(1, 0, 2).reshape(n_dp * n_mp, 6 * share)
@@ -569,12 +963,15 @@
     )
     head_sums = head_sums.reshape(n_mp, 2, n_dp, share).transpose(2, 0, 1, 3).reshape(n_dp * n_mp, 2 * share)
     unit_sums = grad_up_bias.reshape(n_mp, n_dp, -1).transpose(1, 0, 2).reshape(n_dp * n_mp, -1)
-    small = scatter(jnp.concatenate([sums, head_sums, unit_sums], axis=1))[0]
+    small = jnp.concatenate([sums, head_sums, unit_sums], axis=1)
+    small = jnp.pad(small, ((0, 0), (0, -entries % 1024))).reshape(mesh_shape + (-1, 128))
+    done_w, small = scatter_sums([grad_w, small], 3)
+    small = small.reshape(-1)
     (d_out_bias, d_gain1, d_shift1, d_down_bias, d_gain2, d_shift2) = [
         small[i * share : (i + 1) * share] for i in range(6)
     ]
     d_qv = small[6 * share : 8 * share].reshape(2, share)
-    d_up_bias = small[8 * share :]
+    d_up_bias = small[8 * share : entries]
     d_qkv = jnp.stack([done_w[:, i * heads_width : (i + 1) * heads_width] for i in range(3)])
     return (
         output,
@@ -585,9 +982,9 @@
         d_out_bias,
         d_gain1,
         d_shift1,
-        done_w1.astype(F32),
+        done_w1,
         d_up_bias,
-        done_w2.astype(F32).T,
+        done_w2.T,
         d_down_bias,
         d_gain2,
         d_shift2,

time: 656 us -> 394 us (0.60); the launches traced: 643 us -> 389 us
  waiting for transfers between devices: 340 us -> 13.6 us
  Pallas kernels: 147 us -> 334 us
  blocking collectives: 101 us -> 0 us
  local copies, waits for them, and re-layouts: 26.7 us -> 18 us
    reduce_scatter x2 -> x0, waiting for transfers between devices: 219 us -> none  [scatter(): return lax.psum_scatter(partial, BOTH, scatter_dimension=0, tiled=True)]
    pallas_call x0 -> x3, Pallas kernels: none -> 187 us  [the longest x2 121 us: scatter_all(): pl.pallas_call(functools.partial(scatter_kernel, count, n_mp), name='scat...]
    unnamed x2 -> x0, blocking collectives: 101 us -> none
    all_gather x3 -> x2, waiting for transfers between devices: 76.8 us -> 12.2 us  [blocks(): lax.all_gather(local, BOTH, axis=0, tiled=False)]
    unnamed x7 -> x2, waiting for transfers between devices: 43.4 us -> 1.38 us
  transfers between devices with their start and end apart: 8 -> 4, of which waited for: 5 -> 1; matrix products, arithmetic and copies ran while one was open for 5% -> 5% of each run, Pallas kernels for 8% -> 61%
where the time goes in v2:
time: 394 us; the launch traced here: 389 us
  Pallas kernels  334 us (85%)
  local copies, waits for them, and re-layouts  18 us (5%)
  between operations  16 us (4%)
  waiting for transfers between devices  13.6 us (3%)
  other arithmetic  6.98 us (2%)
    pallas_call x2, Pallas kernels, scatter_all(): pl.pallas_call(functools.partial(scatter_kernel, count, n_mp), name='scat...  121 us
    pallas_call x1, Pallas kernels, gather_all(): pl.pallas_call(functools.partial(gather_kernel, count, n_mp), name='gathe...  66.2 us
    pallas_call x1, Pallas kernels, attend_back(): pl.pallas_call(attend_back_kernel, name='attend_back', grid=(groups,), in...  59.7 us
    pallas_call x1, Pallas kernels, attend(): pl.pallas_call(attend_kernel, name='attend', grid=(groups,), in_specs=[pl...  39.3 us
    pallas_call x1, Pallas kernels, down(): pl.pallas_call(functools.partial(down_kernel, groups), name='down', grid=...  36.4 us
    all_gather x2, waiting for transfers between devices, blocks(): lax.all_gather(local, BOTH, axis=0, tiled=False)  12.2 us
    pallas_call x1, Pallas kernels, up(): pl.pallas_call(up_kernel, name='up', grid=(groups,), in_specs=[pl.BlockSp...  11.3 us
  transfers between devices with their start and end apart: 4, of which 1 were waited for; matrix products, arithmetic and copies ran while one was open for 5% of the time, Pallas kernels for 61%

profile of v2, /device:TPU:8, one launch (start us, length us, event | category | flops | bytes accessed | tf_op | source)
XLA Modules:
  0.0 389.4 jit_solution(12232705881103919717)
XLA Ops:
  8.1 0.7 all-gather.7.cloned.1.call-update
  8.8 1.6 copy.73
  11.5 0.8 pad_maximum_fusion.1.refs_0_
  12.2 66.2 %gather.1 = (bf16[8,4,96,768]{3,2,1,0:T(8,128)(2,1)}, f32[8,4,8,128]{3,2,1,0:T(8,128)}) custom-call(bf16[96,768]{1,0:T(8,128)(2,1)} %pad_maximum_fusion.1.refs_0_, f32[8,128]{1,0:T(8,128)} %pad_bitcast_fusion.refs_1_), custom_call_target="tpu_custom_call" | custom-call | tf_op jit(solution)/shard_map/gather/pallas_call | solution.py:674
  78.4 0.9 copy.95
  81.7 0.7 reshape.99.bias_ref
  86.9 1.6 copy.78.other_ref
  88.5 39.3 %attend.1 = (f32[768,768]{1,0:T(8,128)}, bf16[4,768,256]{2,1,0:T(8,128)(2,1)}, bf16[12,768,128]{2,1,0:T(8,128)(2,1)}, bf16[12,1536,128]{2,1,0:T(8,128)(2,1)}, bf16[12,1536,128]{2,1,0:T(8,128)(2,1)}) custom-call(s32[2]{0:T(128)} %pad_add_fusion.valid_ref, bf16[768,768]{1,0:T(8,128)(2,1)} %own_ref.1, bf16[768,768]{1,0:T(8,128)(2,1)} %copy.78.other_ref, ...), custom_call_target="tpu_custom_call" | custom-call | flops 53150220288 | bytes 25165824 | tf_op jit(solution)/shard_map/attend/pallas_call | solution.py:132
  127.9 11.3 %up.1 = (f32[4,768,768]{2,1,0:T(8,128)}, bf16[4,768,768]{2,1,0:T(8,128)(2,1)}, bf16[768,768]{1,0:T(8,128)(2,1)}, bf16[768,768]{1,0:T(8,128)(2,1)}) custom-call(f32[768,768]{1,0:T(8,128)} %get-tuple-element.42.pre_ref, f32[1,768]{1,0:T(1,128)} %slice.102.gain_ref, f32[1,768]{1,0:T(1,128)} %slice.104.shift_ref, bf16[8,4,96,768]{3,2,1,0:T(8,128)(2,1)} %bitcast.81, ...), custom_call_target="tpu_custom_call" | custom-call | flops 3623878656 | bytes 25165824 | tf_op jit(solution)/shard_map/up/pallas_call | solution.py:181
  139.2 12.2 %all-gather.7.cloned.1.call-done = bf16[3072,768]{1,0:T(8,128)(2,1)} async-done(((bf16[96,768]{1,0:T(8,128)(2,1)}), bf16[3072,768]{1,0:T(8,128)(2,1)}) %all-gather.7.cloned.1.call-update) | async-done | bytes 4718608 | tf_op jit(solution)/shard_map/all_gather | solution.py:878
  151.3 36.4 %down.1 = (bf16[768,768]{1,0:T(8,128)(2,1)}, f32[768,768]{1,0:T(8,128)}, bf16[768,768]{1,0:T(8,128)(2,1)}, bf16[768,768]{1,0:T(8,128)(2,1)}, bf16[8,4,96,768]{3,...) custom-call(f32[768,768]{1,0:T(8,128)} %get-tuple-element.42.pre_ref, ...), custom_call_target="tpu_custom_call" | custom-call | flops 18119393280 | bytes 50331648 | tf_op jit(solution)/shard_map/down/pallas_call | solution.py:310
  187.8 59.7 %attend_back.1 = (bf16[8,4,96,768]{3,2,1,0:T(8,128)(2,1)}, f32[768,768]{1,0:T(8,128)}, bf16[768,768]{1,0:T(8,128)(2,1)}, f32[4,1,640]{2,1,0:T(1,128)}) custom-call(bf16[768,768]{1,0:T(8,128)(2,1)} %get-tuple-element.48.grad_ref, bf16[768,768]{1,0:T(8,128)(2,1)} %get-tuple-element.49.grad_t_ref, bf16[768,768]{1,0:T(8,128)(2,1)} %bitcast.59, ...), custom_call_target="tpu_custom_call" | custom-call | flops 108716359680 | bytes 33554432 | tf_op jit(solution)/shard_map/attend_back/pallas_call | solution.py:460
  247.5 0.7 collective-permute-start.1
  248.3 0.7 fusion.3
  250.3 48.4 %scatter.2 = (f32[96,768]{1,0:T(8,128)}, f32[8,128]{1,0:T(8,128)}) custom-call(bf16[8,4,96,768]{3,2,1,0:T(8,128)(2,1)} %get-tuple-element.56.refs_0_, f32[8,4,8,128]{3,2,1,0:T(8,128)} %bitcast.61), custom_call_target="tpu_custom_call" | custom-call | tf_op jit(solution)/shard_map/scatter/pallas_call | solution.py:864
  298.8 1.3 slice.117
  300.0 0.8 slice.112
  301.4 1.2 slice_bitcast_fusion
  302.6 0.7 copy.88
  303.4 72.7 %scatter.3 = (f32[96,768]{1,0:T(8,128)}, f32[96,768]{1,0:T(8,128)}) custom-call(bf16[8,4,96,768]{3,2,1,0:T(8,128)(2,1)} %get-tuple-element.62.refs_0_, bf16[8,4,96,768]{3,2,1,0:T(8,128)(2,1)} %get-tuple-element.63.refs_1_), custom_call_target="tpu_custom_call" | custom-call | tf_op jit(solution)/shard_map/scatter/pallas_call | solution.py:864
  376.1 0.7 pad_maximum_fusion
  377.4 3.5 convert_add_fusion
  380.9 0.7 copy.100
  381.6 0.7 copy.101
  (94 shorter events, 9.9 us)
Async XLA Ops:
  7.2 3.3 copy-start.5
  7.2 3.3 copy-start.19
  7.2 3.4 copy-start.6
  7.2 3.5 copy-start.15
  7.2 3.5 copy-start.14
  7.2 3.5 copy-start.13
  7.2 3.5 copy-start.16
  7.3 3.5 copy-start.12
  7.3 3.5 copy-start.11
  7.3 3.5 copy-start.10
  7.3 72.3 %copy-start.18 = (s32[16]{0:T(128)S(1)}, s32[16]{0:T(128)}, u32[]{:S(2)}) copy-start(s32[16]{0:T(128)} %param.31) | copy-start | bytes 196
  7.3 72.3 %copy-start.17 = (s32[16]{0:T(128)S(1)}, s32[16]{0:T(128)}, u32[]{:S(2)}) copy-start(s32[16]{0:T(128)} %param.30) | copy-start | bytes 196
  7.3 120.6 %all-gather.5.cloned.1.call-start = ((), (), s32[]{:S(2)}) async-start(), calls=%async_computation | async-start | bytes 4866048 | tf_op jit(solution)/shard_map/all_gather | solution.py:878
  8.0 143.3 %all-gather.7.cloned.1.call-start = ((), (), s32[]{:S(2)}) async-start(), calls=%async_computation.1 | async-start | bytes 4866048 | tf_op jit(solution)/shard_map/all_gather | solution.py:878
  10.4 78.2 %copy-start.1 = (bf16[768,768]{0,1:T(8,128)(2,1)}, bf16[768,768]{0,1:T(8,128)(2,1)S(1)}, u32[]{:S(2)}) copy-start(bf16[768,768]{0,1:T(8,128)(2,1)S(1)} %copy.73) | copy-start | bytes 3538948
  10.4 76.6 %collective-permute-start = (bf16[768,768]{0,1:T(8,128)(2,1)S(1)}, bf16[768,768]{0,1:T(8,128)(2,1)S(1)}, u32[]{:S(2)}, u32[]{:S(2)}) collective-permute-start(bf16[768,768]{0,1:T(8,128)(2,1)S(1)} %copy.73), channel_id=1, source_target_pairs={{0,1},{1,0},{2,3},{3,2},{4,5},{5,4},{6,7},{7,6},{8,9},{9,8},{10,11... | collective-permute-start | bytes 3538952 | tf_op jit(solution)/shard_map/ppermute | solution.py:920
  86.9 40.9 %copy-start.2 = (bf16[768,768]{0,1:T(8,128)(2,1)}, bf16[768,768]{0,1:T(8,128)(2,1)S(1)}, u32[]{:S(2)}) copy-start(bf16[768,768]{0,1:T(8,128)(2,1)S(1)} %collective-permute-done) | copy-start | bytes 3538948
  187.8 60.4 %copy-start.8 = (f32[4,1,768]{2,1,0:T(1,128)S(1)}, f32[4,1,768]{2,1,0:T(1,128)}, u32[]{:S(2)}) copy-start(f32[4,1,768]{2,1,0:T(1,128)} %get-tuple-element.59) | copy-start | bytes 36868
  187.8 61.5 %copy-start.7 = (f32[8,768]{1,0:T(8,128)S(1)}, f32[8,768]{1,0:T(8,128)}, u32[]{:S(2)}) copy-start(f32[8,768]{1,0:T(8,128)} %get-tuple-element.57) | copy-start | bytes 73732
  247.5 129.9 %collective-permute-start.1 = (bf16[768,768]{1,0:T(8,128)(2,1)}, bf16[768,768]{1,0:T(8,128)(2,1)S(1)}, u32[]{:S(2)}, u32[]{:S(2)}) collective-permute-start(bf16[768,768]{1,0:T(8,128)(2,1)} %get-tuple-element.55), channel_id=1, source_target_pairs={{0,1},{1,0},{2,3},{3,2},{4,5},{5,4},{6,7},{7,6},{8,9},{9,8},{10,11... | collective-permute-start | bytes 3538952 | tf_op jit(solution)/shard_map/ppermute | solution.py:957
  303.4 73.4 %copy-start.9 = (f32[8,128]{1,0:T(8,128)S(1)}, f32[8,128]{1,0:T(8,128)}, u32[]{:S(2)}) copy-start(f32[8,128]{1,0:T(8,128)} %get-tuple-element.61) | copy-start | bytes 12292
  303.4 74.0 %copy-start = (f32[768,768]{1,0:T(8,128)S(1)}, f32[768,768]{1,0:T(8,128)}, u32[]{:S(2)}) copy-start(f32[768,768]{1,0:T(8,128)} %get-tuple-element.47) | copy-start | bytes 7077892
  377.4 3.5 copy-start.4
  377.4 4.2 %copy-start.3 = (f32[96,768]{1,0:T(8,128)S(1)}, f32[96,768]{1,0:T(8,128)}, u32[]{:S(2)}) copy-start(f32[96,768]{1,0:T(8,128)} %get-tuple-element.65) | copy-start | bytes 884740
Sparse Core Ops, SparseCore 0:
  10.9 75.7 all-gather.4
  89.5 61.8 all-gather.6

commit v3 on v2

--- a/solution.py
+++ b/solution.py
@@ -66,7 +66,7 @@
 
 
 def attend_kernel(
-    valid_ref, own_ref, other_ref, w_ref, qv_bias_ref, out_bias_ref, pre_ref, ctx_ref, q_ref, k_ref, v_ref
+    order_ref, valid_ref, own_ref, other_ref, w_ref, qv_bias_ref, out_bias_ref, pre_ref, ctx_ref, q_ref, k_ref, v_ref
 ):
     group, groups = pl.program_id(0), pl.num_programs(0)
     rows = own_ref.shape[0]
@@ -123,31 +123,35 @@
         pre_ref[...] += part
 
 
-def attend(valid, own, other, weights, qv_bias, out_bias):
+def attend(order, valid, own, other, weights, qv_bias, out_bias):
     rows, width = own.shape
     groups = weights.shape[1]
-    whole = lambda g: (0, 0)
-    by_group = lambda g: (g, 0, 0)
+    whole = lambda g, order, valid: (0, 0)
+    by_group = lambda g, order, valid: (g, 0, 0)
     flops = groups * (2 * 2 * rows * width * 640 + 3 * 4 * rows * SLOT * 128)
     return pl.pallas_call(
         attend_kernel,
         name="attend",
-        grid=(groups,),
-        in_specs=[
-            pl.BlockSpec(memory_space=pltpu.SMEM),
-            pl.BlockSpec((rows, width), whole),
-            pl.BlockSpec((rows, width), whole),
-            pl.BlockSpec((weights.shape[0], 1) + weights.shape[2:], lambda g: (0, g, 0, 0)),
-            pl.BlockSpec((1, 1, 640), by_group),
-            pl.BlockSpec((1, width), whole),
-        ],
-        out_specs=[
-            pl.BlockSpec((rows, width), whole),
-            pl.BlockSpec((1, rows, 256), by_group),
-            pl.BlockSpec((3, rows, 128), by_group),
-            pl.BlockSpec((3, SLOT, 128), by_group),
-            pl.BlockSpec((3, SLOT, 128), by_group),
-        ],
+        grid_spec=pltpu.PrefetchScalarGridSpec(
+            num_scalar_prefetch=2,
+            grid=(groups,),
+            in_specs=[
+                pl.BlockSpec((rows, width), whole),
+                pl.BlockSpec((rows, width), whole),
+                pl.BlockSpec(
+                    (weights.shape[0], 1) + weights.shape[2:], lambda g, order, valid: (0, order[g], 0, 0)
+                ),
+                pl.BlockSpec((1, 1, 640), lambda g, order, valid: (order[g], 0, 0)),
+                pl.BlockSpec((1, width), whole),
+            ],
+            out_specs=[
+                pl.BlockSpec((rows, width), whole),
+                pl.BlockSpec((1, rows, 256), by_group),
+                pl.BlockSpec((3, rows, 128), by_group),
+                pl.BlockSpec((3, SLOT, 128), by_group),
+                pl.BlockSpec((3, SLOT, 128), by_group),
+            ],
+        ),
         out_shape=[
             jax.ShapeDtypeStruct((rows, width), F32),
             jax.ShapeDtypeStruct((groups, rows, 256), BF16),
@@ -157,7 +161,7 @@
         ],
         cost_estimate=pl.CostEstimate(flops=4 * flops, bytes_accessed=24 << 20, transcendentals=12 * rows * SLOT),
         compiler_params=pltpu.CompilerParams(vmem_limit_bytes=60 << 20),
-    )(valid, own, other, weights, qv_bias, out_bias)
+    )(order, valid, own, other, weights, qv_bias, out_bias)
 
 
 def up_kernel(pre_ref, gain_ref, shift_ref, w_ref, bias_ref, hidden_ref, active_ref, low_ref, low_t_ref):
@@ -222,8 +226,7 @@
     grad_pre_ref,
     grad_low_ref,
     grad_low_t_ref,
-    grad_w2_ref,
-    grad_w1_ref,
+    grad_ff_ref,
     sums_ref,
     up_bias_ref,
     total_ref,
@@ -270,9 +273,10 @@
         slope = cdf + hidden * jnp.exp(-0.5 * hidden * hidden) * 0.3989422804014327
         grad_hidden = (grad_active * slope).astype(BF16)
         up_bias_ref[0] = jnp.sum(grad_hidden.astype(F32), axis=0, keepdims=True)
-        shape = grad_w2_ref.shape
-        grad_w2_ref[...] = mul(upper_low_t_ref[...], active_ref[0]).astype(BF16).reshape(shape)
-        grad_w1_ref[...] = mul(low_t_ref[...], grad_hidden).astype(BF16).reshape(shape)
+        part_rows = w1_ref.shape[2]
+        shape = w1_ref.shape
+        grad_ff_ref[:, :, :part_rows] = mul(low_t_ref[...], grad_hidden).astype(BF16).reshape(shape)
+        grad_ff_ref[:, :, part_rows:] = mul(upper_low_t_ref[...], active_ref[0]).astype(BF16).reshape(shape)
         part = mul(grad_hidden, weight(w1_ref, 0, w1_ref.shape[3]), NT)
 
         @pl.when(step == groups)
@@ -326,8 +330,7 @@
             pl.BlockSpec((rows, width), whole),
             pl.BlockSpec((rows, width), whole),
             pl.BlockSpec((width, rows), whole),
-            pl.BlockSpec(block, w_late),
-            pl.BlockSpec(block, w_late),
+            pl.BlockSpec(block[:2] + (2 * block[2],) + block[3:], w_late),
             pl.BlockSpec((8, width), whole),
             pl.BlockSpec((1, 1, units), late),
         ],
@@ -336,8 +339,7 @@
             jax.ShapeDtypeStruct((rows, width), F32),
             jax.ShapeDtypeStruct((rows, width), BF16),
             jax.ShapeDtypeStruct((width, rows), BF16),
-            jax.ShapeDtypeStruct(w2.shape, BF16),
-            jax.ShapeDtypeStruct(w1.shape, BF16),
+            jax.ShapeDtypeStruct(w1.shape[:2] + (2 * w1.shape[2],) + w1.shape[3:], BF16),
             jax.ShapeDtypeStruct((8, width), F32),
             jax.ShapeDtypeStruct((groups, 1, units), F32),
         ],
@@ -354,26 +356,10 @@
     )(pre, cotangent, vectors, active, hidden, w2, w1, low_t)
 
 
-def attend_back_kernel(
-    grad_ref,
-    grad_t_ref,
-    own_t_ref,
-    other_t_ref,
-    w_ref,
-    ctx_ref,
-    q_ref,
-    k_ref,
-    v_ref,
-    grad_w_ref,
-    grad_own_ref,
-    grad_other_ref,
-    sums_ref,
-    other_total_ref,
-):
-    group, groups = pl.program_id(0), pl.num_programs(0)
+def group_back(grad_ref, grad_t_ref, own_t_ref, other_t_ref, weight_of, ctx_ref, q_ref, k_ref, v_ref, after_head):
     rows = grad_ref.shape[0]
     step = 256
-    grad_context = mul(grad_ref[...], weight(w_ref, 512, 768)).astype(BF16).astype(F32)
+    grad_context = mul(grad_ref[...], weight_of(512, 768)).astype(BF16).astype(F32)
     lane = lanes((rows, 128))
     grads = []
     for head in range(3):
@@ -401,6 +387,7 @@
             grad_query.append(mul(keys_t, grad_scores))
         grad_query = jnp.concatenate(grad_query, axis=1).T * SCALE
         grads.append((grad_query, grad_keys, grad_values))
+        after_head(head)
     (q0, k0, v0), (q1, k1, v1), (q2, k2, v2) = grads
     blank = jnp.zeros((rows, 128), F32)
     own = jnp.concatenate(
@@ -419,19 +406,59 @@
     )
     own_sum = jnp.sum(own, axis=0, keepdims=True)
     other_sum = jnp.sum(other, axis=0, keepdims=True)
-    sums_ref[0, :, 0:128] = own_sum[:, 0:128]
-    sums_ref[0, :, 128:640] = own_sum[:, 128:] + other_sum
+    sums = [own_sum[:, 0:128]] + [
+        own_sum[:, i : i + 128] + other_sum[:, i - 128 : i] for i in range(128, 640, 128)
+    ]
     own, other = own.astype(BF16), other.astype(BF16)
     grad_w = mul(own_t_ref[...], own)
     grad_w_other = mul(other_t_ref[...], other)
     grad_out = mul(grad_t_ref[...], ctx_ref[0])
+    columns = [
+        grad_w[:, 0:128],
+        grad_w[:, 128:512] + grad_w_other[:, 0:384],
+        grad_w[:, 512:640] + grad_w_other[:, 384:512] + grad_out[:, 0:128],
+        grad_out[:, 128:256],
+    ]
+    return own, other, sums, columns
+
+
+def attend_back_kernel(
+    grad_ref,
+    grad_t_ref,
+    own_t_ref,
+    other_t_ref,
+    w_ref,
+    ctx_ref,
+    q_ref,
+    k_ref,
+    v_ref,
+    grad_w_ref,
+    grad_own_ref,
+    grad_other_ref,
+    sums_ref,
+    other_total_ref,
+):
+    group, groups = pl.program_id(0), pl.num_programs(0)
+    own, other, sums, columns = group_back(
+        grad_ref,
+        grad_t_ref,
+        own_t_ref,
+        other_t_ref,
+        functools.partial(weight, w_ref),
+        ctx_ref,
+        q_ref,
+        k_ref,
+        v_ref,
+        lambda head: None,
+    )
+    for number, piece in enumerate(sums):
+        sums_ref[0, :, 128 * number : 128 * number + 128] = piece
     shape = (grad_w_ref.shape[0], 1, grad_w_ref.shape[2])
-    grad_w_ref[:, :, :, 0:128] = grad_w[:, 0:128].astype(BF16).reshape(shape + (128,))
-    grad_w_ref[:, :, :, 128:512] = (grad_w[:, 128:512] + grad_w_other[:, 0:384]).astype(BF16).reshape(shape + (384,))
-    grad_w_ref[:, :, :, 512:640] = (
-        (grad_w[:, 512:640] + grad_w_other[:, 384:512] + grad_out[:, 0:128]).astype(BF16).reshape(shape + (128,))
-    )
-    grad_w_ref[:, :, :, 640:768] = grad_out[:, 128:256].astype(BF16).reshape(shape + (128,))
+    first = 0
+    for piece in columns:
+        last = first + piece.shape[1]
+        grad_w_ref[:, :, :, first:last] = piece.astype(BF16).reshape(shape + (last - first,))
+        first = last
     own_part = mul(own, weight(w_ref, 0, 640), NT)
     other_part = mul(other, weight(w_ref, 128, 640), NT)
 
@@ -686,192 +713,369 @@
 SCATTER_KINDS = S0 + 4
 
 
-def scatter_kernel(count, depth, *refs):
-    partials, outs = refs[:count], refs[count : 2 * count]
-    scratch = refs[2 * count : -2]
-    send_sem, recv_sem = refs[-2:]
-    me, z = lax.axis_index("dp"), lax.axis_index("mp")
-
-    def copy(which, kind, place, source, target, to):
+class Reduction:
+    def __init__(self, which, me, z, depth, rows, bufs, send_sem, recv_sem):
+        self.which, self.me, self.z, self.depth, self.rows = which, me, z, depth, rows
+        self.half = halves(rows)[0]
+        self.core, self.diagonal, self.sides, self.line = bufs
+        self.send_sem, self.recv_sem = send_sem, recv_sem
+
+    def copy(self, kind, place, source, target, to):
         return pltpu.make_async_remote_copy(
             src_ref=source,
             dst_ref=target,
-            send_sem=send_sem.at[which, kind, place],
-            recv_sem=recv_sem.at[which, kind, place],
+            send_sem=self.send_sem.at[self.which, kind, place],
+            recv_sem=self.recv_sem.at[self.which, kind, place],
             device_id=to,
             device_id_type=MESH,
         )
 
-    def bufs(which):
-        return scratch[4 * which : 4 * which + 4]
-
-    def add(target, *others):
+    def start(self, kind, place, source, target, bit):
+        self.copy(kind, place, source, target, (self.me ^ bit, self.z)).start()
+
+    def wait(self, kind, place, view):
+        self.copy(kind, place, view, view, (self.me, self.z)).wait_recv()
+
+    def add(self, target, *others):
         total = target[...].astype(F32)
         for other in others:
             total = total + other[...].astype(F32)
         target[...] = total.astype(target.dtype)
 
-    meet(me, z, depth)
-    started = []
-
-    def start(which, kind, place, source, target, to):
-        copy(which, kind, place, source, target, to).start()
-        started.append((which, kind, place, source, target))
-
-    def wait(which, kind, place, view):
-        copy(which, kind, place, view, view, (me, z)).wait_recv()
-
-    places = [depth - 1, 0] + list(range(1, depth - 1))[::-1]
-    order = [(which, place) for which in range(count) for place in places]
-    for which, place in order:
-        core = bufs(which)[0]
+    def to_core(self, place, theirs):
         for number in (3, 1, 2, 0):
-            start(
-                which,
-                S0 + number,
-                place,
-                partials[which].at[me ^ CORE ^ COLUMNS[number], place],
-                core.at[number, place],
-                (me ^ CORE, z),
-            )
-
-    def first_stage(which, place):
-        core, diagonal, sides, _ = bufs(which)
-        rows = core.shape[2]
-        half, _ = halves(rows)
-        to_x, to_y = (me ^ ALONG_X, z), (me ^ ALONG_Y, z)
+            self.start(S0 + number, place, theirs(number), self.core.at[number, place], CORE)
+
+    def first(self, place, mine):
+        half, rows = self.half, self.rows
         for number in (3, 1, 2, 0):
-            view = core.at[number, place]
-            wait(which, S0 + number, place, view)
-            add(view, partials[which].at[me ^ COLUMNS[number], place])
+            view = self.core.at[number, place]
+            self.wait(S0 + number, place, view)
+            self.add(view, mine(number))
             if number == 3:
-                start(which, TO_X, place, view.at[0:half], diagonal.at[place, 0:half], to_x)
+                self.start(TO_X, place, view.at[0:half], self.diagonal.at[place, 0:half], ALONG_X)
                 if half < rows:
-                    start(which, TO_Y, place, view.at[half:rows], diagonal.at[place, half:rows], to_y)
+                    self.start(TO_Y, place, view.at[half:rows], self.diagonal.at[place, half:rows], ALONG_Y)
             if number == 1:
-                if half < rows:
-                    start(which, X_LOW, place, view.at[0:half], sides.at[0, place, 0:half], to_x)
-                else:
-                    start(which, X_LOW, place, view, sides.at[0, place], to_x)
+                self.start(X_LOW, place, view.at[0:half], self.sides.at[0, place, 0:half], ALONG_X)
             if number == 2 and half < rows:
-                start(which, Y_HIGH, place, view.at[half:rows], sides.at[1, place, half:rows], to_y)
-
-    def second_stage(which, place):
-        core, diagonal, sides, _ = bufs(which)
-        rows = core.shape[2]
-        half, _ = halves(rows)
-        view = diagonal.at[place, 0:half]
-        wait(which, TO_X, place, view)
-        mine = core.at[2, place, 0:half]
-        add(mine, view)
-        start(which, Y_LOW, place, mine, sides.at[1, place, 0:half], (me ^ ALONG_Y, z))
+                self.start(Y_HIGH, place, view.at[half:rows], self.sides.at[1, place, half:rows], ALONG_Y)
+
+    def second(self, place):
+        half, rows = self.half, self.rows
+        view = self.diagonal.at[place, 0:half]
+        self.wait(TO_X, place, view)
+        mine = self.core.at[2, place, 0:half]
+        self.add(mine, view)
+        self.start(Y_LOW, place, mine, self.sides.at[1, place, 0:half], ALONG_Y)
         if half < rows:
-            view = diagonal.at[place, half:rows]
-            wait(which, TO_Y, place, view)
-            mine = core.at[1, place, half:rows]
-            add(mine, view)
-            start(which, X_HIGH, place, mine, sides.at[0, place, half:rows], (me ^ ALONG_X, z))
-
-    def third_stage(which, place):
-        core, _, sides, _ = bufs(which)
-        rows = core.shape[2]
-        half, _ = halves(rows)
-        wait(which, X_LOW, place, sides.at[0, place, 0:half])
-        wait(which, Y_LOW, place, sides.at[1, place, 0:half])
+            view = self.diagonal.at[place, half:rows]
+            self.wait(TO_Y, place, view)
+            mine = self.core.at[1, place, half:rows]
+            self.add(mine, view)
+            self.start(X_HIGH, place, mine, self.sides.at[0, place, half:rows], ALONG_X)
+
+    def third(self, place):
+        half, rows = self.half, self.rows
+        self.wait(X_LOW, place, self.sides.at[0, place, 0:half])
+        self.wait(Y_LOW, place, self.sides.at[1, place, 0:half])
         if half < rows:
-            wait(which, Y_HIGH, place, sides.at[1, place, half:rows])
-            wait(which, X_HIGH, place, sides.at[0, place, half:rows])
-        add(core.at[0, place], sides.at[0, place], sides.at[1, place])
-
-    for step in range(len(order) + 4):
-        if step < len(order):
-            first_stage(*order[step])
-        if 0 <= step - 2 < len(order):
-            second_stage(*order[step - 2])
-        if 0 <= step - 4:
-            third_stage(*order[step - 4])
-
-    for which in range(count):
-        core, _, _, line = bufs(which)
-
-        def send(kind, place, to, which=which, core=core, line=line):
-            way = 0 if kind == Z_UP else 1
-            copy(which, kind, place, core.at[0, place], line.at[way, place], (me, to)).start()
-
-        for distance in range(depth - 1, 0, -1):
-            above, below = z + distance, z - distance
-
-            @pl.when(above < depth)
-            def _(above=above):
-                @pl.when(z > 0)
-                def _():
-                    wait(which, Z_UP, above, line.at[0, above])
-                    add(core.at[0, above], line.at[0, above])
-
-                send(Z_UP, above, z + 1)
-
-            @pl.when(below >= 0)
-            def _(below=below):
-                @pl.when(z < depth - 1)
-                def _():
-                    wait(which, Z_DOWN, below, line.at[1, below])
-                    add(core.at[0, below], line.at[1, below])
-
-                send(Z_DOWN, below, z - 1)
-
-    for which in range(count):
-        core, _, _, line = bufs(which)
-        outs[which][...] = core[0, z].astype(F32)
+            self.wait(Y_HIGH, place, self.sides.at[1, place, half:rows])
+            self.wait(X_HIGH, place, self.sides.at[0, place, half:rows])
+        self.add(self.core.at[0, place], self.sides.at[0, place], self.sides.at[1, place])
+
+    def along(self, kind, place):
+        way = 0 if kind == Z_UP else 1
+        to = (self.me, self.z + 1 if kind == Z_UP else self.z - 1)
+        return self.copy(kind, place, self.core.at[0, place], self.line.at[way, place], to)
+
+    def chain(self, distance):
+        z, depth = self.z, self.depth
+        above, below = z + distance, z - distance
+
+        @pl.when(above < depth)
+        def _():
+            @pl.when(z > 0)
+            def _():
+                self.wait(Z_UP, above, self.line.at[0, above])
+                self.add(self.core.at[0, above], self.line.at[0, above])
+
+            self.along(Z_UP, above).start()
+
+        @pl.when(below >= 0)
+        def _():
+            @pl.when(z < depth - 1)
+            def _():
+                self.wait(Z_DOWN, below, self.line.at[1, below])
+                self.add(self.core.at[0, below], self.line.at[1, below])
+
+            self.along(Z_DOWN, below).start()
+
+    def finish(self, out):
+        z, depth = self.z, self.depth
+        out[...] = self.core[0, z].astype(F32)
 
         @pl.when(z > 0)
         def _():
-            wait(which, Z_UP, z, line.at[0, z])
-            outs[which][...] += line[0, z].astype(F32)
+            self.wait(Z_UP, z, self.line.at[0, z])
+            out[...] += self.line[0, z].astype(F32)
 
         @pl.when(z < depth - 1)
         def _():
-            wait(which, Z_DOWN, z, line.at[1, z])
-            outs[which][...] += line[1, z].astype(F32)
-
+            self.wait(Z_DOWN, z, self.line.at[1, z])
+            out[...] += self.line[1, z].astype(F32)
+
+    def drain(self):
+        half, rows = self.half, self.rows
+        pieces = [(S0 + number, 0, rows) for number in range(4)]
+        pieces += [(TO_X, 0, half), (X_LOW, 0, half), (Y_LOW, 0, half)]
+        if half < rows:
+            pieces += [(TO_Y, half, rows), (Y_HIGH, half, rows), (X_HIGH, half, rows)]
+        for place in range(self.depth):
+            for kind, first, last in pieces:
+                view = self.core.at[0, place, first:last]
+                self.copy(kind, place, view, view, (self.me, self.z)).wait_send()
+        for distance in range(1, self.depth):
+            above, below = self.z + distance, self.z - distance
+            pl.when(above < self.depth)(lambda above=above: self.along(Z_UP, above).wait_send())
+            pl.when(below >= 0)(lambda below=below: self.along(Z_DOWN, below).wait_send())
+
+
+def linked_back_kernel(
+    depth,
+    grad_ref,
+    grad_t_ref,
+    own_t_ref,
+    other_t_ref,
+    early_ref,
+    w_hbm,
+    ff_hbm,
+    ctx_ref,
+    q_ref,
+    k_ref,
+    v_ref,
+    ff_out,
+    w_out,
+    small_out,
+    grad_own_ref,
+    w_buf,
+    w_sem,
+    grad_w,
+    grad_small,
+    ff_mine,
+    ff_sem,
+    sent,
+    received,
+    pair_send,
+    pair_recv,
+    *refs,
+):
+    send_sem, recv_sem = refs[-2:]
+    me, z = lax.axis_index("dp"), lax.axis_index("mp")
+    step = pl.program_id(0)
+    rows = grad_ref.shape[0]
+    part = w_buf.shape[2]
+    group_at = lambda s: z ^ (depth - 1 - s)
+    group = group_at(step)
+    arrays = [(2 * part, refs[0:4]), (part, refs[4:8]), (8, refs[8:12])]
+    ff, w, small = [
+        Reduction(i, me, z, depth, size, bufs, send_sem, recv_sem) for i, (size, bufs) in enumerate(arrays)
+    ]
+    places = [depth - 1, 0] + list(range(1, depth - 1))[::-1]
+
+    def load_w(s):
+        return pltpu.make_async_copy(w_hbm.at[:, group_at(s)], w_buf.at[group_at(s)], w_sem.at[s])
+
+    def load_ff(turn, number):
+        source = ff_hbm.at[me ^ COLUMNS[number], places[turn]]
+        return pltpu.make_async_copy(source, ff_mine.at[turn % 2, number], ff_sem.at[turn % 2, number])
+
+    def exchange(place):
+        return pltpu.make_async_remote_copy(
+            src_ref=sent.at[place],
+            dst_ref=received.at[place],
+            send_sem=pair_send.at[place],
+            recv_sem=pair_recv.at[place],
+            device_id=(me, z ^ 1),
+            device_id_type=MESH,
+        )
+
+    @pl.when(step == 0)
+    def _():
+        for s in range(depth):
+            load_w(s).start()
+        for turn in range(2):
+            for number in range(4):
+                load_ff(turn, number).start()
+        meet(me, z, depth)
+        for place in places:
+            ff.to_core(place, lambda number, place=place: ff_hbm.at[me ^ CORE ^ COLUMNS[number], place])
+
+    for s in range(depth):
+        pl.when(step == s)(lambda s=s: load_w(s).wait())
+
+    def ff_first(turn):
+        for number in range(4):
+            load_ff(turn, number).wait()
+        ff.first(places[turn], lambda number: ff_mine.at[turn % 2, number])
+        if turn + 2 < depth:
+            for number in range(4):
+                load_ff(turn + 2, number).start()
+
+    def ff_work(slot):
+        if slot < depth:
+            ff_first(slot)
+        if 0 <= slot - 2 < depth:
+            ff.second(places[slot - 2])
+        if 0 <= slot - 6 < depth:
+            ff.third(places[slot - 6])
+        last = 6 + depth - 1
+        if last <= slot < last + depth - 1:
+            ff.chain(depth - 1 - (slot - last))
+
+    def w_first(s):
+        place = group_at(s)
+        w.first(place, lambda number: grad_w.at[s, me ^ COLUMNS[number]])
+        small.first(place, lambda number: grad_small.at[s, me ^ COLUMNS[number]])
+
+    def w_second(s):
+        w.second(group_at(s))
+        small.second(group_at(s))
+
+    def w_third(s):
+        w.third(group_at(s))
+        small.third(group_at(s))
+
+    def take(place):
+        exchange(place).wait_recv()
+        block = received[place]
+        low = lanes((rows, 128)) < HEAD
+        zero = jnp.zeros((rows, 128), BF16)
+        ends = block[:, 0:128]
+        other = jnp.concatenate([jnp.where(low, zero, ends), block[:, 128:384], jnp.where(low, ends, zero)], axis=1)
+        view = w_buf.at[place]
+        grad_own_ref[...] += mul(other, view[:, :, 128:640].reshape(part * 8, 512), NT)
+
+    def after_head(head):
+        for s in range(depth):
+            slot = 3 * s + head
+            pl.when(step == s)(lambda slot=slot: ff_work(slot))
+
+        @pl.when(step > 0)
+        def _():
+            [w_first, w_second, w_third][head](step - 1)
+
+    own, other, sums, columns = group_back(
+        grad_ref,
+        grad_t_ref,
+        own_t_ref,
+        other_t_ref,
+        lambda first, last: w_buf[group, :, :, first:last].reshape(part * 8, last - first),
+        ctx_ref,
+        q_ref,
+        k_ref,
+        v_ref,
+        after_head,
+    )
+    sent[group, :, 0:128] = other[:, 0:128] + other[:, 384:512]
+    sent[group, :, 128:384] = other[:, 128:384]
+    exchange(group).start()
+    first = 0
+    for piece in columns:
+        last = first + piece.shape[1]
+        grad_w[step, :, :, first:last] = piece.astype(BF16).reshape(8, part, last - first)
+        first = last
+    row = lax.broadcasted_iota(jnp.int32, (8, 128), 0)
+    late = jnp.zeros((8, 128), F32)
+    for number, piece in enumerate(sums):
+        late = jnp.where(row == number, piece, late)
+    for owner in range(8):
+        grad_small[step, owner] = early_ref[owner, group] + late
+    w.to_core(group, lambda number: grad_w.at[step, me ^ CORE ^ COLUMNS[number]])
+    small.to_core(group, lambda number: grad_small.at[step, me ^ CORE ^ COLUMNS[number]])
+    own_part = mul(own, w_buf[group, :, :, 0:640].reshape(part * 8, 640), NT)
+
+    @pl.when(step == 0)
+    def _():
+        grad_own_ref[...] = own_part
+
+    @pl.when(step > 0)
+    def _():
+        grad_own_ref[...] += own_part
+        take(group_at(step - 1) ^ 1)
+
+    @pl.when(step == depth - 1)
+    def _():
+        w_first(depth - 1)
         for distance in range(depth - 1, 0, -1):
-            above, below = z + distance, z - distance
-
-            @pl.when(above < depth)
-            def _(above=above):
-                copy(which, Z_UP, above, core.at[0, above], line.at[0, above], (me, z)).wait_send()
-
-            @pl.when(below >= 0)
-            def _(below=below):
-                copy(which, Z_DOWN, below, core.at[0, below], line.at[1, below], (me, z)).wait_send()
-
-    for which, kind, place, source, target in started:
-        copy(which, kind, place, source, target, (me, z)).wait_send()
-
-
-def scatter_all(partials, number):
-    count = len(partials)
-    n_mp = partials[0].shape[1]
-    sems = pltpu.SemaphoreType.DMA((count, SCATTER_KINDS, n_mp))
+            w.chain(distance)
+            small.chain(distance)
+            if distance == depth - 1:
+                w_second(depth - 1)
+        ff.finish(ff_out)
+        w_third(depth - 1)
+        w.finish(w_out)
+        small.finish(small_out)
+        take(group ^ 1)
+        for array in (ff, w, small):
+            array.drain()
+        for place in range(depth):
+            exchange(place).wait_send()
+
+
+def linked_back(grad, grad_t, own_t, other_t, early, weights, grad_ff, ctx, query, keys, values):
+    rows, width = grad.shape
+    n_dp, groups, part = weights.shape[:3]
+    whole = pl.BlockSpec(memory_space=pltpu.VMEM)
+    anywhere = pl.BlockSpec(memory_space=pl.ANY)
+    by_group = lambda g: (groups - 1 - g, 0, 0)
+    flops = groups * (3 * 2 * rows * width * 640 + 3 * 10 * rows * SLOT * 128)
     scratch = []
-    for a in partials:
-        block = a.shape[2:]
-        scratch += [
-            pltpu.VMEM((4, n_mp) + block, a.dtype),
-            pltpu.VMEM((n_mp,) + block, a.dtype),
-            pltpu.VMEM((2, n_mp) + block, a.dtype),
-            pltpu.VMEM((2, n_mp) + block, a.dtype),
+    for size, columns, kind in ((2 * part, width, BF16), (part, width, BF16), (8, 128, F32)):
+        block = (size, columns)
+        scratch += [pltpu.VMEM((lead, groups) + block, kind) for lead in (4,)]
+        scratch += [pltpu.VMEM((groups,) + block, kind)]
+        scratch += [pltpu.VMEM((2, groups) + block, kind)] * 2
+    sems = pltpu.SemaphoreType.DMA((3, SCATTER_KINDS, groups))
+    pairs = pltpu.SemaphoreType.DMA((groups,))
+    return pl.pallas_call(
+        functools.partial(linked_back_kernel, groups),
+        name="linked_back",
+        grid=(groups,),
+        in_specs=[whole] * 5
+        + [anywhere] * 2
+        + [
+            pl.BlockSpec((1, rows, 256), by_group),
+            pl.BlockSpec((3, rows, 128), by_group),
+            pl.BlockSpec((3, SLOT, 128), by_group),
+            pl.BlockSpec((3, SLOT, 128), by_group),
+        ],
+        out_specs=[whole] * 4,
+        out_shape=[
+            jax.ShapeDtypeStruct((2 * part, width), F32),
+            jax.ShapeDtypeStruct((part, width), F32),
+            jax.ShapeDtypeStruct((8, 128), F32),
+            jax.ShapeDtypeStruct((rows, width), F32),
+        ],
+        scratch_shapes=[
+            pltpu.VMEM((groups, n_dp, part, width), BF16),
+            pltpu.SemaphoreType.DMA((groups,)),
+            pltpu.VMEM((groups, n_dp, part, width), BF16),
+            pltpu.VMEM((groups, n_dp, 8, 128), F32),
+            pltpu.VMEM((2, 4, 2 * part, width), BF16),
+            pltpu.SemaphoreType.DMA((2, 4)),
+            pltpu.VMEM((groups, rows, 384), BF16),
+            pltpu.VMEM((groups, rows, 384), BF16),
+            pairs,
+            pairs,
         ]
-    return pl.pallas_call(
-        functools.partial(scatter_kernel, count, n_mp),
-        name="scatter",
-        in_specs=[pl.BlockSpec(memory_space=pltpu.VMEM)] * count,
-        out_specs=[pl.BlockSpec(memory_space=pltpu.VMEM)] * count,
-        out_shape=[jax.ShapeDtypeStruct(a.shape[2:], F32) for a in partials],
-        scratch_shapes=scratch + [sems, sems],
+        + scratch
+        + [sems, sems],
+        cost_estimate=pl.CostEstimate(flops=4 * flops, bytes_accessed=48 << 20, transcendentals=12 * rows * SLOT),
         compiler_params=pltpu.CompilerParams(
-            collective_id=number, has_side_effects=True, vmem_limit_bytes=60 << 20
+            collective_id=2, has_side_effects=True, vmem_limit_bytes=67043328
         ),
-    )(*partials)
+    )(grad, grad_t, own_t, other_t, early, weights, grad_ff, ctx, query, keys, values)
 
 
 def blocks(local, mesh_shape):
@@ -884,14 +1088,9 @@
     return [blocks(local, mesh_shape) for local in locals_]
 
 
-def scatter_sums(partials, number):
-    if partials[0].shape[0] == 8:
-        return scatter_all(partials, number)
-    done = []
-    for partial in partials:
-        flat = partial.reshape((-1,) + partial.shape[3:])
-        done.append(lax.psum_scatter(flat, BOTH, scatter_dimension=0, tiled=True).astype(F32))
-    return done
+def scatter_sums(partial):
+    flat = partial.reshape((-1,) + partial.shape[3:])
+    return lax.psum_scatter(flat, BOTH, scatter_dimension=0, tiled=True).astype(F32)
 
 
 def body(
@@ -945,34 +1144,47 @@
     length = jnp.sum(jnp.where(clip_slot == slot, clip_lengths, 0))
     valid = jnp.stack([length - half * rows, length - (1 - half) * rows]).astype(jnp.int32)
 
-    pre_one, ctx, query, keys, values = attend(valid, frames, other, w_attn, qv_bias, vectors[0:1])
+    linked = n_dp == 8
+    places = jnp.arange(n_mp, dtype=jnp.int32)
+    order = (lax.axis_index("mp") ^ places) if linked else places
+    pre_one, ctx, query, keys, values = attend(order, valid, frames, other, w_attn, qv_bias, vectors[0:1])
     hidden, active, low, low_t = up(pre_one, vectors[1:2], vectors[2:3], w1, up_bias)
-    output, grad_pre, grad_low, grad_low_t, grad_w2, grad_w1, sums, grad_up_bias = down(
+    output, grad_pre, grad_low, grad_low_t, grad_ff, sums, grad_up_bias = down(
         pre_one, cotangent, vectors, active, hidden, w2, w1, low_t
     )
-    done_w2, done_w1 = scatter_sums([grad_w2, grad_w1], 2)
-    grad_w, grad_own, grad_other, head_sums = attend_back(
-        grad_low, grad_low_t, frames.T, other.T, w_attn, ctx, query, keys, values
-    )
-    returned = lax.ppermute(grad_other, "mp", partner)
-    grad_input = grad_pre + grad_own + returned.astype(F32)
-
     sums = sums[:6].reshape(6, n_dp * n_mp, share).transpose(1, 0, 2).reshape(n_dp * n_mp, 6 * share)
-    head_sums = jnp.concatenate(
-        [head_sums[:, :, :heads_width], head_sums[:, :, 2 * heads_width : 3 * heads_width]], axis=1
-    )
-    head_sums = head_sums.reshape(n_mp, 2, n_dp, share).transpose(2, 0, 1, 3).reshape(n_dp * n_mp, 2 * share)
     unit_sums = grad_up_bias.reshape(n_mp, n_dp, -1).transpose(1, 0, 2).reshape(n_dp * n_mp, -1)
-    small = jnp.concatenate([sums, head_sums, unit_sums], axis=1)
-    small = jnp.pad(small, ((0, 0), (0, -entries % 1024))).reshape(mesh_shape + (-1, 128))
-    done_w, small = scatter_sums([grad_w, small], 3)
+    early = jnp.concatenate([sums, unit_sums], axis=1)
+    entries = early.shape[1]
+    early = jnp.pad(early, ((0, 0), (0, -entries % 128))).reshape(mesh_shape + (-1, 128))
+    early = jnp.pad(early, ((0, 0), (0, 0), (5, 3 - early.shape[2]), (0, 0)))
+    kept = (ctx, query, keys, values)
+    if linked:
+        done_ff, done_w, small, grad_own = linked_back(
+            grad_low, grad_low_t, frames.T, other.T, early, w_attn, grad_ff, *kept
+        )
+        grad_input = grad_pre + grad_own
+    else:
+        grad_w, grad_own, grad_other, head_sums = attend_back(
+            grad_low, grad_low_t, frames.T, other.T, w_attn, *kept
+        )
+        grad_input = grad_pre + grad_own + lax.ppermute(grad_other, "mp", partner).astype(F32)
+        done_ff, done_w = scatter_sums(grad_ff), scatter_sums(grad_w)
+        small = scatter_sums(early + jnp.pad(head_sums.reshape(1, n_mp, 5, 128), ((0, 0), (0, 0), (0, 3), (0, 0))))
+    part = w_ff1.shape[0]
     small = small.reshape(-1)
     (d_out_bias, d_gain1, d_shift1, d_down_bias, d_gain2, d_shift2) = [
-        small[i * share : (i + 1) * share] for i in range(6)
+        small[640 + i * share : 640 + (i + 1) * share] for i in range(6)
     ]
-    d_qv = small[6 * share : 8 * share].reshape(2, share)
-    d_up_bias = small[8 * share : entries]
+    d_up_bias = small[640 + 6 * share : 640 + entries]
+    d_qv = jnp.stack(
+        [
+            lax.dynamic_slice(small, (first + lax.axis_index("dp") * share,), (share,))
+            for first in (0, 2 * heads_width)
+        ]
+    )
     d_qkv = jnp.stack([done_w[:, i * heads_width : (i + 1) * heads_width] for i in range(3)])
+    done_w1, done_w2 = done_ff[:part], done_ff[part:]
     return (
         output,
         grad_input,

time: 394 us -> 350 us (0.89)
  Pallas kernels: 334 us -> 288 us
    pallas_call x4 -> x2, Pallas kernels: 220 us -> 174 us  [the longest x1 134 us: linked_back(): pl.pallas_call(functools.partial(linked_back_kernel, groups), name='linke...]
  transfers between devices with their start and end apart: 4 -> 3, of which waited for: 1 -> 1; matrix products, arithmetic and copies ran while one was open for 5% -> 4% of each run, Pallas kernels for 61% -> 34%
where the time goes in v3:
time: 350 us; the launch traced here: 344 us
  Pallas kernels  288 us (82%)
  local copies, waits for them, and re-layouts  17.9 us (5%)
  between operations  15.8 us (5%)
  waiting for transfers between devices  12.5 us (4%)
  other arithmetic  9.33 us (3%)
    pallas_call x1, Pallas kernels, linked_back(): pl.pallas_call(functools.partial(linked_back_kernel, groups), name='linke...  134 us
    pallas_call x1, Pallas kernels, gather_all(): pl.pallas_call(functools.partial(gather_kernel, count, n_mp), name='gathe...  66.2 us
    pallas_call x1, Pallas kernels, attend(): pl.pallas_call(attend_kernel, name='attend', grid_spec=pltpu.PrefetchScal...  40 us
    pallas_call x1, Pallas kernels, down(): pl.pallas_call(functools.partial(down_kernel, groups), name='down', grid=...  36.6 us
    pallas_call x1, Pallas kernels, up(): pl.pallas_call(up_kernel, name='up', grid=(groups,), in_specs=[pl.BlockSp...  11.2 us
    all_gather x2, waiting for transfers between devices, blocks(): lax.all_gather(local, BOTH, axis=0, tiled=False)  11.1 us
  transfers between devices with their start and end apart: 3, of which 1 were waited for; matrix products, arithmetic and copies ran while one was open for 4% of the time, Pallas kernels for 34%

profile of v3, /device:TPU:8, one launch (start us, length us, event | category | flops | bytes accessed | tf_op | source)
XLA Modules:
  0.0 344.0 jit_solution(15700495487574830683)
XLA Ops:
  7.4 0.7 all-gather.5.cloned.1.call-update
  8.1 0.7 all-gather.7.cloned.1.call-update
  8.8 1.6 copy.69
  11.5 0.8 pad_maximum_fusion.1.refs_0_
  12.2 66.2 %gather.1 = (bf16[8,4,96,768]{3,2,1,0:T(8,128)(2,1)}, f32[8,4,8,128]{3,2,1,0:T(8,128)}) custom-call(bf16[96,768]{1,0:T(8,128)(2,1)} %pad_maximum_fusion.1.refs_0_, f32[8,128]{1,0:T(8,128)} %pad_bitcast_fusion.refs_1_), custom_call_target="tpu_custom_call" | custom-call | tf_op jit(solution)/shard_map/gather/pallas_call | solution.py:701
  78.4 0.9 copy.88
  82.9 0.7 slice.101.shift_ref
  84.3 0.7 reshape.90.bias_ref
  87.5 1.6 copy.74.other_ref
  89.1 40.0 %attend.1 = (f32[768,768]{1,0:T(8,128)}, bf16[4,768,256]{2,1,0:T(8,128)(2,1)}, bf16[12,768,128]{2,1,0:T(8,128)(2,1)}, bf16[12,1536,128]{2,1,0:T(8,128)(2,1)}, bf16[12,1536,128]{2,1,0:T(8,128)(2,1)}) custom-call(s32[4]{0:T(128)} %iota_xor_fusion.order_ref, s32[2]{0:T(128)} %pad_add_fusion.valid_ref, bf16[768,768]{1,0:T(8,128)(2,1)} %own_ref.1, ...), custom_call_target="tpu_custom_call" | custom-call | flops 53150220288 | bytes 25165824 | tf_op jit(solution)/shard_map/attend/pallas_call | solution.py:132
  129.1 11.2 %up.1 = (f32[4,768,768]{2,1,0:T(8,128)}, bf16[4,768,768]{2,1,0:T(8,128)(2,1)}, bf16[768,768]{1,0:T(8,128)(2,1)}, bf16[768,768]{1,0:T(8,128)(2,1)}) custom-call(f32[768,768]{1,0:T(8,128)} %get-tuple-element.37.pre_ref, f32[1,768]{1,0:T(1,128)} %slice.99.gain_ref, f32[1,768]{1,0:T(1,128)} %slice.101.shift_ref, bf16[8,4,96,768]{3,2,1,0:T(8,128)(2,1)} %bitcast.75, ...), custom_call_target="tpu_custom_call" | custom-call | flops 3623878656 | bytes 25165824 | tf_op jit(solution)/shard_map/up/pallas_call | solution.py:185
  140.3 11.1 %all-gather.7.cloned.1.call-done = bf16[3072,768]{1,0:T(8,128)(2,1)} async-done(((bf16[96,768]{1,0:T(8,128)(2,1)}), bf16[3072,768]{1,0:T(8,128)(2,1)}) %all-gather.7.cloned.1.call-update) | async-done | bytes 4718608 | tf_op jit(solution)/shard_map/all_gather | solution.py:1082
  151.4 36.6 %down.1 = (bf16[768,768]{1,0:T(8,128)(2,1)}, f32[768,768]{1,0:T(8,128)}, bf16[768,768]{1,0:T(8,128)(2,1)}, bf16[768,768]{1,0:T(8,128)(2,1)}, bf16[8,4,192,768]{3...) custom-call(f32[768,768]{1,0:T(8,128)} %get-tuple-element.37.pre_ref, bf16[768,768]{1,0:T(8,128)(2,1)} %cot_ref.1, ...), custom_call_target="tpu_custom_call" | custom-call | flops 18119393280 | bytes 50331648 | tf_op jit(solution)/shard_map/down/pallas_call | solution.py:314
  188.0 0.8 reshape.92
  189.0 0.8 reduce
  189.9 0.7 pad.15.early_ref
  190.6 134.3 %linked_back.1 = (f32[192,768]{1,0:T(8,128)}, f32[96,768]{1,0:T(8,128)}, f32[8,128]{1,0:T(8,128)}, f32[768,768]{1,0:T(8,128)}) custom-call(bf16[768,768]{1,0:T(8,128)(2,1)} %get-tuple-element.43.grad_ref, bf16[768,768]{1,0:T(8,128)(2,1)} %get-tuple-element.44.grad_t_ref, bf16[768,768]{1,0:T(8,128)(2,1)} %bitcast.57, bf16[768,768]{1,0:T(8,128)(2,1)} %bitcast.58, ...), custom_call_target="tpu_custom_call" | custom-call | flops 108716359680 | bytes 50331648 | tf_op jit(solution)/shard_map/linked_back/pallas_call | solution.py:1041
  324.9 1.2 slice_bitcast_fusion.1
  326.1 1.9 slice_bitcast_fusion
  328.0 0.7 copy.83
  328.8 1.3 slice.112
  330.0 1.6 fusion.2
  332.2 4.1 %add.29 = f32[768,768]{1,0:T(8,128)} add(f32[768,768]{1,0:T(8,128)} %get-tuple-element.42, f32[768,768]{1,0:T(8,128)} %get-tuple-element.52) | non-fusion elementwise | flops 589824 | bytes 7077888 | tf_op jit(solution)/shard_map/add | solution.py:1166
  336.2 0.7 pad_maximum_fusion
  (73 shorter events, 7.4 us)
Async XLA Ops:
  7.2 3.3 copy-start.13
  7.2 3.4 copy-start.4
  7.2 3.3 copy-start.5
  7.2 3.3 copy-start.6
  7.2 3.3 copy-start.10
  7.2 3.3 copy-start.7
  7.2 3.3 copy-start.8
  7.3 3.3 copy-start.9
  7.3 3.4 copy-start.2
  7.3 4.1 %copy-start.3 = (bf16[192,96]{1,0:T(8,128)(2,1)S(1)}, bf16[192,96]{1,0:T(8,128)(2,1)}, u32[]{:S(2)}) copy-start(bf16[192,96]{1,0:T(8,128)(2,1)} %param.19) | copy-start | bytes 110596
  7.3 72.3 %copy-start.11 = (s32[16]{0:T(128)S(1)}, s32[16]{0:T(128)}, u32[]{:S(2)}) copy-start(s32[16]{0:T(128)} %param.30) | copy-start | bytes 196
  7.3 72.3 %copy-start.12 = (s32[16]{0:T(128)S(1)}, s32[16]{0:T(128)}, u32[]{:S(2)}) copy-start(s32[16]{0:T(128)} %param.31) | copy-start | bytes 196
  7.3 121.8 %all-gather.5.cloned.1.call-start = ((), (), s32[]{:S(2)}) async-start(), calls=%async_computation | async-start | bytes 4866048 | tf_op jit(solution)/shard_map/all_gather | solution.py:1082
  8.0 143.4 %all-gather.7.cloned.1.call-start = ((), (), s32[]{:S(2)}) async-start(), calls=%async_computation.1 | async-start | bytes 4866048 | tf_op jit(solution)/shard_map/all_gather | solution.py:1082
  10.4 78.7 %copy-start = (bf16[768,768]{0,1:T(8,128)(2,1)}, bf16[768,768]{0,1:T(8,128)(2,1)S(1)}, u32[]{:S(2)}) copy-start(bf16[768,768]{0,1:T(8,128)(2,1)S(1)} %copy.69) | copy-start | bytes 3538948
  10.4 77.1 %collective-permute-start = (bf16[768,768]{0,1:T(8,128)(2,1)S(1)}, bf16[768,768]{0,1:T(8,128)(2,1)S(1)}, u32[]{:S(2)}, u32[]{:S(2)}) collective-permute-start(bf16[768,768]{0,1:T(8,128)(2,1)S(1)} %copy.69), channel_id=1, source_target_pairs={{0,1},{1,0},{2,3},{3,2},{4,5},{5,4},{6,7},{7,6},{8,9},{9,8},{10,11... | collective-permute-start | bytes 3538952 | tf_op jit(solution)/shard_map/ppermute | solution.py:1119
  87.5 41.6 %copy-start.1 = (bf16[768,768]{0,1:T(8,128)(2,1)}, bf16[768,768]{0,1:T(8,128)(2,1)S(1)}, u32[]{:S(2)}) copy-start(bf16[768,768]{0,1:T(8,128)(2,1)S(1)} %collective-permute-done) | copy-start | bytes 3538948
Sparse Core Ops, SparseCore 0:
  10.9 75.7 all-gather.4
  89.5 61.8 all-gather.6

commit v4 on v3

--- a/solution.py
+++ b/solution.py
@@ -356,7 +356,7 @@
     )(pre, cotangent, vectors, active, hidden, w2, w1, low_t)
 
 
-def group_back(grad_ref, grad_t_ref, own_t_ref, other_t_ref, weight_of, ctx_ref, q_ref, k_ref, v_ref, after_head):
+def group_back(grad_ref, weight_of, ctx_ref, q_ref, k_ref, v_ref, after_head):
     rows = grad_ref.shape[0]
     step = 256
     grad_context = mul(grad_ref[...], weight_of(512, 768)).astype(BF16).astype(F32)
@@ -409,17 +409,19 @@
     sums = [own_sum[:, 0:128]] + [
         own_sum[:, i : i + 128] + other_sum[:, i - 128 : i] for i in range(128, 640, 128)
     ]
-    own, other = own.astype(BF16), other.astype(BF16)
+    return own.astype(BF16), other.astype(BF16), sums
+
+
+def weight_grads(grad_t_ref, own_t_ref, other_t_ref, ctx_ref, own, other):
     grad_w = mul(own_t_ref[...], own)
     grad_w_other = mul(other_t_ref[...], other)
     grad_out = mul(grad_t_ref[...], ctx_ref[0])
-    columns = [
+    return [
         grad_w[:, 0:128],
         grad_w[:, 128:512] + grad_w_other[:, 0:384],
         grad_w[:, 512:640] + grad_w_other[:, 384:512] + grad_out[:, 0:128],
         grad_out[:, 128:256],
     ]
-    return own, other, sums, columns
 
 
 def attend_back_kernel(
@@ -439,18 +441,10 @@
     other_total_ref,
 ):
     group, groups = pl.program_id(0), pl.num_programs(0)
-    own, other, sums, columns = group_back(
-        grad_ref,
-        grad_t_ref,
-        own_t_ref,
-        other_t_ref,
-        functools.partial(weight, w_ref),
-        ctx_ref,
-        q_ref,
-        k_ref,
-        v_ref,
-        lambda head: None,
+    own, other, sums = group_back(
+        grad_ref, functools.partial(weight, w_ref), ctx_ref, q_ref, k_ref, v_ref, lambda head: None
     )
+    columns = weight_grads(grad_t_ref, own_t_ref, other_t_ref, ctx_ref, own, other)
     for number, piece in enumerate(sums):
         sums_ref[0, :, 128 * number : 128 * number + 128] = piece
     shape = (grad_w_ref.shape[0], 1, grad_w_ref.shape[2])
@@ -742,13 +736,13 @@
             total = total + other[...].astype(F32)
         target[...] = total.astype(target.dtype)
 
-    def to_core(self, place, theirs):
-        for number in (3, 1, 2, 0):
+    def to_core(self, place, theirs, numbers=(3, 1, 2, 0)):
+        for number in numbers:
             self.start(S0 + number, place, theirs(number), self.core.at[number, place], CORE)
 
     def first(self, place, mine):
         half, rows = self.half, self.rows
-        for number in (3, 1, 2, 0):
+        for number in (3, 1, 2):
             view = self.core.at[number, place]
             self.wait(S0 + number, place, view)
             self.add(view, mine(number))
@@ -775,19 +769,32 @@
             self.add(mine, view)
             self.start(X_HIGH, place, mine, self.sides.at[0, place, half:rows], ALONG_X)
 
-    def third(self, place):
+    def third(self, place, mine):
         half, rows = self.half, self.rows
+        self.wait(S0, place, self.core.at[0, place])
         self.wait(X_LOW, place, self.sides.at[0, place, 0:half])
         self.wait(Y_LOW, place, self.sides.at[1, place, 0:half])
         if half < rows:
             self.wait(Y_HIGH, place, self.sides.at[1, place, half:rows])
             self.wait(X_HIGH, place, self.sides.at[0, place, half:rows])
-        self.add(self.core.at[0, place], self.sides.at[0, place], self.sides.at[1, place])
+        self.add(self.core.at[0, place], mine(0), self.sides.at[0, place], self.sides.at[1, place])
 
     def along(self, kind, place):
         way = 0 if kind == Z_UP else 1
         to = (self.me, self.z + 1 if kind == Z_UP else self.z - 1)
         return self.copy(kind, place, self.core.at[0, place], self.line.at[way, place], to)
+
+    def hop(self, place, number):
+        for kind, here in ((Z_UP, number), (Z_DOWN, self.depth - 1 - number)):
+            if (here < place) if kind == Z_UP else (here > place):
+
+                @pl.when(self.z == here)
+                def _(kind=kind):
+                    if number > 0:
+                        view = self.line.at[0 if kind == Z_UP else 1, place]
+                        self.wait(kind, place, view)
+                        self.add(self.core.at[0, place], view)
+                    self.along(kind, place).start()
 
     def chain(self, distance):
         z, depth = self.z, self.depth
@@ -864,6 +871,12 @@
     grad_small,
     ff_mine,
     ff_sem,
+    ff_own,
+    ff_own_sem,
+    grad_heads,
+    grad_queries,
+    others,
+    other_total,
     sent,
     received,
     pair_send,
@@ -873,154 +886,220 @@
     send_sem, recv_sem = refs[-2:]
     me, z = lax.axis_index("dp"), lax.axis_index("mp")
     step = pl.program_id(0)
+    turn = lax.rem(step, depth)
     rows = grad_ref.shape[0]
     part = w_buf.shape[2]
+    width = 8 * part
     group_at = lambda s: z ^ (depth - 1 - s)
-    group = group_at(step)
+    group = group_at(turn)
     arrays = [(2 * part, refs[0:4]), (part, refs[4:8]), (8, refs[8:12])]
     ff, w, small = [
         Reduction(i, me, z, depth, size, bufs, send_sem, recv_sem) for i, (size, bufs) in enumerate(arrays)
     ]
     places = [depth - 1, 0] + list(range(1, depth - 1))[::-1]
+    lane = lanes((rows, 128))
 
     def load_w(s):
         return pltpu.make_async_copy(w_hbm.at[:, group_at(s)], w_buf.at[group_at(s)], w_sem.at[s])
 
-    def load_ff(turn, number):
-        source = ff_hbm.at[me ^ COLUMNS[number], places[turn]]
-        return pltpu.make_async_copy(source, ff_mine.at[turn % 2, number], ff_sem.at[turn % 2, number])
-
-    def exchange(place):
-        return pltpu.make_async_remote_copy(
-            src_ref=sent.at[place],
-            dst_ref=received.at[place],
-            send_sem=pair_send.at[place],
-            recv_sem=pair_recv.at[place],
-            device_id=(me, z ^ 1),
-            device_id_type=MESH,
-        )
+    def load_ff(number, column):
+        source = ff_hbm.at[me ^ COLUMNS[column], places[number]]
+        return pltpu.make_async_copy(source, ff_mine.at[number % 2, column - 1], ff_sem.at[number % 2, column - 1])
+
+    def load_ff_own(place):
+        return pltpu.make_async_copy(ff_hbm.at[me, place], ff_own.at[place], ff_own_sem.at[place])
+
+    exchange = pltpu.make_async_remote_copy(
+        src_ref=sent,
+        dst_ref=received,
+        send_sem=pair_send,
+        recv_sem=pair_recv,
+        device_id=(me, z ^ 1),
+        device_id_type=MESH,
+    )
 
     @pl.when(step == 0)
     def _():
         for s in range(depth):
             load_w(s).start()
-        for turn in range(2):
-            for number in range(4):
-                load_ff(turn, number).start()
+        for number in range(2):
+            for column in (3, 1, 2):
+                load_ff(number, column).start()
         meet(me, z, depth)
+        theirs = lambda place: lambda column: ff_hbm.at[me ^ CORE ^ COLUMNS[column], place]
         for place in places:
-            ff.to_core(place, lambda number, place=place: ff_hbm.at[me ^ CORE ^ COLUMNS[number], place])
+            ff.to_core(place, theirs(place), (3, 1, 2))
+        for place in places:
+            ff.to_core(place, theirs(place), (0,))
+            load_ff_own(place).start()
 
     for s in range(depth):
         pl.when(step == s)(lambda s=s: load_w(s).wait())
 
-    def ff_first(turn):
-        for number in range(4):
-            load_ff(turn, number).wait()
-        ff.first(places[turn], lambda number: ff_mine.at[turn % 2, number])
-        if turn + 2 < depth:
-            for number in range(4):
-                load_ff(turn + 2, number).start()
-
-    def ff_work(slot):
-        if slot < depth:
-            ff_first(slot)
-        if 0 <= slot - 2 < depth:
-            ff.second(places[slot - 2])
-        if 0 <= slot - 6 < depth:
-            ff.third(places[slot - 6])
-        last = 6 + depth - 1
-        if last <= slot < last + depth - 1:
-            ff.chain(depth - 1 - (slot - last))
+    def ff_first(number):
+        for column in (3, 1, 2):
+            load_ff(number, column).wait()
+        ff.first(places[number], lambda column: ff_mine.at[number % 2, column - 1])
+        if number + 2 < depth:
+            for column in (3, 1, 2):
+                load_ff(number + 2, column).start()
+
+    def ff_third(number):
+        place = places[number]
+        load_ff_own(place).wait()
+        ff.third(place, lambda column: ff_own.at[place])
+
+    work = {}
+
+    def plan(slot, action, *arguments):
+        work.setdefault(slot, []).append((action, arguments))
+
+    end = 6 * depth
+    for number, slots in enumerate(((1, 5, 9), (2, 8, 13), (4, 12, 17), (5, 15, 20))):
+        plan(slots[0], ff_first, number)
+        plan(slots[1], ff.second, places[number])
+        plan(slots[2], ff_third, number)
+        for hop in range(depth - 1):
+            plan(min(slots[2] + 4 * hop, end + (number == 3) * (hop - 1)), ff.hop, places[number], hop)
+
+    def do(slot):
+        for action, arguments in work.get(slot, ()):
+            action(*arguments)
 
     def w_first(s):
         place = group_at(s)
-        w.first(place, lambda number: grad_w.at[s, me ^ COLUMNS[number]])
-        small.first(place, lambda number: grad_small.at[s, me ^ COLUMNS[number]])
+        w.first(place, lambda column: grad_w.at[s, me ^ COLUMNS[column]])
+        small.first(place, lambda column: grad_small.at[s, me ^ COLUMNS[column]])
 
     def w_second(s):
         w.second(group_at(s))
         small.second(group_at(s))
 
     def w_third(s):
-        w.third(group_at(s))
-        small.third(group_at(s))
-
-    def take(place):
-        exchange(place).wait_recv()
-        block = received[place]
-        low = lanes((rows, 128)) < HEAD
-        zero = jnp.zeros((rows, 128), BF16)
-        ends = block[:, 0:128]
-        other = jnp.concatenate([jnp.where(low, zero, ends), block[:, 128:384], jnp.where(low, ends, zero)], axis=1)
-        view = w_buf.at[place]
-        grad_own_ref[...] += mul(other, view[:, :, 128:640].reshape(part * 8, 512), NT)
+        place = group_at(s)
+        w.third(place, lambda column: grad_w.at[s, me ^ COLUMNS[column]])
+        small.third(place, lambda column: grad_small.at[s, me ^ COLUMNS[column]])
+
+    def w_chain(distance):
+        w.chain(distance)
+        small.chain(distance)
 
     def after_head(head):
-        for s in range(depth):
-            slot = 3 * s + head
-            pl.when(step == s)(lambda slot=slot: ff_work(slot))
+        for s in range(2 * depth):
+            if 3 * s + head in work:
+                pl.when(step == s)(lambda slot=3 * s + head: do(slot))
+        pl.when(step > depth)(lambda: (w_first, w_second, w_third)[head](step - depth - 1))
+        if head == 2:
+            for s in range(depth - 1):
+                pl.when(step == depth + 1 + s)(lambda s=s: w_chain(depth - 1 - s))
+
+    def weight_of(first, last):
+        return w_buf[group, :, :, first:last].reshape(width, last - first)
+
+    @pl.when(step < depth)
+    def _():
+        grad_context = mul(grad_ref[...], weight_of(512, 768)).astype(BF16).astype(F32)
+        for head in range(3):
+            grad_head = head_block(grad_context, 1 + head)
+            context = head_block(ctx_ref[0].astype(F32), 1 + head)
+            delta = jnp.sum(jnp.where(lane < HEAD, grad_head * context, 0.0), axis=1, keepdims=True)
+            high, middle, low = three_parts(-delta)
+            tail = jnp.where(
+                lane == HEAD, high, jnp.where(lane == HEAD + 1, middle, jnp.where(lane == HEAD + 2, low, 0.0))
+            )
+            grad_heads[turn, head] = jnp.where(lane < HEAD, grad_head, tail).astype(BF16)
+
+    grads = []
+    chunk = 256
+    for head in range(3):
+        keys_t = k_ref[head].T
+        grad_query = []
+        grad_keys = grad_values = None
+        for first in range(0, rows, chunk):
+            query_here = q_ref[head, first : first + chunk, :]
+            grad_here = grad_heads[turn, head, first : first + chunk, :]
+            weights = jnp.exp(mul(k_ref[head], query_here, NT))
+            grad_scores = (weights * mul(v_ref[head], grad_here, NT)).astype(BF16)
+            values_part = mul(weights.astype(BF16), grad_here)
+            keys_part = mul(grad_scores, query_here)
+            grad_values = values_part if grad_values is None else grad_values + values_part
+            grad_keys = keys_part if grad_keys is None else grad_keys + keys_part
+            grad_query.append(mul(keys_t, grad_scores))
+        grads.append((jnp.concatenate(grad_query, axis=1).T * SCALE, grad_keys, grad_values))
+        after_head(head)
+    (q0, k0, v0), (q1, k1, v1), (q2, k2, v2) = grads
+    blank = jnp.zeros((rows, 128), F32)
+    k12, v01 = pair(k1, k2), pair(v0, v1)
+
+    @pl.when(step < depth)
+    def _():
+        grad_queries[turn, :, 0:128] = pair(q0, q1)
+        grad_queries[turn, :, 128:256] = q2
+        other = jnp.concatenate([pair(blank, k0), k12, v01, pair(v2, blank)], axis=1).astype(BF16)
+        others[turn] = other
+        other_part = mul(other, weight_of(128, 640), NT)
+
+        @pl.when(step == 0)
+        def _():
+            other_total[...] = other_part
 
         @pl.when(step > 0)
         def _():
-            [w_first, w_second, w_third][head](step - 1)
-
-    own, other, sums, columns = group_back(
-        grad_ref,
-        grad_t_ref,
-        own_t_ref,
-        other_t_ref,
-        lambda first, last: w_buf[group, :, :, first:last].reshape(part * 8, last - first),
-        ctx_ref,
-        q_ref,
-        k_ref,
-        v_ref,
-        after_head,
-    )
-    sent[group, :, 0:128] = other[:, 0:128] + other[:, 384:512]
-    sent[group, :, 128:384] = other[:, 128:384]
-    exchange(group).start()
-    first = 0
-    for piece in columns:
-        last = first + piece.shape[1]
-        grad_w[step, :, :, first:last] = piece.astype(BF16).reshape(8, part, last - first)
-        first = last
-    row = lax.broadcasted_iota(jnp.int32, (8, 128), 0)
-    late = jnp.zeros((8, 128), F32)
-    for number, piece in enumerate(sums):
-        late = jnp.where(row == number, piece, late)
-    for owner in range(8):
-        grad_small[step, owner] = early_ref[owner, group] + late
-    w.to_core(group, lambda number: grad_w.at[step, me ^ CORE ^ COLUMNS[number]])
-    small.to_core(group, lambda number: grad_small.at[step, me ^ CORE ^ COLUMNS[number]])
-    own_part = mul(own, w_buf[group, :, :, 0:640].reshape(part * 8, 640), NT)
-
-    @pl.when(step == 0)
-    def _():
-        grad_own_ref[...] = own_part
-
-    @pl.when(step > 0)
-    def _():
-        grad_own_ref[...] += own_part
-        take(group_at(step - 1) ^ 1)
-
-    @pl.when(step == depth - 1)
+            other_total[...] += other_part
+
+        @pl.when(step == depth - 1)
+        def _():
+            sent[...] = other_total[...].astype(BF16)
+            exchange.start()
+
+    @pl.when(step >= depth)
+    def _():
+        q01 = pair(q0, q1) + grad_queries[turn, :, 0:128]
+        q2_all = q2 + grad_queries[turn, :, 128:256]
+        own = jnp.concatenate([q01, pair(q2_all, k0), k12, v01, pair(v2, blank)], axis=1)
+        other = others[turn]
+        own_sum = jnp.sum(own, axis=0, keepdims=True)
+        other_sum = jnp.sum(other.astype(F32), axis=0, keepdims=True)
+        row = lax.broadcasted_iota(jnp.int32, (8, 128), 0)
+        late = jnp.where(row == 0, own_sum[:, 0:128], 0.0)
+        for number in range(1, 5):
+            piece = own_sum[:, 128 * number : 128 * number + 128] + other_sum[:, 128 * number - 128 : 128 * number]
+            late = jnp.where(row == number, piece, late)
+        for owner in range(8):
+            grad_small[turn, owner] = early_ref[owner, group] + late
+        own = own.astype(BF16)
+        first = 0
+        for piece in weight_grads(grad_t_ref, own_t_ref, other_t_ref, ctx_ref, own, other):
+            last = first + piece.shape[1]
+            grad_w[turn, :, :, first:last] = piece.astype(BF16).reshape(8, part, last - first)
+            first = last
+        w.to_core(group, lambda column: grad_w.at[turn, me ^ CORE ^ COLUMNS[column]])
+        small.to_core(group, lambda column: grad_small.at[turn, me ^ CORE ^ COLUMNS[column]])
+        own_part = mul(own, weight_of(0, 640), NT)
+
+        @pl.when(step == depth)
+        def _():
+            grad_own_ref[...] = own_part
+
+        @pl.when(step > depth)
+        def _():
+            grad_own_ref[...] += own_part
+
+    @pl.when(step == 2 * depth - 1)
     def _():
         w_first(depth - 1)
-        for distance in range(depth - 1, 0, -1):
-            w.chain(distance)
-            small.chain(distance)
-            if distance == depth - 1:
-                w_second(depth - 1)
+        do(end)
+        exchange.wait_recv()
+        grad_own_ref[...] += received[...].astype(F32)
+        w_second(depth - 1)
+        do(end + 1)
+        w_third(depth - 1)
         ff.finish(ff_out)
-        w_third(depth - 1)
         w.finish(w_out)
         small.finish(small_out)
-        take(group ^ 1)
         for array in (ff, w, small):
             array.drain()
-        for place in range(depth):
-            exchange(place).wait_send()
+        exchange.wait_send()
 
 
 def linked_back(grad, grad_t, own_t, other_t, early, weights, grad_ff, ctx, query, keys, values):
@@ -1028,27 +1107,30 @@
     n_dp, groups, part = weights.shape[:3]
     whole = pl.BlockSpec(memory_space=pltpu.VMEM)
     anywhere = pl.BlockSpec(memory_space=pl.ANY)
-    by_group = lambda g: (groups - 1 - g, 0, 0)
+    by_group = lambda g: (groups - 1 - lax.rem(g, groups), 0, 0)
+    by_half = lambda g: (groups - 1 - lax.rem(g, groups), 1 - g // groups, 0)
     flops = groups * (3 * 2 * rows * width * 640 + 3 * 10 * rows * SLOT * 128)
     scratch = []
     for size, columns, kind in ((2 * part, width, BF16), (part, width, BF16), (8, 128, F32)):
         block = (size, columns)
-        scratch += [pltpu.VMEM((lead, groups) + block, kind) for lead in (4,)]
-        scratch += [pltpu.VMEM((groups,) + block, kind)]
-        scratch += [pltpu.VMEM((2, groups) + block, kind)] * 2
+        scratch += [
+            pltpu.VMEM((4, groups) + block, kind),
+            pltpu.VMEM((groups,) + block, kind),
+            pltpu.VMEM((2, groups) + block, kind),
+            pltpu.VMEM((2, groups) + block, kind),
+        ]
     sems = pltpu.SemaphoreType.DMA((3, SCATTER_KINDS, groups))
-    pairs = pltpu.SemaphoreType.DMA((groups,))
     return pl.pallas_call(
         functools.partial(linked_back_kernel, groups),
         name="linked_back",
-        grid=(groups,),
+        grid=(2 * groups,),
         in_specs=[whole] * 5
         + [anywhere] * 2
         + [
             pl.BlockSpec((1, rows, 256), by_group),
             pl.BlockSpec((3, rows, 128), by_group),
-            pl.BlockSpec((3, SLOT, 128), by_group),
-            pl.BlockSpec((3, SLOT, 128), by_group),
+            pl.BlockSpec((3, rows, 128), by_half),
+            pl.BlockSpec((3, rows, 128), by_half),
         ],
         out_specs=[whole] * 4,
         out_shape=[
@@ -1062,12 +1144,18 @@
             pltpu.SemaphoreType.DMA((groups,)),
             pltpu.VMEM((groups, n_dp, part, width), BF16),
             pltpu.VMEM((groups, n_dp, 8, 128), F32),
-            pltpu.VMEM((2, 4, 2 * part, width), BF16),
-            pltpu.SemaphoreType.DMA((2, 4)),
-            pltpu.VMEM((groups, rows, 384), BF16),
-            pltpu.VMEM((groups, rows, 384), BF16),
-            pairs,
-            pairs,
+            pltpu.VMEM((2, 3, 2 * part, width), BF16),
+            pltpu.SemaphoreType.DMA((2, 3)),
+            pltpu.VMEM((groups, 2 * part, width), BF16),
+            pltpu.SemaphoreType.DMA((groups,)),
+            pltpu.VMEM((groups, 3, rows, 128), BF16),
+            pltpu.VMEM((groups, rows, 256), F32),
+            pltpu.VMEM((groups, rows, 512), BF16),
+            pltpu.VMEM((rows, width), F32),
+            pltpu.VMEM((rows, width), BF16),
+            pltpu.VMEM((rows, width), BF16),
+            pltpu.SemaphoreType.DMA,
+            pltpu.SemaphoreType.DMA,
         ]
         + scratch
         + [sems, sems],

time: 350 us -> 332 us (0.949)
  Pallas kernels: 288 us -> 273 us
    pallas_call x1, Pallas kernels: 134 us -> 119 us  [linked_back(): pl.pallas_call(functools.partial(linked_back_kernel, groups), name='linke...]
  transfers between devices with their start and end apart: 3 -> 3, of which waited for: 1 -> 1; matrix products, arithmetic and copies ran while one was open for 4% -> 4% of each run, Pallas kernels for 34% -> 36%
where the time goes in v4:
time: 332 us; the launch traced here: 329 us
  Pallas kernels  273 us (82%)
  local copies, waits for them, and re-layouts  17.9 us (5%)
  between operations  15.8 us (5%)
  waiting for transfers between devices  12.5 us (4%)
  other arithmetic  9.33 us (3%)
    pallas_call x1, Pallas kernels, linked_back(): pl.pallas_call(functools.partial(linked_back_kernel, groups), name='linke...  119 us
    pallas_call x1, Pallas kernels, gather_all(): pl.pallas_call(functools.partial(gather_kernel, count, n_mp), name='gathe...  66.2 us
    pallas_call x1, Pallas kernels, attend(): pl.pallas_call(attend_kernel, name='attend', grid_spec=pltpu.PrefetchScal...  40 us
    pallas_call x1, Pallas kernels, down(): pl.pallas_call(functools.partial(down_kernel, groups), name='down', grid=...  36.6 us
    pallas_call x1, Pallas kernels, up(): pl.pallas_call(up_kernel, name='up', grid=(groups,), in_specs=[pl.BlockSp...  11.2 us
    all_gather x2, waiting for transfers between devices, blocks(): lax.all_gather(local, BOTH, axis=0, tiled=False)  11.1 us
  transfers between devices with their start and end apart: 3, of which 1 were waited for; matrix products, arithmetic and copies ran while one was open for 4% of the time, Pallas kernels for 36%

profile of v4, /device:TPU:8, one launch (start us, length us, event | category | flops | bytes accessed | tf_op | source)
XLA Modules:
  0.0 328.8 jit_solution(6533641111002622418)
XLA Ops:
  7.4 0.7 all-gather.5.cloned.1.call-update
  8.1 0.7 all-gather.7.cloned.1.call-update
  8.8 1.6 copy.69
  11.5 0.8 pad_maximum_fusion.1.refs_0_
  12.2 66.2 %gather.1 = (bf16[8,4,96,768]{3,2,1,0:T(8,128)(2,1)}, f32[8,4,8,128]{3,2,1,0:T(8,128)}) custom-call(bf16[96,768]{1,0:T(8,128)(2,1)} %pad_maximum_fusion.1.refs_0_, f32[8,128]{1,0:T(8,128)} %pad_bitcast_fusion.refs_1_), custom_call_target="tpu_custom_call" | custom-call | tf_op jit(solution)/shard_map/gather/pallas_call | solution.py:695
  78.4 0.9 copy.88
  82.9 0.7 slice.101.shift_ref
  84.3 0.7 reshape.90.bias_ref
  87.5 1.6 copy.74.other_ref
  89.1 40.0 %attend.1 = (f32[768,768]{1,0:T(8,128)}, bf16[4,768,256]{2,1,0:T(8,128)(2,1)}, bf16[12,768,128]{2,1,0:T(8,128)(2,1)}, bf16[12,1536,128]{2,1,0:T(8,128)(2,1)}, bf16[12,1536,128]{2,1,0:T(8,128)(2,1)}) custom-call(s32[4]{0:T(128)} %iota_xor_fusion.order_ref, s32[2]{0:T(128)} %pad_add_fusion.valid_ref, bf16[768,768]{1,0:T(8,128)(2,1)} %own_ref.1, ...), custom_call_target="tpu_custom_call" | custom-call | flops 53150220288 | bytes 25165824 | tf_op jit(solution)/shard_map/attend/pallas_call | solution.py:132
  129.1 11.2 %up.1 = (f32[4,768,768]{2,1,0:T(8,128)}, bf16[4,768,768]{2,1,0:T(8,128)(2,1)}, bf16[768,768]{1,0:T(8,128)(2,1)}, bf16[768,768]{1,0:T(8,128)(2,1)}) custom-call(f32[768,768]{1,0:T(8,128)} %get-tuple-element.37.pre_ref, f32[1,768]{1,0:T(1,128)} %slice.99.gain_ref, f32[1,768]{1,0:T(1,128)} %slice.101.shift_ref, bf16[8,4,96,768]{3,2,1,0:T(8,128)(2,1)} %bitcast.75, ...), custom_call_target="tpu_custom_call" | custom-call | flops 3623878656 | bytes 25165824 | tf_op jit(solution)/shard_map/up/pallas_call | solution.py:185
  140.3 11.1 %all-gather.7.cloned.1.call-done = bf16[3072,768]{1,0:T(8,128)(2,1)} async-done(((bf16[96,768]{1,0:T(8,128)(2,1)}), bf16[3072,768]{1,0:T(8,128)(2,1)}) %all-gather.7.cloned.1.call-update) | async-done | bytes 4718608 | tf_op jit(solution)/shard_map/all_gather | solution.py:1170
  151.4 36.6 %down.1 = (bf16[768,768]{1,0:T(8,128)(2,1)}, f32[768,768]{1,0:T(8,128)}, bf16[768,768]{1,0:T(8,128)(2,1)}, bf16[768,768]{1,0:T(8,128)(2,1)}, bf16[8,4,192,768]{3...) custom-call(f32[768,768]{1,0:T(8,128)} %get-tuple-element.37.pre_ref, bf16[768,768]{1,0:T(8,128)(2,1)} %cot_ref.1, ...), custom_call_target="tpu_custom_call" | custom-call | flops 18119393280 | bytes 50331648 | tf_op jit(solution)/shard_map/down/pallas_call | solution.py:314
  188.0 0.8 reshape.92
  189.0 0.8 reduce
  189.9 0.7 pad.15.early_ref
  190.6 119.1 %linked_back.1 = (f32[192,768]{1,0:T(8,128)}, f32[96,768]{1,0:T(8,128)}, f32[8,128]{1,0:T(8,128)}, f32[768,768]{1,0:T(8,128)}) custom-call(bf16[768,768]{1,0:T(8,128)(2,1)} %get-tuple-element.43.grad_ref, bf16[768,768]{1,0:T(8,128)(2,1)} %get-tuple-element.44.grad_t_ref, bf16[768,768]{1,0:T(8,128)(2,1)} %bitcast.57, bf16[768,768]{1,0:T(8,128)(2,1)} %bitcast.58, ...), custom_call_target="tpu_custom_call" | custom-call | flops 108716359680 | bytes 50331648 | tf_op jit(solution)/shard_map/linked_back/pallas_call | solution.py:1123
  309.7 1.2 slice_bitcast_fusion.1
  310.9 1.9 slice_bitcast_fusion
  312.8 0.7 copy.83
  313.5 1.3 slice.112
  314.8 1.6 fusion.2
  316.9 4.1 %add.29 = f32[768,768]{1,0:T(8,128)} add(f32[768,768]{1,0:T(8,128)} %get-tuple-element.42, f32[768,768]{1,0:T(8,128)} %get-tuple-element.52) | non-fusion elementwise | flops 589824 | bytes 7077888 | tf_op jit(solution)/shard_map/add | solution.py:1254
  321.0 0.7 pad_maximum_fusion
  (73 shorter events, 7.4 us)
Async XLA Ops:
  7.2 3.3 copy-start.13
  7.2 3.4 %copy-start.4 = (f32[24]{0:T(128)S(1)}, f32[24]{0:T(128)}, u32[]{:S(2)}) copy-start(f32[24]{0:T(128)} %param.20) | copy-start | bytes 292
  7.2 3.3 %copy-start.5 = (f32[24]{0:T(128)S(1)}, f32[24]{0:T(128)}, u32[]{:S(2)}) copy-start(f32[24]{0:T(128)} %param.21) | copy-start | bytes 292
  7.2 3.3 %copy-start.6 = (f32[24]{0:T(128)S(1)}, f32[24]{0:T(128)}, u32[]{:S(2)}) copy-start(f32[24]{0:T(128)} %param.22) | copy-start | bytes 292
  7.2 3.3 %copy-start.10 = (bf16[96]{0:T(256)(128)(2,1)S(1)}, bf16[96]{0:T(256)(128)(2,1)}, u32[]{:S(2)}) copy-start(bf16[96]{0:T(256)(128)(2,1)} %param.24) | copy-start | bytes 580
  7.2 3.3 %copy-start.7 = (f32[24]{0:T(128)S(1)}, f32[24]{0:T(128)}, u32[]{:S(2)}) copy-start(f32[24]{0:T(128)} %param.26) | copy-start | bytes 292
  7.2 3.3 %copy-start.8 = (f32[24]{0:T(128)S(1)}, f32[24]{0:T(128)}, u32[]{:S(2)}) copy-start(f32[24]{0:T(128)} %param.27) | copy-start | bytes 292
  7.3 3.3 %copy-start.9 = (f32[24]{0:T(128)S(1)}, f32[24]{0:T(128)}, u32[]{:S(2)}) copy-start(f32[24]{0:T(128)} %param.28) | copy-start | bytes 292
  7.3 3.4 %copy-start.2 = (bf16[3,96,192]{2,1,0:T(8,128)(2,1)S(1)}, bf16[3,96,192]{2,1,0:T(8,128)(2,1)}, u32[]{:S(2)}) copy-start(bf16[3,96,192]{2,1,0:T(8,128)(2,1)} %param.17) | copy-start | bytes 331780
  7.3 4.1 %copy-start.3 = (bf16[192,96]{1,0:T(8,128)(2,1)S(1)}, bf16[192,96]{1,0:T(8,128)(2,1)}, u32[]{:S(2)}) copy-start(bf16[192,96]{1,0:T(8,128)(2,1)} %param.19) | copy-start | bytes 110596
  7.3 72.3 %copy-start.11 = (s32[16]{0:T(128)S(1)}, s32[16]{0:T(128)}, u32[]{:S(2)}) copy-start(s32[16]{0:T(128)} %param.30) | copy-start | bytes 196
  7.3 72.3 %copy-start.12 = (s32[16]{0:T(128)S(1)}, s32[16]{0:T(128)}, u32[]{:S(2)}) copy-start(s32[16]{0:T(128)} %param.31) | copy-start | bytes 196
  7.3 121.8 %all-gather.5.cloned.1.call-start = ((), (), s32[]{:S(2)}) async-start(), calls=%async_computation | async-start | bytes 4866048 | tf_op jit(solution)/shard_map/all_gather | solution.py:1170
  8.0 143.4 %all-gather.7.cloned.1.call-start = ((), (), s32[]{:S(2)}) async-start(), calls=%async_computation.1 | async-start | bytes 4866048 | tf_op jit(solution)/shard_map/all_gather | solution.py:1170
  10.4 78.7 %copy-start = (bf16[768,768]{0,1:T(8,128)(2,1)}, bf16[768,768]{0,1:T(8,128)(2,1)S(1)}, u32[]{:S(2)}) copy-start(bf16[768,768]{0,1:T(8,128)(2,1)S(1)} %copy.69) | copy-start | bytes 3538948
  10.4 77.1 %collective-permute-start = (bf16[768,768]{0,1:T(8,128)(2,1)S(1)}, bf16[768,768]{0,1:T(8,128)(2,1)S(1)}, u32[]{:S(2)}, u32[]{:S(2)}) collective-permute-start(bf16[768,768]{0,1:T(8,128)(2,1)S(1)} %copy.69), channel_id=1, source_target_pairs={{0,1},{1,0},{2,3},{3,2},{4,5},{5,4},{6,7},{7,6},{8,9},{9,8},{10,11... | collective-permute-start | bytes 3538952 | tf_op jit(solution)/shard_map/ppermute | solution.py:1207
  87.5 41.6 %copy-start.1 = (bf16[768,768]{0,1:T(8,128)(2,1)}, bf16[768,768]{0,1:T(8,128)(2,1)S(1)}, u32[]{:S(2)}) copy-start(bf16[768,768]{0,1:T(8,128)(2,1)S(1)} %collective-permute-done) | copy-start | bytes 3538948
Sparse Core Ops, SparseCore 0:
  10.9 75.7 all-gather.4
  89.5 61.8 all-gather.6

commit v5 on v4

--- a/solution.py
+++ b/solution.py
@@ -65,14 +65,10 @@
     return ref[:, 0, :, first:last].reshape(ref.shape[0] * ref.shape[2], last - first)
 
 
-def attend_kernel(
-    order_ref, valid_ref, own_ref, other_ref, w_ref, qv_bias_ref, out_bias_ref, pre_ref, ctx_ref, q_ref, k_ref, v_ref
-):
-    group, groups = pl.program_id(0), pl.num_programs(0)
+def attend_group(bias, weight_of, valid_ref, own_ref, other_ref, ctx_ref, q_ref, k_ref, v_ref, after_head):
     rows = own_ref.shape[0]
-    bias = qv_bias_ref[0]
-    projected = mul(own_ref[...], weight(w_ref, 0, 640)) + bias
-    projected_other = mul(other_ref[...], weight(w_ref, 128, 640)) + bias[:, 128:]
+    projected = mul(own_ref[...], weight_of(0, 640)) + bias
+    projected_other = mul(other_ref[...], weight_of(128, 640)) + bias[:, 128:]
     lane = lanes((rows, 128))
     row = lax.broadcasted_iota(jnp.int32, (rows, 128), 0)
     contexts = []
@@ -108,11 +104,21 @@
             )
             q_ref[head, first : first + step, :] = kept.astype(BF16)
         contexts.append(jnp.concatenate(pieces, axis=0))
+        after_head(head)
     first_half = jnp.where(lane < HEAD, 0.0, pltpu.roll(contexts[0], HEAD, 1)).astype(BF16)
     second_half = pair(contexts[1], contexts[2]).astype(BF16)
     ctx_ref[0, :, 0:128] = first_half
     ctx_ref[0, :, 128:256] = second_half
-    part = mul(ctx_ref[0], weight(w_ref, 512, 768), NT)
+    return mul(ctx_ref[0], weight_of(512, 768), NT)
+
+
+def attend_kernel(
+    order_ref, valid_ref, own_ref, other_ref, w_ref, qv_bias_ref, out_bias_ref, pre_ref, ctx_ref, q_ref, k_ref, v_ref
+):
+    group = pl.program_id(0)
+    weight_of = functools.partial(weight, w_ref)
+    kept = (ctx_ref, q_ref, k_ref, v_ref)
+    part = attend_group(qv_bias_ref[0], weight_of, valid_ref, own_ref, other_ref, *kept, lambda head: None)
 
     @pl.when(group == 0)
     def _():
@@ -539,6 +545,11 @@
             yield place, (place >= 0) & (place < depth)
 
 
+def near_at(z, depth, distance):
+    for place in (z - distance, z + distance):
+        yield place, (place >= 0) & (place < depth)
+
+
 def given(condition, action):
     if condition is None:
         action()
@@ -554,9 +565,7 @@
 GATHER_KINDS = C0 + 4
 
 
-def gather_kernel(count, depth, *refs):
-    locals_, wholes = refs[:count], refs[count : 2 * count]
-    send_sem, recv_sem = refs[2 * count :]
+def gather_stages(depth, locals_, wholes, send_sem, recv_sem):
     me, z = lax.axis_index("dp"), lax.axis_index("mp")
 
     def copy(which, kind, place, source, target, to):
@@ -568,8 +577,6 @@
             device_id=to,
             device_id_type=MESH,
         )
-
-    meet(me, z, depth)
 
     def column(which, place, source, owner, kinds):
         whole = wholes[which]
@@ -649,28 +656,19 @@
         for number, bit in enumerate(COLUMNS):
             arrived(which, C0 + number, place, me ^ CORE ^ bit, 0, rows)
 
-    order = []
-    for which in range(count):
+    def begin(which):
         pltpu.make_async_copy(
             locals_[which], wholes[which].at[me, z], send_sem.at[which, GATHER_KINDS, 0]
         ).start()
-        order += [(which,) + item for item in near_first(z, depth)]
-    lag = len(order) // count
-    for step in range(len(order) + 2 * lag):
-        if step < len(order):
-            first_stage(*order[step])
-        if 0 <= step - lag < len(order):
-            second_stage(*order[step - lag])
-        if 0 <= step - 2 * lag:
-            third_stage(*order[step - 2 * lag])
-    for which in range(count):
+
+    def finish(which):
         rows = locals_[which].shape[0]
         half, _ = halves(rows)
         for place in range(depth):
             last_stage(which, place)
         for place, condition in near_first(z, depth):
 
-            def sent(which=which, place=place, own=condition is None):
+            def sent(place=place, own=condition is None):
                 whole = wholes[which].at[me, place]
                 pieces = [(X, 0, rows), (Y, 0, rows), (VIA_Y, 0, half)] + [(C0 + n, 0, rows) for n in range(4)]
                 if half < rows:
@@ -687,6 +685,163 @@
         pltpu.make_async_copy(
             locals_[which], wholes[which].at[me, z], send_sem.at[which, GATHER_KINDS, 0]
         ).wait()
+
+    return begin, first_stage, second_stage, third_stage, finish
+
+
+def gather_kernel(count, depth, *refs):
+    locals_, wholes = refs[:count], refs[count : 2 * count]
+    me, z = lax.axis_index("dp"), lax.axis_index("mp")
+    meet(me, z, depth)
+    begin, first, second, third, finish = gather_stages(depth, locals_, wholes, *refs[2 * count :])
+    order = []
+    for which in range(count):
+        begin(which)
+        order += [(which,) + item for item in near_first(z, depth)]
+    lag = len(order) // count
+    for step in range(len(order) + 2 * lag):
+        if step < len(order):
+            first(*order[step])
+        if 0 <= step - lag < len(order):
+            second(*order[step - lag])
+        if 0 <= step - 2 * lag:
+            third(*order[step - 2 * lag])
+    for which in range(count):
+        finish(which)
+
+
+FIRST_AT = {1: [(0, 1)], 2: [(1, 1)], 3: [(0, 2)], 4: [(1, 2)], 5: [(0, 3)], 6: [(1, 3)]}
+SECOND_AT = {2: [(0, 0)], 3: [(1, 0)], 5: [(0, 1)], 8: [(1, 1)], 9: [(0, 2)], 10: [(1, 2), (0, 3)], 11: [(1, 3)]}
+THIRD_AT = {6: [(0, 0)], 7: [(1, 0)], 9: [(0, 1)], 11: [(1, 1)], 12: [(0, 2), (1, 2), (0, 3), (1, 3)]}
+
+
+def linked_attend_kernel(
+    depth,
+    valid_ref,
+    own_ref,
+    other_ref,
+    qv_bias_ref,
+    out_bias_ref,
+    w1_ref,
+    w2_ref,
+    w_hbm,
+    pre_ref,
+    ctx_ref,
+    q_ref,
+    k_ref,
+    v_ref,
+    w1_out,
+    w2_out,
+    w_buf,
+    w_sem,
+    send_sem,
+    recv_sem,
+):
+    me, z = lax.axis_index("dp"), lax.axis_index("mp")
+    step = pl.program_id(0)
+    group = z ^ step
+    part, width = w_buf.shape[2:]
+
+    def load_w(s):
+        return pltpu.make_async_copy(w_hbm.at[:, z ^ s], w_buf.at[s], w_sem.at[s])
+
+    begin, first, second, third, finish = gather_stages(depth, (w1_ref, w2_ref), (w1_out, w2_out), send_sem, recv_sem)
+
+    def around(stage, which, distance):
+        for place, condition in near_first(z, depth) if distance == 0 else near_at(z, depth, distance):
+            if distance == 0 and condition is not None:
+                break
+            stage(which, place, condition)
+
+    def do(slot):
+        for stage, plan in ((first, FIRST_AT), (second, SECOND_AT), (third, THIRD_AT)):
+            for which, distance in plan.get(slot, ()):
+                around(stage, which, distance)
+
+    @pl.when(step == 0)
+    def _():
+        for s in range(depth):
+            load_w(s).start()
+        meet(me, z, depth)
+        for which in range(2):
+            begin(which)
+            around(first, which, 0)
+
+    for s in range(depth):
+        pl.when(step == s)(lambda s=s: load_w(s).wait())
+
+    def after_head(head):
+        for s in range(depth):
+            pl.when(step == s)(lambda s=s: do(3 * s + head))
+
+    part_sum = attend_group(
+        qv_bias_ref[group],
+        lambda low, high: w_buf[step, :, :, low:high].reshape(8 * part, high - low),
+        valid_ref,
+        own_ref,
+        other_ref,
+        ctx_ref,
+        q_ref,
+        k_ref,
+        v_ref,
+        after_head,
+    )
+
+    @pl.when(step == 0)
+    def _():
+        pre_ref[...] = part_sum + (out_bias_ref[...] + own_ref[...].astype(F32))
+
+    @pl.when(step > 0)
+    def _():
+        pre_ref[...] += part_sum
+
+    @pl.when(step == depth - 1)
+    def _():
+        do(3 * depth)
+        for which in range(2):
+            finish(which)
+
+
+def linked_attend(valid, own, other, weights, qv_bias, out_bias, w1, w2):
+    rows, width = own.shape
+    n_dp, groups, part = weights.shape[:3]
+    whole = pl.BlockSpec(memory_space=pltpu.VMEM)
+    anywhere = pl.BlockSpec(memory_space=pl.ANY)
+    by_group = lambda g: (g, 0, 0)
+    flops = groups * (2 * 2 * rows * width * 640 + 3 * 4 * rows * SLOT * 128)
+    sems = pltpu.SemaphoreType.DMA((2, GATHER_KINDS + 1, groups))
+    return pl.pallas_call(
+        functools.partial(linked_attend_kernel, groups),
+        name="linked_attend",
+        grid=(groups,),
+        in_specs=[pl.BlockSpec(memory_space=pltpu.SMEM)] + [whole] * 6 + [anywhere],
+        out_specs=[
+            whole,
+            pl.BlockSpec((1, rows, 256), by_group),
+            pl.BlockSpec((3, rows, 128), by_group),
+            pl.BlockSpec((3, SLOT, 128), by_group),
+            pl.BlockSpec((3, SLOT, 128), by_group),
+            anywhere,
+            anywhere,
+        ],
+        out_shape=[
+            jax.ShapeDtypeStruct((rows, width), F32),
+            jax.ShapeDtypeStruct((groups, rows, 256), BF16),
+            jax.ShapeDtypeStruct((3 * groups, rows, 128), BF16),
+            jax.ShapeDtypeStruct((3 * groups, SLOT, 128), BF16),
+            jax.ShapeDtypeStruct((3 * groups, SLOT, 128), BF16),
+            jax.ShapeDtypeStruct((n_dp, groups) + w1.shape, BF16),
+            jax.ShapeDtypeStruct((n_dp, groups) + w2.shape, BF16),
+        ],
+        scratch_shapes=[
+            pltpu.VMEM((groups, n_dp, part, width), BF16),
+            pltpu.SemaphoreType.DMA((groups,)),
+            sems,
+            sems,
+        ],
+        cost_estimate=pl.CostEstimate(flops=4 * flops, bytes_accessed=36 << 20, transcendentals=12 * rows * SLOT),
+        compiler_params=pltpu.CompilerParams(collective_id=3, has_side_effects=True, vmem_limit_bytes=60 << 20),
+    )(valid, own, other, qv_bias, out_bias, w1, w2, weights)
 
 
 def gather_all(locals_, n_dp, n_mp, number):
@@ -1213,7 +1368,6 @@
     small = jnp.pad(small, (0, -entries % 1024)).reshape(-1, 128)
     mesh_shape = (n_dp, n_mp)
     w_attn, small = gather_first([packed, small], mesh_shape)
-    w1, w2 = blocks(w_ff1, mesh_shape), blocks(w_ff2.T, mesh_shape)
     small = small.reshape(n_dp * n_mp, -1)[:, :entries]
     vectors = small[:, : 6 * share].reshape(n_dp * n_mp, 6, share).transpose(1, 0, 2).reshape(6, width)
     vectors = jnp.concatenate([vectors, jnp.zeros((2, width), F32)])
@@ -1233,9 +1387,14 @@
     valid = jnp.stack([length - half * rows, length - (1 - half) * rows]).astype(jnp.int32)
 
     linked = n_dp == 8
-    places = jnp.arange(n_mp, dtype=jnp.int32)
-    order = (lax.axis_index("mp") ^ places) if linked else places
-    pre_one, ctx, query, keys, values = attend(order, valid, frames, other, w_attn, qv_bias, vectors[0:1])
+    if linked:
+        pre_one, ctx, query, keys, values, w1, w2 = linked_attend(
+            valid, frames, other, w_attn, qv_bias, vectors[0:1], w_ff1, w_ff2.T
+        )
+    else:
+        w1, w2 = blocks(w_ff1, mesh_shape), blocks(w_ff2.T, mesh_shape)
+        order = jnp.arange(n_mp, dtype=jnp.int32)
+        pre_one, ctx, query, keys, values = attend(order, valid, frames, other, w_attn, qv_bias, vectors[0:1])
     hidden, active, low, low_t = up(pre_one, vectors[1:2], vectors[2:3], w1, up_bias)
     output, grad_pre, grad_low, grad_low_t, grad_ff, sums, grad_up_bias = down(
         pre_one, cotangent, vectors, active, hidden, w2, w1, low_t

time: 332 us -> 308 us (0.928)
  between operations: 15.8 us -> 2.49 us
  waiting for transfers between devices: 12.5 us -> 0.01 us
    pallas_call x1, Pallas kernels: 66.2 us -> 53.3 us  [gather_all(): pl.pallas_call(functools.partial(gather_kernel, count, n_mp), name='gathe...]
    pallas_call x1, Pallas kernels: 40 us -> 52.4 us  [linked_attend(): pl.pallas_call(functools.partial(linked_attend_kernel, groups), name='lin...]
    all_gather x2 -> x0, waiting for transfers between devices: 11.1 us -> none  [blocks(): lax.all_gather(local, BOTH, axis=0, tiled=False)]
  transfers between devices with their start and end apart: 3 -> 1, of which waited for: 1 -> 0; matrix products, arithmetic and copies ran while one was open for 4% -> 3% of each run, Pallas kernels for 36% -> 18%
where the time goes in v5:
time: 308 us; the launch traced here: 304 us
  Pallas kernels  275 us (89%)
  local copies, waits for them, and re-layouts  17.9 us (6%)
  other arithmetic  8.81 us (3%)
    pallas_call x1, Pallas kernels, linked_back(): pl.pallas_call(functools.partial(linked_back_kernel, groups), name='linke...  121 us
    pallas_call x1, Pallas kernels, gather_all(): pl.pallas_call(functools.partial(gather_kernel, count, n_mp), name='gathe...  53.3 us
    pallas_call x1, Pallas kernels, linked_attend(): pl.pallas_call(functools.partial(linked_attend_kernel, groups), name='lin...  52.4 us
    pallas_call x1, Pallas kernels, down(): pl.pallas_call(functools.partial(down_kernel, groups), name='down', grid=...  36.2 us
    pallas_call x1, Pallas kernels, up(): pl.pallas_call(up_kernel, name='up', grid=(groups,), in_specs=[pl.BlockSp...  11.7 us
  transfers between devices with their start and end apart: 1, of which 0 were waited for; matrix products, arithmetic and copies ran while one was open for 3% of the time, Pallas kernels for 18%

profile of v5, /device:TPU:8, one launch (start us, length us, event | category | flops | bytes accessed | tf_op | source)
XLA Modules:
  0.0 304.1 jit_solution(955293400638497581)
XLA Ops:
  0.8 1.7 copy.69
  3.5 0.8 pad_maximum_fusion.1.refs_0_
  4.3 53.3 %gather.1 = (bf16[8,4,96,768]{3,2,1,0:T(8,128)(2,1)}, f32[8,4,8,128]{3,2,1,0:T(8,128)}) custom-call(bf16[96,768]{1,0:T(8,128)(2,1)} %pad_maximum_fusion.1.refs_0_, f32[8,128]{1,0:T(8,128)} %pad_bitcast_fusion.refs_1_), custom_call_target="tpu_custom_call" | custom-call | tf_op jit(solution)/shard_map/gather/pallas_call | solution.py:850
  57.6 0.9 copy.88
  58.8 0.6 fusion
  61.3 0.7 slice.97.out_bias_ref
  62.1 0.7 slice.101.shift_ref
  62.9 0.7 slice.99.gain_ref
  63.5 0.7 reshape.83.bias_ref
  66.1 1.6 copy.74.other_ref
  67.8 52.4 %linked_attend.1 = (f32[768,768]{1,0:T(8,128)}, bf16[4,768,256]{2,1,0:T(8,128)(2,1)}, bf16[12,768,128]{2,1,0:T(8,128)(2,1)}, bf16[12,1536,128]{2,1,0:T(8,128)(2,...) custom-call(s32[2]{0:T(128)} %pad_add_fusion.valid_ref, ...), custom_call_target="tpu_custom_call" | custom-call | flops 53150220288 | bytes 37748736 | tf_op jit(solution)/shard_map/linked_attend/pallas_call | solution.py:813
  120.1 11.7 %up.1 = (f32[4,768,768]{2,1,0:T(8,128)}, bf16[4,768,768]{2,1,0:T(8,128)(2,1)}, bf16[768,768]{1,0:T(8,128)(2,1)}, bf16[768,768]{1,0:T(8,128)(2,1)}) custom-call(f32[768,768]{1,0:T(8,128)} %get-tuple-element.39.pre_ref, f32[1,768]{1,0:T(1,128)} %slice.99.gain_ref, f32[1,768]{1,0:T(1,128)} %slice.101.shift_ref, ...), custom_call_target="tpu_custom_call" | custom-call | flops 3623878656 | bytes 25165824 | tf_op jit(solution)/shard_map/up/pallas_call | solution.py:191
  131.8 36.2 %down.1 = (bf16[768,768]{1,0:T(8,128)(2,1)}, f32[768,768]{1,0:T(8,128)}, bf16[768,768]{1,0:T(8,128)(2,1)}, bf16[768,768]{1,0:T(8,128)(2,1)}, bf16[8,4,192,768]{3...) custom-call(f32[768,768]{1,0:T(8,128)} %get-tuple-element.39.pre_ref, bf16[768,768]{1,0:T(8,128)(2,1)} %cot_ref.1, ...), custom_call_target="tpu_custom_call" | custom-call | flops 18119393280 | bytes 50331648 | tf_op jit(solution)/shard_map/down/pallas_call | solution.py:320
  168.0 0.8 reshape.84
  169.0 0.8 reduce
  169.9 0.7 pad.15.early_ref
  170.6 121.3 %linked_back.1 = (f32[192,768]{1,0:T(8,128)}, f32[96,768]{1,0:T(8,128)}, f32[8,128]{1,0:T(8,128)}, f32[768,768]{1,0:T(8,128)}) custom-call(bf16[768,768]{1,0:T(8,128)(2,1)} %get-tuple-element.47.grad_ref, bf16[768,768]{1,0:T(8,128)(2,1)} %get-tuple-element.48.grad_t_ref, bf16[768,768]{1,0:T(8,128)(2,1)} %bitcast.55, bf16[768,768]{1,0:T(8,128)(2,1)} %bitcast.56, ...), custom_call_target="tpu_custom_call" | custom-call | flops 108716359680 | bytes 50331648 | tf_op jit(solution)/shard_map/linked_back/pallas_call | solution.py:1278
  291.9 1.2 slice_bitcast_fusion.1
  293.1 1.9 slice_bitcast_fusion
  295.0 0.7 copy.83
  295.7 1.3 slice.112
  297.0 1.6 fusion.2
  299.1 4.1 %add.29 = f32[768,768]{1,0:T(8,128)} add(f32[768,768]{1,0:T(8,128)} %get-tuple-element.46, f32[768,768]{1,0:T(8,128)} %get-tuple-element.56) | non-fusion elementwise | flops 589824 | bytes 7077888 | tf_op jit(solution)/shard_map/add | solution.py:1413
  303.2 0.7 pad_maximum_fusion
  (66 shorter events, 4.8 us)
Async XLA Ops:
  0.7 1.9 copy-start.2
  0.7 1.9 copy-start.3
  0.7 2.0 copy-start.13
  0.7 2.1 copy-start.4
  0.7 2.1 copy-start.5
  0.7 2.1 copy-start.6
  0.7 2.1 copy-start.10
  0.7 2.1 copy-start.7
  0.7 2.1 copy-start.8
  0.7 2.1 copy-start.9
  0.8 58.0 %copy-start.11 = (s32[16]{0:T(128)S(1)}, s32[16]{0:T(128)}, u32[]{:S(2)}) copy-start(s32[16]{0:T(128)} %param.30) | copy-start | bytes 196
  0.8 58.0 %copy-start.12 = (s32[16]{0:T(128)S(1)}, s32[16]{0:T(128)}, u32[]{:S(2)}) copy-start(s32[16]{0:T(128)} %param.31) | copy-start | bytes 196
  2.4 65.3 %copy-start = (bf16[768,768]{0,1:T(8,128)(2,1)}, bf16[768,768]{0,1:T(8,128)(2,1)S(1)}, u32[]{:S(2)}) copy-start(bf16[768,768]{0,1:T(8,128)(2,1)S(1)} %copy.69) | copy-start | bytes 3538948
  2.5 63.7 %collective-permute-start = (bf16[768,768]{0,1:T(8,128)(2,1)S(1)}, bf16[768,768]{0,1:T(8,128)(2,1)S(1)}, u32[]{:S(2)}, u32[]{:S(2)}) collective-permute-start(bf16[768,768]{0,1:T(8,128)(2,1)S(1)} %copy.69), channel_id=1, source_target_pairs={{0,1},{1,0},{2,3},{3,2},{4,5},{5,4},{6,7},{7,6},{8,9},{9,8},{10,11... | collective-permute-start | bytes 3538952 | tf_op jit(solution)/shard_map/ppermute | solution.py:1362
  66.1 54.0 %copy-start.1 = (bf16[768,768]{0,1:T(8,128)(2,1)}, bf16[768,768]{0,1:T(8,128)(2,1)S(1)}, u32[]{:S(2)}) copy-start(bf16[768,768]{0,1:T(8,128)(2,1)S(1)} %collective-permute-done) | copy-start | bytes 3538948
